TPU v7x, 32 devices: a whole 2x2x4 slice. The times are simulated.
32 devices in a mesh: grp: 2 (over x), tok: 8 (over z, y), side: 2 (over core).
Axes of the slice: x: 2, y: 2, z: 4, core: 2. Of those that a mesh axis runs over, the one named last changes fastest.
Arguments:
- hidden_in: bfloat16 [512, 3072], P(('grp', 'tok')), parts along dimension 0, may hold values from -6 to 6
- queries: bfloat16 [512, 24, 128], P(('grp', 'tok'), 'side'), parts along dimension 0, may hold values from -32 to 32
- key_new: bfloat16 [512, 4, 128], P(('grp', 'tok'), 'side'), parts along dimension 0, may hold values from -32 to 32
- value_new: bfloat16 [512, 4, 128], P(('grp', 'tok'), 'side'), parts along dimension 0, may hold values from -6 to 6
- cache_keys: bfloat16 [512, 4, 128, 128], P(('grp', 'tok'), 'side'), parts along dimension 0, may hold values from -32 to 32
- cache_values: bfloat16 [512, 4, 128, 128], P(('grp', 'tok'), 'side'), parts along dimension 0, may hold values from -6 to 6
- lengths: int32 [512], P(('grp', 'tok')), parts along dimension 0, may hold values from 1 to 128, 16384 in all
- out_weight: bfloat16 [3072, 3072], P('side', 'tok'), may hold values from -0.109375 to 0.109375
- norm_gain: float32 [3072], replicated, may hold values from 0.1 to 1.9
- router_weight: float32 [3072, 4], replicated, may hold values from -0.109375 to 0.109375
- gate_weight: bfloat16 [3072, 32768], P(None, ('tok', 'side')), may hold values from -0.109375 to 0.109375
- up_weight: bfloat16 [3072, 32768], P(None, ('tok', 'side')), may hold values from -0.109375 to 0.109375
- down_weight: bfloat16 [32768, 3072], P(('tok', 'side')), may hold values from -0.0625 to 0.0625
- routes: int32 [512, 2], P('grp'), parts along dimension 0, may hold values from 0 to 3, all different within a row; in each aligned block of 32 rows (0 to 31, 32 to 63, ...) at most 24 rows name the same one
Outputs:
- mixed: bfloat16 [512, 3072], P(('grp', 'tok')), parts along dimension 0
There are 2 independent parts, one for each index of `grp`. A program takes and returns all parts, laid end to end along the dimension named above; an argument that names none is the same for every part. Nothing has to cross between parts.
Inputs may be any that keep to these rules, and one draw needn't show every extreme that they name: Every sequence has at least one valid cache position and some sequence has 128; in each serving group the lengths sum to 16384. `routes`: each row names two different experts; among the rows of one index of tok (aligned blocks of 32 rows) no expert is named by more than 24 rows, and some expert reaches 24 in some block.
All inputs are finite; a program needn't handle non-finite values.
Results may differ from a plain program's by a relative error of at most 0.0075.
Values may be sent and summed in bfloat16 or wider, within the bound.
No kernel may reach another device: no remote copies, remote signals or barrier semaphores. Data moves between devices by JAX's collectives and lax.ppermute only.
A program may use at most 128 MiB of HBM per device.

v0:
```python
import math

import jax
import jax.numpy as jnp
from jax import lax
from jax.experimental import pallas as pl
from jax.experimental.pallas import tpu as pltpu
from jax.sharding import PartitionSpec as P


def attend(queries, key_new, value_new, cache_keys, cache_values, lengths):
    seq_count, head_count, head_width = queries.shape
    kv_count = key_new.shape[1]
    places = cache_keys.shape[2]
    scaling = 1.0 / math.sqrt(head_width)
    grouped = queries.reshape(seq_count, kv_count, head_count // kv_count, head_width)
    scores = (
        jnp.einsum("skgd,skpd->skgp", grouped, cache_keys, preferred_element_type=jnp.float32)
        * scaling
    )
    usable = jnp.arange(places, dtype=jnp.int32)[None, :] < lengths[:, None]
    scores = jnp.where(usable[:, None, None, :], scores, -jnp.inf)
    own_score = (
        jnp.einsum("skgd,skd->skg", grouped, key_new, preferred_element_type=jnp.float32) * scaling
    )
    top_score = jnp.maximum(jnp.max(scores, axis=-1), own_score)
    weights = jnp.exp(scores - top_score[..., None])
    own_weight = jnp.exp(own_score - top_score)
    totals = jnp.sum(weights, axis=-1) + own_weight
    prob_low = (weights / totals[..., None]).astype(jnp.bfloat16)
    own_low = (own_weight / totals).astype(jnp.bfloat16)
    mixture = jnp.einsum(
        "skgp,skpd->skgd", prob_low, cache_values, preferred_element_type=jnp.float32
    )
    mixture = (
        mixture
        + own_low.astype(jnp.float32)[..., None] * value_new.astype(jnp.float32)[:, :, None, :]
    )
    return mixture.astype(jnp.bfloat16).reshape(seq_count, head_count * head_width)


def scales(normed, picks, mine, router_weight):
    logits = jnp.dot(normed.astype(jnp.float32), router_weight, precision=lax.Precision.HIGHEST)
    chosen = jnp.sum(picks * logits[:, None, :], axis=-1)
    leading = jax.nn.sigmoid(chosen[:, 0] - chosen[:, 1])
    return (leading * mine[:, 0] + (1.0 - leading) * mine[:, 1])[:, None]


def cut(array, start, size, axis):
    return lax.dynamic_slice_in_dim(array, start, size, axis, allow_negative_indices=False)


def experts_kernel(own, other, gate, up, down, kept, sent, block, active):
    rows = own.shape[0]
    step = min(512, gate.shape[1])
    block[:rows] = own[...]
    block[rows:] = other[...]
    for c in range(0, gate.shape[1], step):
        gated = jnp.dot(block[...], gate[:, c : c + step], preferred_element_type=jnp.float32)
        upward = jnp.dot(block[...], up[:, c : c + step], preferred_element_type=jnp.float32)
        active[:, c : c + step] = (jax.nn.silu(gated) * upward).astype(jnp.bfloat16)
    for c in range(0, down.shape[1], 512):
        out = jnp.dot(active[...], down[:, c : c + 512], preferred_element_type=jnp.float32)
        kept[:, c : c + 512] = out[:rows]
        sent[:, c : c + 512] = out[rows:].astype(jnp.bfloat16)


def stage(weight):
    def body(source, target):
        pltpu.sync_copy(source, target)

    return pl.pallas_call(
        body,
        in_specs=[pl.BlockSpec(memory_space=pltpu.HBM)],
        out_specs=pl.BlockSpec(memory_space=pltpu.VMEM),
        out_shape=pltpu.VMEM(weight.shape, weight.dtype),
        cost_estimate=pl.CostEstimate(
            flops=weight.size * 600, transcendentals=0, bytes_accessed=2 * weight.size
        ),
        compiler_params=pltpu.CompilerParams(vmem_limit_bytes=1 << 20),
        name="stage",
    )(pltpu.with_memory_space_constraint(weight, pltpu.HBM))


def run_experts(own, other, *weights):
    rows, width = own.shape
    size = weights[0].size
    fast = pl.BlockSpec(memory_space=pltpu.VMEM)
    return pl.pallas_call(
        experts_kernel,
        in_specs=[fast] * 5,
        out_specs=[fast] * 2,
        out_shape=[
            jax.ShapeDtypeStruct((rows, width), jnp.float32),
            jax.ShapeDtypeStruct((rows, width), jnp.bfloat16),
        ],
        scratch_shapes=[
            pltpu.VMEM((2 * rows, width), jnp.bfloat16),
            pltpu.VMEM((2 * rows, weights[0].shape[1]), jnp.bfloat16),
        ],
        cost_estimate=pl.CostEstimate(
            flops=3 * size * 600, transcendentals=0, bytes_accessed=4 * size
        ),
        compiler_params=pltpu.CompilerParams(vmem_limit_bytes=12 << 20),
        name="experts",
    )(own, other, *[pltpu.with_memory_space_constraint(w, pltpu.VMEM) for w in weights])


def pick(stack, index):
    return cut(stack, index, 1, 0).reshape(stack.shape[1:])


def local(
    hidden_in,
    queries,
    key_new,
    value_new,
    cache_keys,
    cache_values,
    lengths,
    out_weight,
    norm_gain,
    router_weight,
    gate_weight,
    up_weight,
    down_weight,
    routes,
):
    rows, width = hidden_in.shape
    toks = lax.axis_size("tok")
    sides = lax.axis_size("side")
    experts = router_weight.shape[1]
    lines = toks // 2
    half = rows // sides
    cols = out_weight.shape[1]
    span = out_weight.shape[0]
    tok = lax.axis_index("tok")
    side = lax.axis_index("side")
    first_swap = [(t, t ^ 1) for t in range(toks)]
    side_swap = [(0, 1), (1, 0)]

    def across(value):
        return lax.ppermute(value, "side", side_swap)

    def near(value):
        return lax.ppermute(value, "tok", first_swap)

    def line(value, k):
        return lax.ppermute(value, "tok", [(t, t ^ (2 * k)) for t in range(toks)])

    groups = lax.axis_size("grp")
    group = lax.axis_index("grp")
    level = tok // 2
    parity = tok % 2

    def over(value, k):
        return lax.ppermute(value, "grp", [(g, g ^ k) for g in range(groups)])

    shares = groups + 1 if span % (8 * (groups + 1)) == 0 else groups
    share = span // shares
    brought = near(cut(out_weight, group * share, share, 0))
    rest = [near(out_weight[groups * share :])] if shares > groups else []
    gathered = jnp.stack([brought] + [over(brought, k) for k in range(1, groups)])

    hidden_half = cut(hidden_in, side * half, half, 0)
    attn_out = attend(queries, key_new, value_new, cache_keys, cache_values, lengths)
    own_routes = lax.dynamic_slice(
        routes.reshape(lines, 2, sides, half, -1),
        (0, parity, side, 0, 0),
        (lines, 1, 1, half, routes.shape[1]),
        allow_negative_indices=False,
    ).reshape(lines * half, -1)
    expert = tok // (toks // experts)
    picks = (
        own_routes[:, :, None] == jnp.arange(experts, dtype=jnp.int32)[None, None, :]
    ).astype(jnp.float32)
    mine = (own_routes == expert).astype(jnp.float32)
    order = [level ^ b for b in range(lines)]
    starts = [b * (2 * cols) for b in order]
    shares_order = [group ^ b for b in range(groups)]
    even = parity == 0
    first_side = side == 0
    corner = level * half
    (attn_out, picks, mine, order, starts, shares_order, even, first_side, corner, side, away) = (
        lax.optimization_barrier(
            (
                attn_out,
                picks,
                mine,
                order,
                starts,
                shares_order,
                even,
                first_side,
                corner,
                side,
                1 - side,
            )
        )
    )
    staged = [stage(w) for w in (gate_weight, up_weight, down_weight)]
    arrived = []
    for k in range(lines):
        part = cut(hidden_half, starts[k], 2 * cols, 1)
        folds = span // (2 * cols)
        deep = half // folds
        extra = jnp.concatenate([part[i * deep : (i + 1) * deep] for i in range(folds)], axis=1)
        message = jnp.concatenate([attn_out, extra], axis=0)
        arrived.append(line(message, k) if k else message)
    arrived, staged[0] = lax.optimization_barrier((arrived, staged[0]))
    blocks = jnp.concatenate([m[:rows] for m in arrived], axis=0)
    hidden_blocks = jnp.stack(
        [
            jnp.concatenate(
                [m[rows:, i * 2 * cols : (i + 1) * 2 * cols] for i in range(folds)], axis=0
            )
            for m in arrived
        ]
    )
    far_weight = jnp.concatenate([pick(gathered, b) for b in shares_order] + rest, axis=0)
    own_columns = jnp.dot(blocks, out_weight, preferred_element_type=jnp.float32)
    far_columns = jnp.dot(blocks, far_weight, preferred_element_type=jnp.float32)
    columns = jnp.concatenate(
        [
            jnp.where(even, own_columns, far_columns),
            jnp.where(even, far_columns, own_columns),
        ],
        axis=1,
    ).reshape(lines, sides, half, 2 * cols)
    other = cut(columns, away, 1, 1).reshape(lines, half, 2 * cols)
    own = cut(columns, side, 1, 1).reshape(lines, half, 2 * cols)
    relative = (hidden_blocks.astype(jnp.float32) + (own + across(other))).astype(jnp.bfloat16)
    residual = jnp.concatenate([pick(relative, b) for b in order], axis=0)
    parts = jnp.stack([residual] + [line(residual, k) for k in range(1, lines)])
    parts, staged = lax.optimization_barrier((parts, staged))
    stream = jnp.concatenate([pick(parts, b) for b in order], axis=1)
    wide = stream.astype(jnp.float32)
    normed = (
        wide * lax.rsqrt(jnp.mean(wide * wide, axis=-1, keepdims=True) + 1e-05) * norm_gain
    ).astype(jnp.bfloat16)
    distant = near(normed)
    mate_rows = across(normed)
    scale = scales(normed, picks, mine, router_weight)
    kept, sent = run_experts(normed, mate_rows, *staged)
    distant, sent = lax.optimization_barrier((distant, sent))
    back = across(sent)
    far_mates = across(distant)
    far_mates, back = lax.optimization_barrier((far_mates, back))
    far_kept, far_sent = run_experts(distant, far_mates, *staged)
    outward = (far_kept + across(far_sent).astype(jnp.float32)).astype(jnp.bfloat16)
    local_sum = kept + back.astype(jnp.float32)
    pair = ((local_sum + near(outward).astype(jnp.float32)) * scale).reshape(lines, half, width)
    pair_low = pair.astype(jnp.bfloat16)
    total = pick(pair, order[0])
    for k in range(1, lines):
        total = total + line(pick(pair_low, order[k]), k).astype(jnp.float32)
    mine_stream = cut(wide, corner, half, 0)
    result = (mine_stream + total).astype(jnp.bfloat16)
    mate = across(result)
    low = jnp.where(first_side, result, mate)
    high = jnp.where(first_side, mate, result)
    return jnp.concatenate([low, high], axis=0)


def solution(mesh):
    return jax.shard_map(
        local,
        mesh=mesh,
        in_specs=(
            P(("grp", "tok"), None),
            P(("grp", "tok"), "side", None),
            P(("grp", "tok"), "side", None),
            P(("grp", "tok"), "side", None),
            P(("grp", "tok"), "side", None, None),
            P(("grp", "tok"), "side", None, None),
            P(("grp", "tok")),
            P("side", "tok"),
            P(),
            P(),
            P(None, ("tok", "side")),
            P(None, ("tok", "side")),
            P(("tok", "side"), None),
            P("grp", None),
        ),
        out_specs=P(("grp", "tok"), None),
        check_vma=False,
    )
```

profile of v0, /device:TPU:0, one launch (start us, length us, event | category | flops | bytes accessed | tf_op | source)
XLA Modules:
  0.0 95.9 jit_solution(15307618450289847920)
XLA Ops:
  0.0 0.9 reshape.98
  1.1 0.9 iota_compare_fusion
  2.0 0.7 convert_element_type.64
  2.7 1.1 %fusion.19 = f32[32,2,1,6]{3,2,1,0:T(1,128)S(1)} fusion(bf16[32,2,6,128]{3,0,2,1:T(8,128)(2,1)} %bitcast.83, bf16[32,2,128,1]{2,1,0,3:T(2,128)(2,1)} %bitcast.91), kind=kOutput, calls=%fused_computation.39 | convolution fusion | flops 98304 | bytes 116224 | tf_op jit(solution)/shard_map/skgd,skd->skg/dot_general | solution.py:24
  3.8 2.2 %fusion.37 = (f32[32,2,6]{2,1,0:T(2,128)S(1)}, f32[32,2,6,128]{3,2,1,0:T(8,128)S(1)}) fusion(bf16[32,2,128,128]{3,2,1,0:T(8,128)(2,1)S(1)} %copy-done, bf16[32,2,6,128]{3,0,2,1:T(8,128)(2,1)} %bitcast.84, pred[32,128]{1,0:T(8,128)(4,1)S(1)} %iota_compare_fusion), kind=kOutput, calls=%fused_computation.92 | convolution fusion | flops 12729984 | bytes 2397696 | tf_op jit(solution)/shard_map/skgd,skpd->skgp/dot_general | solution.py:18
  6.0 0.3 fusion.12
  6.4 0.7 fusion.7
  7.3 0.1 fusion.32
  7.5 5.1 %collective-permute-start.2 = (bf16[40,1536]{1,0:T(8,128)(2,1)S(1)}, bf16[40,1536]{1,0:T(8,128)(2,1)S(1)}, u32[]{:S(2)}, u32[]{:S(2)}) collective-permute-start(bf16[40,1536]{1,0:T(8,128)(2,1)S(1)} %get-tuple-element.112), channel_id=1, source_target_pairs={{0,12},{2,14},{4,8},{6,10},{8,4},{10,6},{12,0},{14,2},{1,13},{3,15... | collective-permute-start | bytes 368648 | tf_op jit(solution)/shard_map/ppermute | solution.py:149
  12.7 0.6 collective-permute-start.1
  13.4 1.7 %collective-permute-start.3 = (bf16[512,384]{1,0:T(8,128)(2,1)S(1)}, bf16[512,384]{1,0:T(8,128)(2,1)S(1)}, u32[]{:S(2)}, u32[]{:S(2)}) collective-permute-start(bf16[512,384]{1,0:T(8,128)(2,1)S(1)} %get-tuple-element.75), channel_id=1, source_target_pairs={{0,2},{2,0},{4,6},{6,4},{8,10},{10,8},{12,14},{14,12},{1,3},{3,1},... | collective-permute-start | bytes 1179656 | tf_op jit(solution)/shard_map/ppermute | solution.py:146
  15.1 0.4 collective-permute-start.5
  15.5 4.6 %stage.3.gate = bf16[3072,2048]{1,0:T(8,128)(2,1)S(1)} custom-call(bf16[3072,2048]{1,0:T(8,128)(2,1)} %source.3), custom_call_target="tpu_custom_call" | custom-call | flops 3774873600 | bytes 12582912 | tf_op jit(solution)/shard_map/stage/pallas_call | solution.py:72
  20.0 4.6 %stage.4.up = bf16[3072,2048]{1,0:T(8,128)(2,1)S(1)} custom-call(bf16[3072,2048]{1,0:T(8,128)(2,1)} %source.4), custom_call_target="tpu_custom_call" | custom-call | flops 3774873600 | bytes 12582912 | tf_op jit(solution)/shard_map/stage/pallas_call | solution.py:72
  24.6 0.8 collective-permute-done.3
  25.4 1.6 %collective-permute-start.4 = (bf16[512,384]{1,0:T(8,128)(2,1)S(1)}, bf16[512,384]{1,0:T(8,128)(2,1)S(1)}, u32[]{:S(2)}, u32[]{:S(2)}) collective-permute-start(bf16[512,384]{1,0:T(8,128)(2,1)S(1)} %collective-permute-done.3), channel_id=1, source_target_pairs={{0,16},{16,0},{1,17},{17,1},{2,18},{18,2},{3,19},{19,3},{4,20},{20... | collective-permute-start | bytes 1179656 | tf_op jit(solution)/shard_map/ppermute | solution.py:157
  27.1 7.3 %collective-permute-done.4 = bf16[512,384]{1,0:T(8,128)(2,1)S(1)} collective-permute-done((bf16[512,384]{1,0:T(8,128)(2,1)S(1)}, bf16[512,384]{1,0:T(8,128)(2,1)S(1)}, u32[]{:S(2)}, u32[]{:S(2)}) %collective-permute-start.4) | collective-permute-done | bytes 393248 | tf_op jit(solution)/shard_map/ppermute | solution.py:157
  34.5 0.3 fusion.11
  34.8 0.4 fusion
  35.2 0.4 broadcast_select_fusion.1
  35.7 1.4 %collective-permute-done.6 = f32[4,16,768]{2,1,0:T(8,128)S(1)} collective-permute-done((f32[4,16,768]{2,1,0:T(8,128)S(1)}, f32[4,16,768]{2,1,0:T(8,128)S(1)}, u32[]{:S(2)}, u32[]{:S(2)}) %collective-permute-start.6) | collective-permute-done | bytes 196640 | tf_op jit(solution)/shard_map/ppermute | solution.py:143
  37.2 2.4 %collective-permute-start.8 = (bf16[64,768]{1,0:T(8,128)(2,1)S(1)}, bf16[64,768]{1,0:T(8,128)(2,1)S(1)}, u32[]{:S(2)}, u32[]{:S(2)}) collective-permute-start(bf16[64,768]{1,0:T(8,128)(2,1)S(1)} %get-tuple-element.107), channel_id=1, source_target_pairs={{0,8},{2,10},{4,12},{6,14},{8,0},{10,2},{12,4},{14,6},{1,9},{3,11}... | collective-permute-start | bytes 294920 | tf_op jit(solution)/shard_map/ppermute | solution.py:149
  39.6 1.7 %collective-permute-start.7 = (bf16[64,768]{1,0:T(8,128)(2,1)S(1)}, bf16[64,768]{1,0:T(8,128)(2,1)S(1)}, u32[]{:S(2)}, u32[]{:S(2)}) collective-permute-start(bf16[64,768]{1,0:T(8,128)(2,1)S(1)} %get-tuple-element.107), channel_id=1, source_target_pairs={{0,4},{2,6},{4,0},{6,2},{8,12},{10,14},{12,8},{14,10},{1,5},{3,7},... | collective-permute-start | bytes 294920 | tf_op jit(solution)/shard_map/ppermute | solution.py:149
  41.3 0.4 collective-permute-start.9
  41.7 4.6 %stage.5.down = bf16[2048,3072]{1,0:T(8,128)(2,1)S(1)} custom-call(bf16[2048,3072]{1,0:T(8,128)(2,1)} %source.5), custom_call_target="tpu_custom_call" | custom-call | flops 3774873600 | bytes 12582912 | tf_op jit(solution)/shard_map/stage/pallas_call | solution.py:72
  46.3 0.4 collective-permute-done.8
  46.6 1.6 %collective-permute-done.9 = bf16[64,768]{1,0:T(8,128)(2,1)S(1)} collective-permute-done((bf16[64,768]{1,0:T(8,128)(2,1)S(1)}, bf16[64,768]{1,0:T(8,128)(2,1)S(1)}, u32[]{:S(2)}, u32[]{:S(2)}) %collective-permute-start.9) | collective-permute-done | bytes 98336 | tf_op jit(solution)/shard_map/ppermute | solution.py:149
  48.3 0.2 multiply_reduce_fusion
  48.5 0.2 multiply_convert_fusion.own
  48.8 1.6 %collective-permute-start.11 = (bf16[64,3072]{1,0:T(8,128)(2,1)S(1)}, bf16[64,3072]{1,0:T(8,128)(2,1)S(1)}, u32[]{:S(2)}, u32[]{:S(2)}) collective-permute-start(bf16[64,3072]{1,0:T(8,128)(2,1)S(1)} %multiply_convert_fusion.own), channel_id=1, source_target_pairs={{0,2},{2,0},{4,6},{6,4},{8,10},{10,8},{12,14},{14,12},{1,3},{3,1},... | collective-permute-start | bytes 1179656 | tf_op jit(solution)/shard_map/ppermute | solution.py:146
  50.5 5.1 %experts.2 = (f32[64,3072]{1,0:T(8,128)S(1)}, bf16[64,3072]{1,0:T(8,128)(2,1)S(1)}) custom-call(bf16[64,3072]{1,0:T(8,128)(2,1)S(1)} %multiply_convert_fusion.own, bf16[64,3072]{1,0:T(8,128)(2,1)S(1)} %collective-permute-done.10.other, bf16[3072,2048]{1,0:T(8,128)(2,1)S(1)} %stage.3.gate, bf16[3072,2048]{1,0:T(8,128)(2,1)S(1)} %stage.4.up, ...), custom_call_target="tpu_custom_call" | custom-call | flops 11324620800 | bytes 25165824 | tf_op jit(solution)/shard_map/experts/pallas_call | solution.py:89
  55.6 4.7 %collective-permute-done.11.own = bf16[64,3072]{1,0:T(8,128)(2,1)S(1)} collective-permute-done((bf16[64,3072]{1,0:T(8,128)(2,1)S(1)}, bf16[64,3072]{1,0:T(8,128)(2,1)S(1)}, u32[]{:S(2)}, u32[]{:S(2)}) %collective-permute-start.11) | collective-permute-done | bytes 393248 | tf_op jit(solution)/shard_map/ppermute | solution.py:146
  60.3 0.5 collective-permute-start.12
  60.8 1.2 %collective-permute-done.13 = bf16[64,3072]{1,0:T(8,128)(2,1)S(1)} collective-permute-done((bf16[64,3072]{1,0:T(8,128)(2,1)S(1)}, bf16[64,3072]{1,0:T(8,128)(2,1)S(1)}, u32[]{:S(2)}, u32[]{:S(2)}) %collective-permute-start.13) | collective-permute-done | bytes 393248 | tf_op jit(solution)/shard_map/ppermute | solution.py:143
  62.0 0.6 collective-permute-done.12.other
  62.6 5.3 %experts.3 = (f32[64,3072]{1,0:T(8,128)S(1)}, bf16[64,3072]{1,0:T(8,128)(2,1)S(1)}) custom-call(bf16[64,3072]{1,0:T(8,128)(2,1)S(1)} %collective-permute-done.11.own, bf16[64,3072]{1,0:T(8,128)(2,1)S(1)} %collective-permute-done.12.other, bf16[3072,2048]{1,0:T(8,128)(2,1)S(1)} %stage.3.gate, bf16[3072,2048]{1,0:T(8,128)(2,1)S(1)} %stage.4.up, ...), custom_call_target="tpu_custom_call" | custom-call | flops 11324620800 | bytes 25165824 | tf_op jit(solution)/shard_map/experts/pallas_call | solution.py:89
  67.9 0.2 collective-permute-start.14
  68.1 1.6 %collective-permute-done.14 = bf16[64,3072]{1,0:T(8,128)(2,1)S(1)} collective-permute-done((bf16[64,3072]{1,0:T(8,128)(2,1)S(1)}, bf16[64,3072]{1,0:T(8,128)(2,1)S(1)}, u32[]{:S(2)}, u32[]{:S(2)}) %collective-permute-start.14) | collective-permute-done | bytes 393248 | tf_op jit(solution)/shard_map/ppermute | solution.py:143
  69.7 1.6 %collective-permute-start.15 = (bf16[64,3072]{1,0:T(8,128)(2,1)S(1)}, bf16[64,3072]{1,0:T(8,128)(2,1)S(1)}, u32[]{:S(2)}, u32[]{:S(2)}) collective-permute-start(bf16[64,3072]{1,0:T(8,128)(2,1)S(1)} %add_convert_fusion), channel_id=1, source_target_pairs={{0,2},{2,0},{4,6},{6,4},{8,10},{10,8},{12,14},{14,12},{1,3},{3,1},... | collective-permute-start | bytes 1179656 | tf_op jit(solution)/shard_map/ppermute | solution.py:146
  71.3 0.4 fusion.38
  71.8 9.2 %collective-permute-done.15 = bf16[64,3072]{1,0:T(8,128)(2,1)S(1)} collective-permute-done((bf16[64,3072]{1,0:T(8,128)(2,1)S(1)}, bf16[64,3072]{1,0:T(8,128)(2,1)S(1)}, u32[]{:S(2)}, u32[]{:S(2)}) %collective-permute-start.15) | collective-permute-done | bytes 393248 | tf_op jit(solution)/shard_map/ppermute | solution.py:146
  81.0 0.2 add_multiply_fusion
  81.2 1.8 %collective-permute-start.16 = (bf16[16,3072]{1,0:T(8,128)(2,1)S(1)}, bf16[16,3072]{1,0:T(8,128)(2,1)S(1)}, u32[]{:S(2)}, u32[]{:S(2)}) collective-permute-start(bf16[16,3072]{1,0:T(8,128)(2,1)S(1)} %get-tuple-element.79), channel_id=1, source_target_pairs={{0,4},{2,6},{4,0},{6,2},{8,12},{10,14},{12,8},{14,10},{1,5},{3,7},... | collective-permute-start | bytes 294920 | tf_op jit(solution)/shard_map/ppermute | solution.py:149
  83.0 3.2 %collective-permute-start.18 = (bf16[16,3072]{1,0:T(8,128)(2,1)S(1)}, bf16[16,3072]{1,0:T(8,128)(2,1)S(1)}, u32[]{:S(2)}, u32[]{:S(2)}) collective-permute-start(bf16[16,3072]{1,0:T(8,128)(2,1)S(1)} %get-tuple-element.80), channel_id=1, source_target_pairs={{0,12},{2,14},{4,8},{6,10},{8,4},{10,6},{12,0},{14,2},{1,13},{3,15... | collective-permute-start | bytes 294920 | tf_op jit(solution)/shard_map/ppermute | solution.py:149
  86.2 5.0 %collective-permute-done.18 = bf16[16,3072]{1,0:T(8,128)(2,1)S(1)} collective-permute-done((bf16[16,3072]{1,0:T(8,128)(2,1)S(1)}, bf16[16,3072]{1,0:T(8,128)(2,1)S(1)}, u32[]{:S(2)}, u32[]{:S(2)}) %collective-permute-start.18) | collective-permute-done | bytes 98336 | tf_op jit(solution)/shard_map/ppermute | solution.py:149
  91.3 2.4 %collective-permute-done.17 = bf16[16,3072]{1,0:T(8,128)(2,1)S(1)} collective-permute-done((bf16[16,3072]{1,0:T(8,128)(2,1)S(1)}, bf16[16,3072]{1,0:T(8,128)(2,1)S(1)}, u32[]{:S(2)}, u32[]{:S(2)}) %collective-permute-start.17) | collective-permute-done | bytes 98336 | tf_op jit(solution)/shard_map/ppermute | solution.py:149
  93.9 1.3 %collective-permute-done.19 = bf16[16,3072]{1,0:T(8,128)(2,1)S(1)} collective-permute-done((bf16[16,3072]{1,0:T(8,128)(2,1)S(1)}, bf16[16,3072]{1,0:T(8,128)(2,1)S(1)}, u32[]{:S(2)}, u32[]{:S(2)}) %collective-permute-start.19) | collective-permute-done | bytes 98336 | tf_op jit(solution)/shard_map/ppermute | solution.py:143
  95.2 0.7 pad_maximum_fusion.3
  (62 shorter events, 1.5 us)
Async XLA Ops:
  0.0 3.8 %copy-start = (bf16[32,2,128,128]{3,2,1,0:T(8,128)(2,1)S(1)}, bf16[32,2,128,128]{3,2,1,0:T(8,128)(2,1)}, u32[]{:S(2)}) copy-start(bf16[32,2,128,128]{3,2,1,0:T(8,128)(2,1)} %param.18) | copy-start | bytes 6291460
  1.1 5.3 %copy-start.6 = (bf16[32,2,128,128]{3,2,1,0:T(8,128)(2,1)S(1)}, bf16[32,2,128,128]{3,2,1,0:T(8,128)(2,1)}, u32[]{:S(2)}) copy-start(bf16[32,2,128,128]{3,2,1,0:T(8,128)(2,1)} %param.19) | copy-start | bytes 6291460
  6.4 0.9 copy-start.4
  6.4 6.9 %copy-start.2 = (bf16[1536,384]{1,0:T(8,128)(2,1)S(1)}, bf16[1536,384]{1,0:T(8,128)(2,1)}, u32[]{:S(2)}) copy-start(bf16[1536,384]{1,0:T(8,128)(2,1)} %param.21) | copy-start | bytes 3538948
  7.5 17.1 %collective-permute-start.2 = (bf16[40,1536]{1,0:T(8,128)(2,1)S(1)}, bf16[40,1536]{1,0:T(8,128)(2,1)S(1)}, u32[]{:S(2)}, u32[]{:S(2)}) collective-permute-start(bf16[40,1536]{1,0:T(8,128)(2,1)S(1)} %get-tuple-element.112), channel_id=1, source_target_pairs={{0,12},{2,14},{4,8},{6,10},{8,4},{10,6},{12,0},{14,2},{1,13},{3,15... | collective-permute-start | bytes 368648 | tf_op jit(solution)/shard_map/ppermute | solution.py:149
  12.6 12.0 %collective-permute-start = (bf16[40,1536]{1,0:T(8,128)(2,1)S(1)}, bf16[40,1536]{1,0:T(8,128)(2,1)S(1)}, u32[]{:S(2)}, u32[]{:S(2)}) collective-permute-start(bf16[40,1536]{1,0:T(8,128)(2,1)S(1)} %get-tuple-element.113), channel_id=1, source_target_pairs={{0,4},{2,6},{4,0},{6,2},{8,12},{10,14},{12,8},{14,10},{1,5},{3,7},... | collective-permute-start | bytes 368648 | tf_op jit(solution)/shard_map/ppermute | solution.py:149
  12.7 12.0 %collective-permute-start.1 = (bf16[40,1536]{1,0:T(8,128)(2,1)S(1)}, bf16[40,1536]{1,0:T(8,128)(2,1)S(1)}, u32[]{:S(2)}, u32[]{:S(2)}) collective-permute-start(bf16[40,1536]{1,0:T(8,128)(2,1)S(1)} %get-tuple-element.114), channel_id=1, source_target_pairs={{0,8},{2,10},{4,12},{6,14},{8,0},{10,2},{12,4},{14,6},{1,9},{3,11}... | collective-permute-start | bytes 368648 | tf_op jit(solution)/shard_map/ppermute | solution.py:149
  13.4 12.1 %collective-permute-start.3 = (bf16[512,384]{1,0:T(8,128)(2,1)S(1)}, bf16[512,384]{1,0:T(8,128)(2,1)S(1)}, u32[]{:S(2)}, u32[]{:S(2)}) collective-permute-start(bf16[512,384]{1,0:T(8,128)(2,1)S(1)} %get-tuple-element.75), channel_id=1, source_target_pairs={{0,2},{2,0},{4,6},{6,4},{8,10},{10,8},{12,14},{14,12},{1,3},{3,1},... | collective-permute-start | bytes 1179656 | tf_op jit(solution)/shard_map/ppermute | solution.py:146
  15.1 19.7 %collective-permute-start.5 = (bf16[512,384]{1,0:T(8,128)(2,1)S(1)}, bf16[512,384]{1,0:T(8,128)(2,1)S(1)}, u32[]{:S(2)}, u32[]{:S(2)}) collective-permute-start(bf16[512,384]{1,0:T(8,128)(2,1)S(1)} %get-tuple-element.76), channel_id=1, source_target_pairs={{0,2},{2,0},{4,6},{6,4},{8,10},{10,8},{12,14},{14,12},{1,3},{3,1},... | collective-permute-start | bytes 1179656 | tf_op jit(solution)/shard_map/ppermute | solution.py:146
  25.4 9.0 %collective-permute-start.4 = (bf16[512,384]{1,0:T(8,128)(2,1)S(1)}, bf16[512,384]{1,0:T(8,128)(2,1)S(1)}, u32[]{:S(2)}, u32[]{:S(2)}) collective-permute-start(bf16[512,384]{1,0:T(8,128)(2,1)S(1)} %collective-permute-done.3), channel_id=1, source_target_pairs={{0,16},{16,0},{1,17},{17,1},{2,18},{18,2},{3,19},{19,3},{4,20},{20... | collective-permute-start | bytes 1179656 | tf_op jit(solution)/shard_map/ppermute | solution.py:157
  35.6 1.5 %collective-permute-start.6 = (f32[4,16,768]{2,1,0:T(8,128)S(1)}, f32[4,16,768]{2,1,0:T(8,128)S(1)}, u32[]{:S(2)}, u32[]{:S(2)}) collective-permute-start(f32[4,16,768]{2,1,0:T(8,128)S(1)} %dynamic-slice_bitcast_fusion), channel_id=1, source_target_pairs={{0,1},{1,0},{2,3},{3,2},{4,5},{5,4},{6,7},{7,6},{8,9},{9,8},{10,11... | collective-permute-start | bytes 589832 | tf_op jit(solution)/shard_map/ppermute | solution.py:143
  37.2 11.3 %copy-start.5 = (f32[3072]{0:T(1024)S(1)}, f32[3072]{0:T(1024)}, u32[]{:S(2)}) copy-start(f32[3072]{0:T(1024)} %param.22) | copy-start | bytes 36868
  37.2 9.4 %collective-permute-start.8 = (bf16[64,768]{1,0:T(8,128)(2,1)S(1)}, bf16[64,768]{1,0:T(8,128)(2,1)S(1)}, u32[]{:S(2)}, u32[]{:S(2)}) collective-permute-start(bf16[64,768]{1,0:T(8,128)(2,1)S(1)} %get-tuple-element.107), channel_id=1, source_target_pairs={{0,8},{2,10},{4,12},{6,14},{8,0},{10,2},{12,4},{14,6},{1,9},{3,11}... | collective-permute-start | bytes 294920 | tf_op jit(solution)/shard_map/ppermute | solution.py:149
  39.6 7.1 %collective-permute-start.7 = (bf16[64,768]{1,0:T(8,128)(2,1)S(1)}, bf16[64,768]{1,0:T(8,128)(2,1)S(1)}, u32[]{:S(2)}, u32[]{:S(2)}) collective-permute-start(bf16[64,768]{1,0:T(8,128)(2,1)S(1)} %get-tuple-element.107), channel_id=1, source_target_pairs={{0,4},{2,6},{4,0},{6,2},{8,12},{10,14},{12,8},{14,10},{1,5},{3,7},... | collective-permute-start | bytes 294920 | tf_op jit(solution)/shard_map/ppermute | solution.py:149
  41.3 6.9 %collective-permute-start.9 = (bf16[64,768]{1,0:T(8,128)(2,1)S(1)}, bf16[64,768]{1,0:T(8,128)(2,1)S(1)}, u32[]{:S(2)}, u32[]{:S(2)}) collective-permute-start(bf16[64,768]{1,0:T(8,128)(2,1)S(1)} %get-tuple-element.107), channel_id=1, source_target_pairs={{0,12},{2,14},{4,8},{6,10},{8,4},{10,6},{12,0},{14,2},{1,13},{3,15... | collective-permute-start | bytes 294920 | tf_op jit(solution)/shard_map/ppermute | solution.py:149
  48.7 1.8 %collective-permute-start.10 = (bf16[64,3072]{1,0:T(8,128)(2,1)S(1)}, bf16[64,3072]{1,0:T(8,128)(2,1)S(1)}, u32[]{:S(2)}, u32[]{:S(2)}) collective-permute-start(bf16[64,3072]{1,0:T(8,128)(2,1)S(1)} %multiply_convert_fusion.own), channel_id=1, source_target_pairs={{0,1},{1,0},{2,3},{3,2},{4,5},{5,4},{6,7},{7,6},{8,9},{9,8},{10,11... | collective-permute-start | bytes 1179656 | tf_op jit(solution)/shard_map/ppermute | solution.py:143
  48.8 11.5 %collective-permute-start.11 = (bf16[64,3072]{1,0:T(8,128)(2,1)S(1)}, bf16[64,3072]{1,0:T(8,128)(2,1)S(1)}, u32[]{:S(2)}, u32[]{:S(2)}) collective-permute-start(bf16[64,3072]{1,0:T(8,128)(2,1)S(1)} %multiply_convert_fusion.own), channel_id=1, source_target_pairs={{0,2},{2,0},{4,6},{6,4},{8,10},{10,8},{12,14},{14,12},{1,3},{3,1},... | collective-permute-start | bytes 1179656 | tf_op jit(solution)/shard_map/ppermute | solution.py:146
  60.3 11.0 %copy-start.3 = (f32[3072,4]{0,1:T(4,128)S(1)}, f32[3072,4]{0,1:T(4,128)}, u32[]{:S(2)}) copy-start(f32[3072,4]{0,1:T(4,128)} %param.23) | copy-start | bytes 147460
  60.3 1.7 %collective-permute-start.13 = (bf16[64,3072]{1,0:T(8,128)(2,1)S(1)}, bf16[64,3072]{1,0:T(8,128)(2,1)S(1)}, u32[]{:S(2)}, u32[]{:S(2)}) collective-permute-start(bf16[64,3072]{1,0:T(8,128)(2,1)S(1)} %get-tuple-element.68), channel_id=1, source_target_pairs={{0,1},{1,0},{2,3},{3,2},{4,5},{5,4},{6,7},{7,6},{8,9},{9,8},{10,11... | collective-permute-start | bytes 1179656 | tf_op jit(solution)/shard_map/ppermute | solution.py:143
  60.3 2.3 %collective-permute-start.12 = (bf16[64,3072]{1,0:T(8,128)(2,1)S(1)}, bf16[64,3072]{1,0:T(8,128)(2,1)S(1)}, u32[]{:S(2)}, u32[]{:S(2)}) collective-permute-start(bf16[64,3072]{1,0:T(8,128)(2,1)S(1)} %collective-permute-done.11.own), channel_id=1, source_target_pairs={{0,1},{1,0},{2,3},{3,2},{4,5},{5,4},{6,7},{7,6},{8,9},{9,8},{10,11... | collective-permute-start | bytes 1179656 | tf_op jit(solution)/shard_map/ppermute | solution.py:143
  67.9 1.8 %collective-permute-start.14 = (bf16[64,3072]{1,0:T(8,128)(2,1)S(1)}, bf16[64,3072]{1,0:T(8,128)(2,1)S(1)}, u32[]{:S(2)}, u32[]{:S(2)}) collective-permute-start(bf16[64,3072]{1,0:T(8,128)(2,1)S(1)} %get-tuple-element.72), channel_id=1, source_target_pairs={{0,1},{1,0},{2,3},{3,2},{4,5},{5,4},{6,7},{7,6},{8,9},{9,8},{10,11... | collective-permute-start | bytes 1179656 | tf_op jit(solution)/shard_map/ppermute | solution.py:143
  69.7 11.2 %collective-permute-start.15 = (bf16[64,3072]{1,0:T(8,128)(2,1)S(1)}, bf16[64,3072]{1,0:T(8,128)(2,1)S(1)}, u32[]{:S(2)}, u32[]{:S(2)}) collective-permute-start(bf16[64,3072]{1,0:T(8,128)(2,1)S(1)} %add_convert_fusion), channel_id=1, source_target_pairs={{0,2},{2,0},{4,6},{6,4},{8,10},{10,8},{12,14},{14,12},{1,3},{3,1},... | collective-permute-start | bytes 1179656 | tf_op jit(solution)/shard_map/ppermute | solution.py:146
  81.1 14.8 %copy-start.1 = (bf16[32,2,128,128]{3,2,1,0:T(8,128)(2,1)S(1)}, bf16[32,2,128,128]{3,2,1,0:T(8,128)(2,1)}, u32[]{:S(2)}) copy-start(bf16[32,2,128,128]{3,2,1,0:T(8,128)(2,1)} %param.18) | copy-start | bytes 6291460
  81.2 5.0 %collective-permute-start.16 = (bf16[16,3072]{1,0:T(8,128)(2,1)S(1)}, bf16[16,3072]{1,0:T(8,128)(2,1)S(1)}, u32[]{:S(2)}, u32[]{:S(2)}) collective-permute-start(bf16[16,3072]{1,0:T(8,128)(2,1)S(1)} %get-tuple-element.79), channel_id=1, source_target_pairs={{0,4},{2,6},{4,0},{6,2},{8,12},{10,14},{12,8},{14,10},{1,5},{3,7},... | collective-permute-start | bytes 294920 | tf_op jit(solution)/shard_map/ppermute | solution.py:149
  83.0 8.3 %collective-permute-start.18 = (bf16[16,3072]{1,0:T(8,128)(2,1)S(1)}, bf16[16,3072]{1,0:T(8,128)(2,1)S(1)}, u32[]{:S(2)}, u32[]{:S(2)}) collective-permute-start(bf16[16,3072]{1,0:T(8,128)(2,1)S(1)} %get-tuple-element.80), channel_id=1, source_target_pairs={{0,12},{2,14},{4,8},{6,10},{8,4},{10,6},{12,0},{14,2},{1,13},{3,15... | collective-permute-start | bytes 294920 | tf_op jit(solution)/shard_map/ppermute | solution.py:149
  86.2 7.6 %collective-permute-start.17 = (bf16[16,3072]{1,0:T(8,128)(2,1)S(1)}, bf16[16,3072]{1,0:T(8,128)(2,1)S(1)}, u32[]{:S(2)}, u32[]{:S(2)}) collective-permute-start(bf16[16,3072]{1,0:T(8,128)(2,1)S(1)} %get-tuple-element.81), channel_id=1, source_target_pairs={{0,8},{2,10},{4,12},{6,14},{8,0},{10,2},{12,4},{14,6},{1,9},{3,11}... | collective-permute-start | bytes 294920 | tf_op jit(solution)/shard_map/ppermute | solution.py:149
  93.8 1.4 %collective-permute-start.19 = (bf16[16,3072]{1,0:T(8,128)(2,1)S(1)}, bf16[16,3072]{1,0:T(8,128)(2,1)S(1)}, u32[]{:S(2)}, u32[]{:S(2)}) collective-permute-start(bf16[16,3072]{1,0:T(8,128)(2,1)S(1)} %fusion.16), channel_id=1, source_target_pairs={{0,1},{1,0},{2,3},{3,2},{4,5},{5,4},{6,7},{7,6},{8,9},{9,8},{10,11... | collective-permute-start | bytes 294920 | tf_op jit(solution)/shard_map/ppermute | solution.py:143
where the time goes:
time: 96.2 us; the launch traced here: 95.9 us
  waiting for transfers between devices  37.6 us (39%)
  Pallas kernels  24.1 us (25%)
  starting transfers between devices  23 us (24%)
  matrix products  5.16 us (5%)
  other arithmetic  3.98 us (4%)
  local copies, waits for them, and re-layouts  1.59 us (2%)
    ppermute x9, starting transfers between devices, line(): return lax.ppermute(value, 'tok', [(t, t ^ 2 * k) for t in range(toks)])  15.2 us
    ppermute x4, waiting for transfers between devices, near(): return lax.ppermute(value, 'tok', first_swap)  14.7 us
    pallas_call x3, Pallas kernels, stage(): pl.pallas_call(body, in_specs=[pl.BlockSpec(memory_space=pltpu.HBM)], out...  13.7 us
    pallas_call x2, Pallas kernels, run_experts(): pl.pallas_call(experts_kernel, in_specs=[fast] * 5, out_specs=[fast] * 2,...  10.4 us
    ppermute x9, waiting for transfers between devices, line(): return lax.ppermute(value, 'tok', [(t, t ^ 2 * k) for t in range(toks)])  9.46 us
    ppermute x1, waiting for transfers between devices, over(): return lax.ppermute(value, 'grp', [(g, g ^ k) for g in range(groups)])  7.31 us
    ppermute x6, waiting for transfers between devices, across(): return lax.ppermute(value, 'side', side_swap)  6.18 us
    ppermute x4, starting transfers between devices, near(): return lax.ppermute(value, 'tok', first_swap)  5.25 us
  transfers between devices with their start and end apart: 20, of which 14 were waited for; matrix products, arithmetic and copies ran while one was open for 1% of the time, Pallas kernels for 20%

commit v1 on v0

--- a/solution.py
+++ b/solution.py
@@ -164,29 +164,32 @@
 
     hidden_half = cut(hidden_in, side * half, half, 0)
     attn_out = attend(queries, key_new, value_new, cache_keys, cache_values, lengths)
-    own_routes = lax.dynamic_slice(
-        routes.reshape(lines, 2, sides, half, -1),
-        (0, parity, side, 0, 0),
-        (lines, 1, 1, half, routes.shape[1]),
-        allow_negative_indices=False,
-    ).reshape(lines * half, -1)
     expert = tok // (toks // experts)
-    picks = (
-        own_routes[:, :, None] == jnp.arange(experts, dtype=jnp.int32)[None, None, :]
-    ).astype(jnp.float32)
-    mine = (own_routes == expert).astype(jnp.float32)
+    expert_ids = jnp.arange(experts, dtype=jnp.int32)
+
+    def masks(which):
+        chosen = lax.dynamic_slice(
+            routes.reshape(lines, 2, sides, half, -1),
+            (0, which, side, 0, 0),
+            (lines, 1, 1, half, routes.shape[1]),
+            allow_negative_indices=False,
+        ).reshape(lines * half, -1)
+        picks = (chosen[:, :, None] == expert_ids[None, None, :]).astype(jnp.float32)
+        return picks, (chosen == expert).astype(jnp.float32)
+
+    own_masks, far_masks = masks(parity), masks(1 - parity)
     order = [level ^ b for b in range(lines)]
     starts = [b * (2 * cols) for b in order]
     shares_order = [group ^ b for b in range(groups)]
     even = parity == 0
     first_side = side == 0
     corner = level * half
-    (attn_out, picks, mine, order, starts, shares_order, even, first_side, corner, side, away) = (
+    (attn_out, own_masks, far_masks, order, starts, shares_order, even, first_side, corner, side, away) = (
         lax.optimization_barrier(
             (
                 attn_out,
-                picks,
-                mine,
+                own_masks,
+                far_masks,
                 order,
                 starts,
                 shares_order,
@@ -240,21 +243,31 @@
     ).astype(jnp.bfloat16)
     distant = near(normed)
     mate_rows = across(normed)
-    scale = scales(normed, picks, mine, router_weight)
+    mine_stream = lax.optimization_barrier(cut(wide, corner, half, 0) * 1.0)
+    scale = scales(normed, *own_masks, router_weight)
     kept, sent = run_experts(normed, mate_rows, *staged)
-    distant, sent = lax.optimization_barrier((distant, sent))
     back = across(sent)
+
+    def reduce_line(values, weights):
+        weighted = (values * weights).reshape(lines, half, width)
+        low = weighted.astype(jnp.bfloat16)
+        return pick(weighted, order[0]), [
+            line(pick(low, order[k]), k) for k in range(1, lines)
+        ]
+
+    own_part, own_others = reduce_line(kept + back.astype(jnp.float32), scale)
+    distant, _ = lax.optimization_barrier((distant, own_part))
     far_mates = across(distant)
-    far_mates, back = lax.optimization_barrier((far_mates, back))
     far_kept, far_sent = run_experts(distant, far_mates, *staged)
-    outward = (far_kept + across(far_sent).astype(jnp.float32)).astype(jnp.bfloat16)
-    local_sum = kept + back.astype(jnp.float32)
-    pair = ((local_sum + near(outward).astype(jnp.float32)) * scale).reshape(lines, half, width)
-    pair_low = pair.astype(jnp.bfloat16)
-    total = pick(pair, order[0])
-    for k in range(1, lines):
-        total = total + line(pick(pair_low, order[k]), k).astype(jnp.float32)
-    mine_stream = cut(wide, corner, half, 0)
+    far_scale = scales(distant, *far_masks, router_weight)
+    far_part, far_others = reduce_line(
+        far_kept + across(far_sent).astype(jnp.float32), far_scale
+    )
+    for value in far_others:
+        far_part = far_part + value.astype(jnp.float32)
+    total = own_part
+    for value in own_others + [near(far_part.astype(jnp.bfloat16))]:
+        total = total + value.astype(jnp.float32)
     result = (mine_stream + total).astype(jnp.bfloat16)
     mate = across(result)
     low = jnp.where(first_side, result, mate)

time: 96.2 us -> 94.1 us (0.978)
  waiting for transfers between devices: 37.6 us -> 30.3 us
  starting transfers between devices: 23 us -> 26 us
  local copies, waits for them, and re-layouts: 1.59 us -> 2.85 us
    ppermute x4, waiting for transfers between devices: 14.7 us -> 2.8 us  [near(): return lax.ppermute(value, 'tok', first_swap)]
    ppermute x9 -> x12, waiting for transfers between devices: 9.46 us -> 12.9 us  [line(): return lax.ppermute(value, 'tok', [(t, t ^ 2 * k) for t in range(toks)])]
    ppermute x9 -> x12, starting transfers between devices: 15.2 us -> 17.3 us  [line(): return lax.ppermute(value, 'tok', [(t, t ^ 2 * k) for t in range(toks)])]
    dynamic_slice x1 -> x2, local copies, waits for them, and re-layouts: 0.08 us -> 1.37 us  [cut(): lax.dynamic_slice_in_dim(array, start, size, axis, allow_negative_indices...]
    dot_general x1, matrix products: 0.37 us -> 1.46 us  [local(): jnp.dot(blocks, far_weight, preferred_element_type=jnp.float32)]
    ppermute x4, starting transfers between devices: 5.25 us -> 6.3 us  [near(): return lax.ppermute(value, 'tok', first_swap)]
  transfers between devices with their start and end apart: 20 -> 23, of which waited for: 14 -> 12; matrix products, arithmetic and copies ran while one was open for 1% -> 9% of each run, Pallas kernels for 20% -> 20%
where the time goes in v1:
time: 94.1 us; the launch traced here: 93.7 us
  waiting for transfers between devices  30.3 us (32%)
  starting transfers between devices  26 us (28%)
  Pallas kernels  24.1 us (26%)
  matrix products  5.77 us (6%)
  other arithmetic  4.17 us (4%)
  local copies, waits for them, and re-layouts  2.85 us (3%)
    ppermute x12, starting transfers between devices, line(): return lax.ppermute(value, 'tok', [(t, t ^ 2 * k) for t in range(toks)])  17.3 us
    pallas_call x3, Pallas kernels, stage(): pl.pallas_call(body, in_specs=[pl.BlockSpec(memory_space=pltpu.HBM)], out...  13.7 us
    ppermute x12, waiting for transfers between devices, line(): return lax.ppermute(value, 'tok', [(t, t ^ 2 * k) for t in range(toks)])  12.9 us
    pallas_call x2, Pallas kernels, run_experts(): pl.pallas_call(experts_kernel, in_specs=[fast] * 5, out_specs=[fast] * 2,...  10.4 us
    ppermute x1, waiting for transfers between devices, over(): return lax.ppermute(value, 'grp', [(g, g ^ k) for g in range(groups)])  7.95 us
    ppermute x6, waiting for transfers between devices, across(): return lax.ppermute(value, 'side', side_swap)  6.63 us
    ppermute x4, starting transfers between devices, near(): return lax.ppermute(value, 'tok', first_swap)  6.3 us
    ppermute x4, waiting for transfers between devices, near(): return lax.ppermute(value, 'tok', first_swap)  2.8 us
  transfers between devices with their start and end apart: 23, of which 12 were waited for; matrix products, arithmetic and copies ran while one was open for 9% of the time, Pallas kernels for 20%

profile of v1, /device:TPU:0, one launch (start us, length us, event | category | flops | bytes accessed | tf_op | source)
XLA Modules:
  0.0 93.7 jit_solution(12323829590096137097)
XLA Ops:
  0.0 1.3 %constant_dynamic-slice_fusion.1 = (bf16[512,384]{1,0:T(8,128)(2,1)S(1)}, bf16[512,384]{1,0:T(8,128)(2,1)S(1)}) fusion(bf16[1536,384]{1,0:T(8,128)(2,1)} %param.21, s32[]{:T(128)S(6)} %mul.133), kind=kLoop, calls=%fused_computation.80 | loop fusion | bytes 1572868 | tf_op jit(solution)/shard_map/dynamic_slice | solution.py:50
  1.4 3.1 %collective-permute-start.5 = (bf16[512,384]{1,0:T(8,128)(2,1)S(1)}, bf16[512,384]{1,0:T(8,128)(2,1)}, u32[]{:S(2)}, u32[]{:S(2)}) collective-permute-start(bf16[512,384]{1,0:T(8,128)(2,1)S(1)} %get-tuple-element.74), channel_id=1, source_target_pairs={{0,2},{2,0},{4,6},{6,4},{8,10},{10,8},{12,14},{14,12},{1,3},{3,1},... | collective-permute-start | bytes 1179656 | tf_op jit(solution)/shard_map/ppermute | solution.py:146
  4.5 0.8 reshape.117
  5.5 0.9 iota_compare_fusion
  6.4 0.7 convert_element_type.83
  7.1 1.1 %fusion.18 = f32[32,2,1,6]{3,2,1,0:T(1,128)S(1)} fusion(bf16[32,2,6,128]{3,0,2,1:T(8,128)(2,1)} %bitcast.101, bf16[32,2,128,1]{2,1,0,3:T(2,128)(2,1)} %bitcast.110), kind=kOutput, calls=%fused_computation.40 | convolution fusion | flops 98304 | bytes 116224 | tf_op jit(solution)/shard_map/skgd,skd->skg/dot_general | solution.py:24
  8.3 1.3 %fusion.37 = (f32[32,2,6]{2,1,0:T(2,128)S(1)}, f32[32,2,6,128]{3,2,1,0:T(8,128)S(1)}) fusion(bf16[32,2,128,128]{3,2,1,0:T(8,128)(2,1)S(1)} %copy-done, bf16[32,2,6,128]{3,0,2,1:T(8,128)(2,1)S(1)} %bitcast.102, pred[32,128]{1,0:T(8,128)(4,1)S(1)} %iota_compare_fusion), kind=kOutput, calls=%fused_computation.103 | convolution fusion | flops 12729984 | bytes 2397696 | tf_op jit(solution)/shard_map/skgd,skpd->skgp/dot_general | solution.py:18
  9.6 0.3 fusion.12
  10.0 0.7 fusion.7
  10.7 0.1 reshape.116
  10.9 0.1 fusion.32
  11.1 2.1 %collective-permute-start = (bf16[40,1536]{1,0:T(8,128)(2,1)S(1)}, bf16[40,1536]{1,0:T(8,128)(2,1)S(1)}, u32[]{:S(2)}, u32[]{:S(2)}) collective-permute-start(bf16[40,1536]{1,0:T(8,128)(2,1)S(1)} %get-tuple-element.114), channel_id=1, source_target_pairs={{0,4},{2,6},{4,0},{6,2},{8,12},{10,14},{12,8},{14,10},{1,5},{3,7},... | collective-permute-start | bytes 368648 | tf_op jit(solution)/shard_map/ppermute | solution.py:149
  13.1 2.6 %collective-permute-start.1 = (bf16[40,1536]{1,0:T(8,128)(2,1)S(1)}, bf16[40,1536]{1,0:T(8,128)(2,1)S(1)}, u32[]{:S(2)}, u32[]{:S(2)}) collective-permute-start(bf16[40,1536]{1,0:T(8,128)(2,1)S(1)} %get-tuple-element.115), channel_id=1, source_target_pairs={{0,8},{2,10},{4,12},{6,14},{8,0},{10,2},{12,4},{14,6},{1,9},{3,11}... | collective-permute-start | bytes 368648 | tf_op jit(solution)/shard_map/ppermute | solution.py:149
  15.7 4.6 %stage.3.gate = bf16[3072,2048]{1,0:T(8,128)(2,1)S(1)} custom-call(bf16[3072,2048]{1,0:T(8,128)(2,1)} %source.3), custom_call_target="tpu_custom_call" | custom-call | flops 3774873600 | bytes 12582912 | tf_op jit(solution)/shard_map/stage/pallas_call | solution.py:72
  20.3 4.6 %stage.4.up = bf16[3072,2048]{1,0:T(8,128)(2,1)S(1)} custom-call(bf16[3072,2048]{1,0:T(8,128)(2,1)} %source.4), custom_call_target="tpu_custom_call" | custom-call | flops 3774873600 | bytes 12582912 | tf_op jit(solution)/shard_map/stage/pallas_call | solution.py:72
  24.9 1.8 %collective-permute-start.4 = (bf16[512,384]{1,0:T(8,128)(2,1)S(1)}, bf16[512,384]{1,0:T(8,128)(2,1)S(1)}, u32[]{:S(2)}, u32[]{:S(2)}) collective-permute-start(bf16[512,384]{1,0:T(8,128)(2,1)S(1)} %collective-permute-done.3), channel_id=1, source_target_pairs={{0,16},{16,0},{1,17},{17,1},{2,18},{18,2},{3,19},{19,3},{4,20},{20... | collective-permute-start | bytes 1179656 | tf_op jit(solution)/shard_map/ppermute | solution.py:157
  26.8 7.9 %collective-permute-done.4 = bf16[512,384]{1,0:T(8,128)(2,1)S(1)} collective-permute-done((bf16[512,384]{1,0:T(8,128)(2,1)S(1)}, bf16[512,384]{1,0:T(8,128)(2,1)S(1)}, u32[]{:S(2)}, u32[]{:S(2)}) %collective-permute-start.4) | collective-permute-done | bytes 393248 | tf_op jit(solution)/shard_map/ppermute | solution.py:157
  34.7 0.3 fusion.11
  35.1 1.5 %fusion = f32[128,384]{1,0:T(8,128)S(1)} fusion(bf16[512,384]{1,0:T(8,128)(2,1)} %collective-permute-done.5, bf16[512,384]{1,0:T(8,128)(2,1)S(1)} %get-tuple-element.76, bf16[512,384]{1,0:T(8,128)(2,1)S(1)} %get-tuple-element.75, bf16[32,1536]{1,0:T(8,128)(2,1)S(1)} %slice.106, bf16[32,1536]{1,0:T(8,128)(2,1)S(1)} %slice.105, ...), kind=kOutput, calls=%fused_computation | convolution fusion | flops 156106752 | bytes 1769472 | tf_op jit(solution)/shard_map/dot_general | solution.py:225
  36.6 0.4 broadcast_select_fusion.1
  37.1 1.4 %collective-permute-done.6 = f32[4,16,768]{2,1,0:T(8,128)S(1)} collective-permute-done((f32[4,16,768]{2,1,0:T(8,128)S(1)}, f32[4,16,768]{2,1,0:T(8,128)S(1)}, u32[]{:S(2)}, u32[]{:S(2)}) %collective-permute-start.6) | collective-permute-done | bytes 196640 | tf_op jit(solution)/shard_map/ppermute | solution.py:143
  38.6 3.6 %collective-permute-start.9 = (bf16[64,768]{1,0:T(8,128)(2,1)S(1)}, bf16[64,768]{1,0:T(8,128)(2,1)S(1)}, u32[]{:S(2)}, u32[]{:S(2)}) collective-permute-start(bf16[64,768]{1,0:T(8,128)(2,1)S(1)} %get-tuple-element.108), channel_id=1, source_target_pairs={{0,12},{2,14},{4,8},{6,10},{8,4},{10,6},{12,0},{14,2},{1,13},{3,15... | collective-permute-start | bytes 294920 | tf_op jit(solution)/shard_map/ppermute | solution.py:149
  42.2 0.8 collective-permute-start.7
  43.1 4.6 %stage.5.down = bf16[2048,3072]{1,0:T(8,128)(2,1)S(1)} custom-call(bf16[2048,3072]{1,0:T(8,128)(2,1)} %source.5), custom_call_target="tpu_custom_call" | custom-call | flops 3774873600 | bytes 12582912 | tf_op jit(solution)/shard_map/stage/pallas_call | solution.py:72
  47.7 3.2 %collective-permute-done.8 = bf16[64,768]{1,0:T(8,128)(2,1)S(1)} collective-permute-done((bf16[64,768]{1,0:T(8,128)(2,1)S(1)}, bf16[64,768]{1,0:T(8,128)(2,1)S(1)}, u32[]{:S(2)}, u32[]{:S(2)}) %collective-permute-start.8) | collective-permute-done | bytes 98336 | tf_op jit(solution)/shard_map/ppermute | solution.py:149
  51.0 0.2 multiply_reduce_fusion
  51.2 0.2 multiply_convert_fusion.own
  51.5 1.6 %collective-permute-start.15 = (bf16[64,3072]{1,0:T(8,128)(2,1)S(1)}, bf16[64,3072]{1,0:T(8,128)(2,1)S(1)}, u32[]{:S(2)}, u32[]{:S(2)}) collective-permute-start(bf16[64,3072]{1,0:T(8,128)(2,1)S(1)} %multiply_convert_fusion.own), channel_id=1, source_target_pairs={{0,2},{2,0},{4,6},{6,4},{8,10},{10,8},{12,14},{14,12},{1,3},{3,1},... | collective-permute-start | bytes 1179656 | tf_op jit(solution)/shard_map/ppermute | solution.py:146
  53.2 5.1 %experts.2 = (f32[64,3072]{1,0:T(8,128)S(1)}, bf16[64,3072]{1,0:T(8,128)(2,1)S(1)}) custom-call(bf16[64,3072]{1,0:T(8,128)(2,1)S(1)} %multiply_convert_fusion.own, bf16[64,3072]{1,0:T(8,128)(2,1)S(1)} %collective-permute-done.10.other, bf16[3072,2048]{1,0:T(8,128)(2,1)S(1)} %stage.3.gate, bf16[3072,2048]{1,0:T(8,128)(2,1)S(1)} %stage.4.up, ...), custom_call_target="tpu_custom_call" | custom-call | flops 11324620800 | bytes 25165824 | tf_op jit(solution)/shard_map/experts/pallas_call | solution.py:89
  58.3 0.2 collective-permute-start.11
  58.5 0.4 fusion.38
  58.9 1.1 %collective-permute-done.11 = bf16[64,3072]{1,0:T(8,128)(2,1)S(1)} collective-permute-done((bf16[64,3072]{1,0:T(8,128)(2,1)S(1)}, bf16[64,3072]{1,0:T(8,128)(2,1)S(1)}, u32[]{:S(2)}, u32[]{:S(2)}) %collective-permute-start.11) | collective-permute-done | bytes 393248 | tf_op jit(solution)/shard_map/ppermute | solution.py:143
  60.2 2.8 %collective-permute-done.15.own = bf16[64,3072]{1,0:T(8,128)(2,1)S(1)} collective-permute-done((bf16[64,3072]{1,0:T(8,128)(2,1)S(1)}, bf16[64,3072]{1,0:T(8,128)(2,1)S(1)}, u32[]{:S(2)}, u32[]{:S(2)}) %collective-permute-start.15) | collective-permute-done | bytes 393248 | tf_op jit(solution)/shard_map/ppermute | solution.py:146
  63.0 1.7 %collective-permute-done.16.other = bf16[64,3072]{1,0:T(8,128)(2,1)S(1)} collective-permute-done((bf16[64,3072]{1,0:T(8,128)(2,1)S(1)}, bf16[64,3072]{1,0:T(8,128)(2,1)S(1)}, u32[]{:S(2)}, u32[]{:S(2)}) %collective-permute-start.16) | collective-permute-done | bytes 393248 | tf_op jit(solution)/shard_map/ppermute | solution.py:143
  64.7 5.3 %experts.3 = (f32[64,3072]{1,0:T(8,128)S(1)}, bf16[64,3072]{1,0:T(8,128)(2,1)S(1)}) custom-call(bf16[64,3072]{1,0:T(8,128)(2,1)S(1)} %collective-permute-done.15.own, bf16[64,3072]{1,0:T(8,128)(2,1)S(1)} %collective-permute-done.16.other, bf16[3072,2048]{1,0:T(8,128)(2,1)S(1)} %stage.3.gate, bf16[3072,2048]{1,0:T(8,128)(2,1)S(1)} %stage.4.up, ...), custom_call_target="tpu_custom_call" | custom-call | flops 11324620800 | bytes 25165824 | tf_op jit(solution)/shard_map/experts/pallas_call | solution.py:89
  70.0 0.2 collective-permute-start.17
  70.2 0.4 fusion.39
  70.7 1.1 %collective-permute-done.17 = bf16[64,3072]{1,0:T(8,128)(2,1)S(1)} collective-permute-done((bf16[64,3072]{1,0:T(8,128)(2,1)S(1)}, bf16[64,3072]{1,0:T(8,128)(2,1)S(1)}, u32[]{:S(2)}, u32[]{:S(2)}) %collective-permute-start.17) | collective-permute-done | bytes 393248 | tf_op jit(solution)/shard_map/ppermute | solution.py:143
  72.0 2.4 %collective-permute-start.20 = (bf16[16,3072]{1,0:T(8,128)(2,1)S(1)}, bf16[16,3072]{1,0:T(8,128)(2,1)S(1)}, u32[]{:S(2)}, u32[]{:S(2)}) collective-permute-start(bf16[16,3072]{1,0:T(8,128)(2,1)S(1)} %get-tuple-element.81), channel_id=1, source_target_pairs={{0,12},{2,14},{4,8},{6,10},{8,4},{10,6},{12,0},{14,2},{1,13},{3,15... | collective-permute-start | bytes 294920 | tf_op jit(solution)/shard_map/ppermute | solution.py:149
  74.5 2.0 %collective-permute-start.18 = (bf16[16,3072]{1,0:T(8,128)(2,1)S(1)}, bf16[16,3072]{1,0:T(8,128)(2,1)S(1)}, u32[]{:S(2)}, u32[]{:S(2)}) collective-permute-start(bf16[16,3072]{1,0:T(8,128)(2,1)S(1)} %get-tuple-element.80), channel_id=1, source_target_pairs={{0,4},{2,6},{4,0},{6,2},{8,12},{10,14},{12,8},{14,10},{1,5},{3,7},... | collective-permute-start | bytes 294920 | tf_op jit(solution)/shard_map/ppermute | solution.py:149
  76.5 2.4 %collective-permute-start.14 = (bf16[16,3072]{1,0:T(8,128)(2,1)S(1)}, bf16[16,3072]{1,0:T(8,128)(2,1)S(1)}, u32[]{:S(2)}, u32[]{:S(2)}) collective-permute-start(bf16[16,3072]{1,0:T(8,128)(2,1)S(1)} %get-tuple-element.78), channel_id=1, source_target_pairs={{0,12},{2,14},{4,8},{6,10},{8,4},{10,6},{12,0},{14,2},{1,13},{3,15... | collective-permute-start | bytes 294920 | tf_op jit(solution)/shard_map/ppermute | solution.py:149
  78.9 0.7 collective-permute-done.20
  79.6 1.3 %collective-permute-start.12 = (bf16[16,3072]{1,0:T(8,128)(2,1)S(1)}, bf16[16,3072]{1,0:T(8,128)(2,1)S(1)}, u32[]{:S(2)}, u32[]{:S(2)}) collective-permute-start(bf16[16,3072]{1,0:T(8,128)(2,1)S(1)} %get-tuple-element.77), channel_id=1, source_target_pairs={{0,4},{2,6},{4,0},{6,2},{8,12},{10,14},{12,8},{14,10},{1,5},{3,7},... | collective-permute-start | bytes 294920 | tf_op jit(solution)/shard_map/ppermute | solution.py:149
  81.0 5.8 %collective-permute-done.19 = bf16[16,3072]{1,0:T(8,128)(2,1)S(1)} collective-permute-done((bf16[16,3072]{1,0:T(8,128)(2,1)S(1)}, bf16[16,3072]{1,0:T(8,128)(2,1)S(1)}, u32[]{:S(2)}, u32[]{:S(2)}) %collective-permute-start.19) | collective-permute-done | bytes 98336 | tf_op jit(solution)/shard_map/ppermute | solution.py:149
  86.9 1.6 %collective-permute-start.21 = (bf16[16,3072]{1,0:T(8,128)(2,1)S(1)}, bf16[16,3072]{1,0:T(8,128)(2,1)S(1)}, u32[]{:S(2)}, u32[]{:S(2)}) collective-permute-start(bf16[16,3072]{1,0:T(8,128)(2,1)S(1)} %fusion.15), channel_id=1, source_target_pairs={{0,2},{2,0},{4,6},{6,4},{8,10},{10,8},{12,14},{14,12},{1,3},{3,1},... | collective-permute-start | bytes 294920 | tf_op jit(solution)/shard_map/ppermute | solution.py:146
  88.5 3.1 %collective-permute-done.13 = bf16[16,3072]{1,0:T(8,128)(2,1)S(1)} collective-permute-done((bf16[16,3072]{1,0:T(8,128)(2,1)S(1)}, bf16[16,3072]{1,0:T(8,128)(2,1)S(1)}, u32[]{:S(2)}, u32[]{:S(2)}) %collective-permute-start.13) | collective-permute-done | bytes 98336 | tf_op jit(solution)/shard_map/ppermute | solution.py:149
  91.8 1.3 %collective-permute-done.22 = bf16[16,3072]{1,0:T(8,128)(2,1)S(1)} collective-permute-done((bf16[16,3072]{1,0:T(8,128)(2,1)S(1)}, bf16[16,3072]{1,0:T(8,128)(2,1)S(1)}, u32[]{:S(2)}, u32[]{:S(2)}) %collective-permute-start.22) | collective-permute-done | bytes 98336 | tf_op jit(solution)/shard_map/ppermute | solution.py:143
  93.0 0.7 pad_maximum_fusion.3
  (80 shorter events, 1.9 us)
Async XLA Ops:
  0.0 8.2 %copy-start = (bf16[32,2,128,128]{3,2,1,0:T(8,128)(2,1)S(1)}, bf16[32,2,128,128]{3,2,1,0:T(8,128)(2,1)}, u32[]{:S(2)}) copy-start(bf16[32,2,128,128]{3,2,1,0:T(8,128)(2,1)} %param.18) | copy-start | bytes 6291460
  0.0 8.2 %copy-start.4 = (bf16[32,12,128]{2,0,1:T(8,128)(2,1)S(1)}, bf16[32,12,128]{2,0,1:T(8,128)(2,1)}, u32[]{:S(2)}) copy-start(bf16[32,12,128]{2,0,1:T(8,128)(2,1)} %param.15) | copy-start | bytes 294916
  1.4 33.7 %collective-permute-start.5 = (bf16[512,384]{1,0:T(8,128)(2,1)S(1)}, bf16[512,384]{1,0:T(8,128)(2,1)}, u32[]{:S(2)}, u32[]{:S(2)}) collective-permute-start(bf16[512,384]{1,0:T(8,128)(2,1)S(1)} %get-tuple-element.74), channel_id=1, source_target_pairs={{0,2},{2,0},{4,6},{6,4},{8,10},{10,8},{12,14},{14,12},{1,3},{3,1},... | collective-permute-start | bytes 1179656 | tf_op jit(solution)/shard_map/ppermute | solution.py:146
  4.4 20.5 %collective-permute-start.3 = (bf16[512,384]{1,0:T(8,128)(2,1)S(1)}, bf16[512,384]{1,0:T(8,128)(2,1)S(1)}, u32[]{:S(2)}, u32[]{:S(2)}) collective-permute-start(bf16[512,384]{1,0:T(8,128)(2,1)S(1)} %get-tuple-element.73), channel_id=1, source_target_pairs={{0,2},{2,0},{4,6},{6,4},{8,10},{10,8},{12,14},{14,12},{1,3},{3,1},... | collective-permute-start | bytes 1179656 | tf_op jit(solution)/shard_map/ppermute | solution.py:146
  5.5 4.4 %copy-start.7 = (bf16[32,2,128,128]{3,2,1,0:T(8,128)(2,1)S(1)}, bf16[32,2,128,128]{3,2,1,0:T(8,128)(2,1)}, u32[]{:S(2)}) copy-start(bf16[32,2,128,128]{3,2,1,0:T(8,128)(2,1)} %param.19) | copy-start | bytes 6291460
  10.0 0.9 copy-start.5
  11.1 13.8 %collective-permute-start = (bf16[40,1536]{1,0:T(8,128)(2,1)S(1)}, bf16[40,1536]{1,0:T(8,128)(2,1)S(1)}, u32[]{:S(2)}, u32[]{:S(2)}) collective-permute-start(bf16[40,1536]{1,0:T(8,128)(2,1)S(1)} %get-tuple-element.114), channel_id=1, source_target_pairs={{0,4},{2,6},{4,0},{6,2},{8,12},{10,14},{12,8},{14,10},{1,5},{3,7},... | collective-permute-start | bytes 368648 | tf_op jit(solution)/shard_map/ppermute | solution.py:149
  13.1 11.7 %collective-permute-start.1 = (bf16[40,1536]{1,0:T(8,128)(2,1)S(1)}, bf16[40,1536]{1,0:T(8,128)(2,1)S(1)}, u32[]{:S(2)}, u32[]{:S(2)}) collective-permute-start(bf16[40,1536]{1,0:T(8,128)(2,1)S(1)} %get-tuple-element.115), channel_id=1, source_target_pairs={{0,8},{2,10},{4,12},{6,14},{8,0},{10,2},{12,4},{14,6},{1,9},{3,11}... | collective-permute-start | bytes 368648 | tf_op jit(solution)/shard_map/ppermute | solution.py:149
  15.7 9.2 %collective-permute-start.2 = (bf16[40,1536]{1,0:T(8,128)(2,1)S(1)}, bf16[40,1536]{1,0:T(8,128)(2,1)S(1)}, u32[]{:S(2)}, u32[]{:S(2)}) collective-permute-start(bf16[40,1536]{1,0:T(8,128)(2,1)S(1)} %get-tuple-element.113), channel_id=1, source_target_pairs={{0,12},{2,14},{4,8},{6,10},{8,4},{10,6},{12,0},{14,2},{1,13},{3,15... | collective-permute-start | bytes 368648 | tf_op jit(solution)/shard_map/ppermute | solution.py:149
  24.9 9.8 %collective-permute-start.4 = (bf16[512,384]{1,0:T(8,128)(2,1)S(1)}, bf16[512,384]{1,0:T(8,128)(2,1)S(1)}, u32[]{:S(2)}, u32[]{:S(2)}) collective-permute-start(bf16[512,384]{1,0:T(8,128)(2,1)S(1)} %collective-permute-done.3), channel_id=1, source_target_pairs={{0,16},{16,0},{1,17},{17,1},{2,18},{18,2},{3,19},{19,3},{4,20},{20... | collective-permute-start | bytes 1179656 | tf_op jit(solution)/shard_map/ppermute | solution.py:157
  35.1 1.5 %copy-start.2 = (bf16[1536,384]{1,0:T(8,128)(2,1)S(1)}, bf16[1536,384]{1,0:T(8,128)(2,1)}, u32[]{:S(2)}) copy-start(bf16[1536,384]{1,0:T(8,128)(2,1)} %param.21) | copy-start | bytes 3538948
  37.0 1.5 %collective-permute-start.6 = (f32[4,16,768]{2,1,0:T(8,128)S(1)}, f32[4,16,768]{2,1,0:T(8,128)S(1)}, u32[]{:S(2)}, u32[]{:S(2)}) collective-permute-start(f32[4,16,768]{2,1,0:T(8,128)S(1)} %dynamic-slice_bitcast_fusion.1), channel_id=1, source_target_pairs={{0,1},{1,0},{2,3},{3,2},{4,5},{5,4},{6,7},{7,6},{8,9},{9,8},{10,11... | collective-permute-start | bytes 589832 | tf_op jit(solution)/shard_map/ppermute | solution.py:143
  38.6 12.6 %copy-start.6 = (f32[3072]{0:T(1024)S(1)}, f32[3072]{0:T(1024)}, u32[]{:S(2)}) copy-start(f32[3072]{0:T(1024)} %param.22) | copy-start | bytes 36868
  38.6 9.0 %collective-permute-start.9 = (bf16[64,768]{1,0:T(8,128)(2,1)S(1)}, bf16[64,768]{1,0:T(8,128)(2,1)S(1)}, u32[]{:S(2)}, u32[]{:S(2)}) collective-permute-start(bf16[64,768]{1,0:T(8,128)(2,1)S(1)} %get-tuple-element.108), channel_id=1, source_target_pairs={{0,12},{2,14},{4,8},{6,10},{8,4},{10,6},{12,0},{14,2},{1,13},{3,15... | collective-permute-start | bytes 294920 | tf_op jit(solution)/shard_map/ppermute | solution.py:149
  42.2 8.7 %collective-permute-start.8 = (bf16[64,768]{1,0:T(8,128)(2,1)S(1)}, bf16[64,768]{1,0:T(8,128)(2,1)S(1)}, u32[]{:S(2)}, u32[]{:S(2)}) collective-permute-start(bf16[64,768]{1,0:T(8,128)(2,1)S(1)} %get-tuple-element.108), channel_id=1, source_target_pairs={{0,8},{2,10},{4,12},{6,14},{8,0},{10,2},{12,4},{14,6},{1,9},{3,11}... | collective-permute-start | bytes 294920 | tf_op jit(solution)/shard_map/ppermute | solution.py:149
  42.2 8.7 %collective-permute-start.7 = (bf16[64,768]{1,0:T(8,128)(2,1)S(1)}, bf16[64,768]{1,0:T(8,128)(2,1)S(1)}, u32[]{:S(2)}, u32[]{:S(2)}) collective-permute-start(bf16[64,768]{1,0:T(8,128)(2,1)S(1)} %get-tuple-element.108), channel_id=1, source_target_pairs={{0,4},{2,6},{4,0},{6,2},{8,12},{10,14},{12,8},{14,10},{1,5},{3,7},... | collective-permute-start | bytes 294920 | tf_op jit(solution)/shard_map/ppermute | solution.py:149
  51.4 7.1 %copy-start.3 = (f32[3072,4]{0,1:T(4,128)S(1)}, f32[3072,4]{0,1:T(4,128)}, u32[]{:S(2)}) copy-start(f32[3072,4]{0,1:T(4,128)} %param.23) | copy-start | bytes 147460
  51.4 1.8 %collective-permute-start.10 = (bf16[64,3072]{1,0:T(8,128)(2,1)S(1)}, bf16[64,3072]{1,0:T(8,128)(2,1)S(1)}, u32[]{:S(2)}, u32[]{:S(2)}) collective-permute-start(bf16[64,3072]{1,0:T(8,128)(2,1)S(1)} %multiply_convert_fusion.own), channel_id=1, source_target_pairs={{0,1},{1,0},{2,3},{3,2},{4,5},{5,4},{6,7},{7,6},{8,9},{9,8},{10,11... | collective-permute-start | bytes 1179656 | tf_op jit(solution)/shard_map/ppermute | solution.py:143
  51.5 11.5 %collective-permute-start.15 = (bf16[64,3072]{1,0:T(8,128)(2,1)S(1)}, bf16[64,3072]{1,0:T(8,128)(2,1)S(1)}, u32[]{:S(2)}, u32[]{:S(2)}) collective-permute-start(bf16[64,3072]{1,0:T(8,128)(2,1)S(1)} %multiply_convert_fusion.own), channel_id=1, source_target_pairs={{0,2},{2,0},{4,6},{6,4},{8,10},{10,8},{12,14},{14,12},{1,3},{3,1},... | collective-permute-start | bytes 1179656 | tf_op jit(solution)/shard_map/ppermute | solution.py:146
  58.3 1.8 %collective-permute-start.11 = (bf16[64,3072]{1,0:T(8,128)(2,1)S(1)}, bf16[64,3072]{1,0:T(8,128)(2,1)S(1)}, u32[]{:S(2)}, u32[]{:S(2)}) collective-permute-start(bf16[64,3072]{1,0:T(8,128)(2,1)S(1)} %get-tuple-element.65), channel_id=1, source_target_pairs={{0,1},{1,0},{2,3},{3,2},{4,5},{5,4},{6,7},{7,6},{8,9},{9,8},{10,11... | collective-permute-start | bytes 1179656 | tf_op jit(solution)/shard_map/ppermute | solution.py:143
  63.0 1.7 %collective-permute-start.16 = (bf16[64,3072]{1,0:T(8,128)(2,1)S(1)}, bf16[64,3072]{1,0:T(8,128)(2,1)S(1)}, u32[]{:S(2)}, u32[]{:S(2)}) collective-permute-start(bf16[64,3072]{1,0:T(8,128)(2,1)S(1)} %collective-permute-done.15.own), channel_id=1, source_target_pairs={{0,1},{1,0},{2,3},{3,2},{4,5},{5,4},{6,7},{7,6},{8,9},{9,8},{10,11... | collective-permute-start | bytes 1179656 | tf_op jit(solution)/shard_map/ppermute | solution.py:143
  70.0 1.8 %collective-permute-start.17 = (bf16[64,3072]{1,0:T(8,128)(2,1)S(1)}, bf16[64,3072]{1,0:T(8,128)(2,1)S(1)}, u32[]{:S(2)}, u32[]{:S(2)}) collective-permute-start(bf16[64,3072]{1,0:T(8,128)(2,1)S(1)} %get-tuple-element.70), channel_id=1, source_target_pairs={{0,1},{1,0},{2,3},{3,2},{4,5},{5,4},{6,7},{7,6},{8,9},{9,8},{10,11... | collective-permute-start | bytes 1179656 | tf_op jit(solution)/shard_map/ppermute | solution.py:143
  71.9 21.8 %copy-start.1 = (bf16[32,2,128,128]{3,2,1,0:T(8,128)(2,1)S(1)}, bf16[32,2,128,128]{3,2,1,0:T(8,128)(2,1)}, u32[]{:S(2)}) copy-start(bf16[32,2,128,128]{3,2,1,0:T(8,128)(2,1)} %param.18) | copy-start | bytes 6291460
  72.0 7.6 %collective-permute-start.20 = (bf16[16,3072]{1,0:T(8,128)(2,1)S(1)}, bf16[16,3072]{1,0:T(8,128)(2,1)S(1)}, u32[]{:S(2)}, u32[]{:S(2)}) collective-permute-start(bf16[16,3072]{1,0:T(8,128)(2,1)S(1)} %get-tuple-element.81), channel_id=1, source_target_pairs={{0,12},{2,14},{4,8},{6,10},{8,4},{10,6},{12,0},{14,2},{1,13},{3,15... | collective-permute-start | bytes 294920 | tf_op jit(solution)/shard_map/ppermute | solution.py:149
  74.4 12.3 %collective-permute-start.19 = (bf16[16,3072]{1,0:T(8,128)(2,1)S(1)}, bf16[16,3072]{1,0:T(8,128)(2,1)S(1)}, u32[]{:S(2)}, u32[]{:S(2)}) collective-permute-start(bf16[16,3072]{1,0:T(8,128)(2,1)S(1)} %get-tuple-element.82), channel_id=1, source_target_pairs={{0,8},{2,10},{4,12},{6,14},{8,0},{10,2},{12,4},{14,6},{1,9},{3,11}... | collective-permute-start | bytes 294920 | tf_op jit(solution)/shard_map/ppermute | solution.py:149
  74.5 12.3 %collective-permute-start.18 = (bf16[16,3072]{1,0:T(8,128)(2,1)S(1)}, bf16[16,3072]{1,0:T(8,128)(2,1)S(1)}, u32[]{:S(2)}, u32[]{:S(2)}) collective-permute-start(bf16[16,3072]{1,0:T(8,128)(2,1)S(1)} %get-tuple-element.80), channel_id=1, source_target_pairs={{0,4},{2,6},{4,0},{6,2},{8,12},{10,14},{12,8},{14,10},{1,5},{3,7},... | collective-permute-start | bytes 294920 | tf_op jit(solution)/shard_map/ppermute | solution.py:149
  76.5 12.0 %collective-permute-start.14 = (bf16[16,3072]{1,0:T(8,128)(2,1)S(1)}, bf16[16,3072]{1,0:T(8,128)(2,1)S(1)}, u32[]{:S(2)}, u32[]{:S(2)}) collective-permute-start(bf16[16,3072]{1,0:T(8,128)(2,1)S(1)} %get-tuple-element.78), channel_id=1, source_target_pairs={{0,12},{2,14},{4,8},{6,10},{8,4},{10,6},{12,0},{14,2},{1,13},{3,15... | collective-permute-start | bytes 294920 | tf_op jit(solution)/shard_map/ppermute | solution.py:149
  78.9 12.6 %collective-permute-start.13 = (bf16[16,3072]{1,0:T(8,128)(2,1)S(1)}, bf16[16,3072]{1,0:T(8,128)(2,1)S(1)}, u32[]{:S(2)}, u32[]{:S(2)}) collective-permute-start(bf16[16,3072]{1,0:T(8,128)(2,1)S(1)} %get-tuple-element.79), channel_id=1, source_target_pairs={{0,8},{2,10},{4,12},{6,14},{8,0},{10,2},{12,4},{14,6},{1,9},{3,11}... | collective-permute-start | bytes 294920 | tf_op jit(solution)/shard_map/ppermute | solution.py:149
  79.6 11.9 %collective-permute-start.12 = (bf16[16,3072]{1,0:T(8,128)(2,1)S(1)}, bf16[16,3072]{1,0:T(8,128)(2,1)S(1)}, u32[]{:S(2)}, u32[]{:S(2)}) collective-permute-start(bf16[16,3072]{1,0:T(8,128)(2,1)S(1)} %get-tuple-element.77), channel_id=1, source_target_pairs={{0,4},{2,6},{4,0},{6,2},{8,12},{10,14},{12,8},{14,10},{1,5},{3,7},... | collective-permute-start | bytes 294920 | tf_op jit(solution)/shard_map/ppermute | solution.py:149
  86.9 4.7 %collective-permute-start.21 = (bf16[16,3072]{1,0:T(8,128)(2,1)S(1)}, bf16[16,3072]{1,0:T(8,128)(2,1)S(1)}, u32[]{:S(2)}, u32[]{:S(2)}) collective-permute-start(bf16[16,3072]{1,0:T(8,128)(2,1)S(1)} %fusion.15), channel_id=1, source_target_pairs={{0,2},{2,0},{4,6},{6,4},{8,10},{10,8},{12,14},{14,12},{1,3},{3,1},... | collective-permute-start | bytes 294920 | tf_op jit(solution)/shard_map/ppermute | solution.py:146
  91.7 1.4 %collective-permute-start.22 = (bf16[16,3072]{1,0:T(8,128)(2,1)S(1)}, bf16[16,3072]{1,0:T(8,128)(2,1)S(1)}, u32[]{:S(2)}, u32[]{:S(2)}) collective-permute-start(bf16[16,3072]{1,0:T(8,128)(2,1)S(1)} %add_convert_fusion), channel_id=1, source_target_pairs={{0,1},{1,0},{2,3},{3,2},{4,5},{5,4},{6,7},{7,6},{8,9},{9,8},{10,11... | collective-permute-start | bytes 294920 | tf_op jit(solution)/shard_map/ppermute | solution.py:143

commit v2 on v1

--- a/solution.py
+++ b/solution.py
@@ -163,7 +163,6 @@
     gathered = jnp.stack([brought] + [over(brought, k) for k in range(1, groups)])
 
     hidden_half = cut(hidden_in, side * half, half, 0)
-    attn_out = attend(queries, key_new, value_new, cache_keys, cache_values, lengths)
     expert = tok // (toks // experts)
     expert_ids = jnp.arange(experts, dtype=jnp.int32)
 
@@ -184,23 +183,10 @@
     even = parity == 0
     first_side = side == 0
     corner = level * half
-    (attn_out, own_masks, far_masks, order, starts, shares_order, even, first_side, corner, side, away) = (
-        lax.optimization_barrier(
-            (
-                attn_out,
-                own_masks,
-                far_masks,
-                order,
-                starts,
-                shares_order,
-                even,
-                first_side,
-                corner,
-                side,
-                1 - side,
-            )
-        )
-    )
+    ahead = (own_masks, far_masks, order, starts, shares_order, even, first_side, corner, side)
+    queries, ahead, away = lax.optimization_barrier((queries, ahead, 1 - side))
+    own_masks, far_masks, order, starts, shares_order, even, first_side, corner, side = ahead
+    attn_out = attend(queries, key_new, value_new, cache_keys, cache_values, lengths)
     staged = [stage(w) for w in (gate_weight, up_weight, down_weight)]
     arrived = []
     for k in range(lines):
@@ -251,9 +237,10 @@
     def reduce_line(values, weights):
         weighted = (values * weights).reshape(lines, half, width)
         low = weighted.astype(jnp.bfloat16)
-        return pick(weighted, order[0]), [
-            line(pick(low, order[k]), k) for k in range(1, lines)
-        ]
+        others = []
+        for k in range(1, lines):
+            others.append(line(pick(low, order[k]), k))
+        return pick(weighted, order[0]), others
 
     own_part, own_others = reduce_line(kept + back.astype(jnp.float32), scale)
     distant, _ = lax.optimization_barrier((distant, own_part))

time: 94.1 us -> 94.1 us (level)
  no operation moved by 1% of the time
where the time goes in v2:
time: 94.1 us; the launch traced here: 93.8 us
  waiting for transfers between devices  30.3 us (32%)
  starting transfers between devices  26 us (28%)
  Pallas kernels  24.1 us (26%)
  matrix products  5.76 us (6%)
  other arithmetic  4.17 us (4%)
  local copies, waits for them, and re-layouts  2.87 us (3%)
    ppermute x12, starting transfers between devices, line(): return lax.ppermute(value, 'tok', [(t, t ^ 2 * k) for t in range(toks)])  17.3 us
    pallas_call x3, Pallas kernels, stage(): pl.pallas_call(body, in_specs=[pl.BlockSpec(memory_space=pltpu.HBM)], out...  13.7 us
    ppermute x12, waiting for transfers between devices, line(): return lax.ppermute(value, 'tok', [(t, t ^ 2 * k) for t in range(toks)])  12.9 us
    pallas_call x2, Pallas kernels, run_experts(): pl.pallas_call(experts_kernel, in_specs=[fast] * 5, out_specs=[fast] * 2,...  10.4 us
    ppermute x1, waiting for transfers between devices, over(): return lax.ppermute(value, 'grp', [(g, g ^ k) for g in range(groups)])  7.95 us
    ppermute x6, waiting for transfers between devices, across(): return lax.ppermute(value, 'side', side_swap)  6.64 us
    ppermute x4, starting transfers between devices, near(): return lax.ppermute(value, 'tok', first_swap)  6.31 us
    ppermute x4, waiting for transfers between devices, near(): return lax.ppermute(value, 'tok', first_swap)  2.8 us
  transfers between devices with their start and end apart: 23, of which 12 were waited for; matrix products, arithmetic and copies ran while one was open for 9% of the time, Pallas kernels for 20%

profile of v2, /device:TPU:0, one launch (start us, length us, event | category | flops | bytes accessed | tf_op | source)
XLA Modules:
  0.0 93.8 jit_solution(6101978570054624654)
XLA Ops:
  0.0 1.3 %constant_dynamic-slice_fusion.1 = (bf16[512,384]{1,0:T(8,128)(2,1)S(1)}, bf16[512,384]{1,0:T(8,128)(2,1)S(1)}) fusion(bf16[1536,384]{1,0:T(8,128)(2,1)} %param.21, s32[]{:T(128)S(6)} %mul.133), kind=kLoop, calls=%fused_computation.80 | loop fusion | bytes 1572868 | tf_op jit(solution)/shard_map/dynamic_slice | solution.py:50
  1.4 3.1 %collective-permute-start.5 = (bf16[512,384]{1,0:T(8,128)(2,1)S(1)}, bf16[512,384]{1,0:T(8,128)(2,1)}, u32[]{:S(2)}, u32[]{:S(2)}) collective-permute-start(bf16[512,384]{1,0:T(8,128)(2,1)S(1)} %get-tuple-element.74), channel_id=1, source_target_pairs={{0,2},{2,0},{4,6},{6,4},{8,10},{10,8},{12,14},{14,12},{1,3},{3,1},... | collective-permute-start | bytes 1179656 | tf_op jit(solution)/shard_map/ppermute | solution.py:146
  4.5 0.8 reshape.115
  5.5 0.9 iota_compare_fusion
  6.4 0.7 convert_element_type.87
  7.2 1.1 %fusion.18 = f32[32,2,1,6]{3,2,1,0:T(1,128)S(1)} fusion(bf16[32,2,6,128]{3,0,2,1:T(8,128)(2,1)} %bitcast.101, bf16[32,2,128,1]{2,1,0,3:T(2,128)(2,1)} %bitcast.110), kind=kOutput, calls=%fused_computation.40 | convolution fusion | flops 98304 | bytes 116224 | tf_op jit(solution)/shard_map/skgd,skd->skg/dot_general | solution.py:24
  8.3 1.3 %fusion.37 = (f32[32,2,6]{2,1,0:T(2,128)S(1)}, f32[32,2,6,128]{3,2,1,0:T(8,128)S(1)}) fusion(bf16[32,2,128,128]{3,2,1,0:T(8,128)(2,1)S(1)} %copy-done, bf16[32,2,6,128]{3,0,2,1:T(8,128)(2,1)S(1)} %bitcast.102, pred[32,128]{1,0:T(8,128)(4,1)S(1)} %iota_compare_fusion), kind=kOutput, calls=%fused_computation.103 | convolution fusion | flops 12729984 | bytes 2397696 | tf_op jit(solution)/shard_map/skgd,skpd->skgp/dot_general | solution.py:18
  9.6 0.3 fusion.12
  10.0 0.7 fusion.7
  10.7 0.1 reshape.117
  10.9 0.1 fusion.32
  11.1 2.1 %collective-permute-start = (bf16[40,1536]{1,0:T(8,128)(2,1)S(1)}, bf16[40,1536]{1,0:T(8,128)(2,1)S(1)}, u32[]{:S(2)}, u32[]{:S(2)}) collective-permute-start(bf16[40,1536]{1,0:T(8,128)(2,1)S(1)} %get-tuple-element.114), channel_id=1, source_target_pairs={{0,4},{2,6},{4,0},{6,2},{8,12},{10,14},{12,8},{14,10},{1,5},{3,7},... | collective-permute-start | bytes 368648 | tf_op jit(solution)/shard_map/ppermute | solution.py:149
  13.2 2.6 %collective-permute-start.1 = (bf16[40,1536]{1,0:T(8,128)(2,1)S(1)}, bf16[40,1536]{1,0:T(8,128)(2,1)S(1)}, u32[]{:S(2)}, u32[]{:S(2)}) collective-permute-start(bf16[40,1536]{1,0:T(8,128)(2,1)S(1)} %get-tuple-element.115), channel_id=1, source_target_pairs={{0,8},{2,10},{4,12},{6,14},{8,0},{10,2},{12,4},{14,6},{1,9},{3,11}... | collective-permute-start | bytes 368648 | tf_op jit(solution)/shard_map/ppermute | solution.py:149
  15.7 4.6 %stage.3.gate = bf16[3072,2048]{1,0:T(8,128)(2,1)S(1)} custom-call(bf16[3072,2048]{1,0:T(8,128)(2,1)} %source.3), custom_call_target="tpu_custom_call" | custom-call | flops 3774873600 | bytes 12582912 | tf_op jit(solution)/shard_map/stage/pallas_call | solution.py:72
  20.3 4.6 %stage.4.up = bf16[3072,2048]{1,0:T(8,128)(2,1)S(1)} custom-call(bf16[3072,2048]{1,0:T(8,128)(2,1)} %source.4), custom_call_target="tpu_custom_call" | custom-call | flops 3774873600 | bytes 12582912 | tf_op jit(solution)/shard_map/stage/pallas_call | solution.py:72
  25.0 1.8 %collective-permute-start.4 = (bf16[512,384]{1,0:T(8,128)(2,1)S(1)}, bf16[512,384]{1,0:T(8,128)(2,1)S(1)}, u32[]{:S(2)}, u32[]{:S(2)}) collective-permute-start(bf16[512,384]{1,0:T(8,128)(2,1)S(1)} %collective-permute-done.3), channel_id=1, source_target_pairs={{0,16},{16,0},{1,17},{17,1},{2,18},{18,2},{3,19},{19,3},{4,20},{20... | collective-permute-start | bytes 1179656 | tf_op jit(solution)/shard_map/ppermute | solution.py:157
  26.8 7.9 %collective-permute-done.4 = bf16[512,384]{1,0:T(8,128)(2,1)S(1)} collective-permute-done((bf16[512,384]{1,0:T(8,128)(2,1)S(1)}, bf16[512,384]{1,0:T(8,128)(2,1)S(1)}, u32[]{:S(2)}, u32[]{:S(2)}) %collective-permute-start.4) | collective-permute-done | bytes 393248 | tf_op jit(solution)/shard_map/ppermute | solution.py:157
  34.8 0.3 fusion.11
  35.1 1.5 %fusion = f32[128,384]{1,0:T(8,128)S(1)} fusion(bf16[512,384]{1,0:T(8,128)(2,1)} %collective-permute-done.5, bf16[512,384]{1,0:T(8,128)(2,1)S(1)} %get-tuple-element.76, bf16[512,384]{1,0:T(8,128)(2,1)S(1)} %get-tuple-element.75, bf16[32,1536]{1,0:T(8,128)(2,1)S(1)} %slice.106, bf16[32,1536]{1,0:T(8,128)(2,1)S(1)} %slice.105, ...), kind=kOutput, calls=%fused_computation | convolution fusion | flops 156106752 | bytes 1769472 | tf_op jit(solution)/shard_map/dot_general | solution.py:211
  36.6 0.4 broadcast_select_fusion.1
  37.1 1.4 %collective-permute-done.6 = f32[4,16,768]{2,1,0:T(8,128)S(1)} collective-permute-done((f32[4,16,768]{2,1,0:T(8,128)S(1)}, f32[4,16,768]{2,1,0:T(8,128)S(1)}, u32[]{:S(2)}, u32[]{:S(2)}) %collective-permute-start.6) | collective-permute-done | bytes 196640 | tf_op jit(solution)/shard_map/ppermute | solution.py:143
  38.6 3.6 %collective-permute-start.9 = (bf16[64,768]{1,0:T(8,128)(2,1)S(1)}, bf16[64,768]{1,0:T(8,128)(2,1)S(1)}, u32[]{:S(2)}, u32[]{:S(2)}) collective-permute-start(bf16[64,768]{1,0:T(8,128)(2,1)S(1)} %get-tuple-element.108), channel_id=1, source_target_pairs={{0,12},{2,14},{4,8},{6,10},{8,4},{10,6},{12,0},{14,2},{1,13},{3,15... | collective-permute-start | bytes 294920 | tf_op jit(solution)/shard_map/ppermute | solution.py:149
  42.3 0.8 collective-permute-start.7
  43.1 4.6 %stage.5.down = bf16[2048,3072]{1,0:T(8,128)(2,1)S(1)} custom-call(bf16[2048,3072]{1,0:T(8,128)(2,1)} %source.5), custom_call_target="tpu_custom_call" | custom-call | flops 3774873600 | bytes 12582912 | tf_op jit(solution)/shard_map/stage/pallas_call | solution.py:72
  47.7 3.3 %collective-permute-done.8 = bf16[64,768]{1,0:T(8,128)(2,1)S(1)} collective-permute-done((bf16[64,768]{1,0:T(8,128)(2,1)S(1)}, bf16[64,768]{1,0:T(8,128)(2,1)S(1)}, u32[]{:S(2)}, u32[]{:S(2)}) %collective-permute-start.8) | collective-permute-done | bytes 98336 | tf_op jit(solution)/shard_map/ppermute | solution.py:149
  51.0 0.2 multiply_reduce_fusion
  51.2 0.2 multiply_convert_fusion.own
  51.5 1.6 %collective-permute-start.15 = (bf16[64,3072]{1,0:T(8,128)(2,1)S(1)}, bf16[64,3072]{1,0:T(8,128)(2,1)S(1)}, u32[]{:S(2)}, u32[]{:S(2)}) collective-permute-start(bf16[64,3072]{1,0:T(8,128)(2,1)S(1)} %multiply_convert_fusion.own), channel_id=1, source_target_pairs={{0,2},{2,0},{4,6},{6,4},{8,10},{10,8},{12,14},{14,12},{1,3},{3,1},... | collective-permute-start | bytes 1179656 | tf_op jit(solution)/shard_map/ppermute | solution.py:146
  53.2 5.1 %experts.2 = (f32[64,3072]{1,0:T(8,128)S(1)}, bf16[64,3072]{1,0:T(8,128)(2,1)S(1)}) custom-call(bf16[64,3072]{1,0:T(8,128)(2,1)S(1)} %multiply_convert_fusion.own, bf16[64,3072]{1,0:T(8,128)(2,1)S(1)} %collective-permute-done.10.other, bf16[3072,2048]{1,0:T(8,128)(2,1)S(1)} %stage.3.gate, bf16[3072,2048]{1,0:T(8,128)(2,1)S(1)} %stage.4.up, ...), custom_call_target="tpu_custom_call" | custom-call | flops 11324620800 | bytes 25165824 | tf_op jit(solution)/shard_map/experts/pallas_call | solution.py:89
  58.3 0.2 collective-permute-start.11
  58.5 0.4 fusion.38
  59.0 1.1 %collective-permute-done.11 = bf16[64,3072]{1,0:T(8,128)(2,1)S(1)} collective-permute-done((bf16[64,3072]{1,0:T(8,128)(2,1)S(1)}, bf16[64,3072]{1,0:T(8,128)(2,1)S(1)}, u32[]{:S(2)}, u32[]{:S(2)}) %collective-permute-start.11) | collective-permute-done | bytes 393248 | tf_op jit(solution)/shard_map/ppermute | solution.py:143
  60.2 2.8 %collective-permute-done.15.own = bf16[64,3072]{1,0:T(8,128)(2,1)S(1)} collective-permute-done((bf16[64,3072]{1,0:T(8,128)(2,1)S(1)}, bf16[64,3072]{1,0:T(8,128)(2,1)S(1)}, u32[]{:S(2)}, u32[]{:S(2)}) %collective-permute-start.15) | collective-permute-done | bytes 393248 | tf_op jit(solution)/shard_map/ppermute | solution.py:146
  63.1 1.7 %collective-permute-done.16.other = bf16[64,3072]{1,0:T(8,128)(2,1)S(1)} collective-permute-done((bf16[64,3072]{1,0:T(8,128)(2,1)S(1)}, bf16[64,3072]{1,0:T(8,128)(2,1)S(1)}, u32[]{:S(2)}, u32[]{:S(2)}) %collective-permute-start.16) | collective-permute-done | bytes 393248 | tf_op jit(solution)/shard_map/ppermute | solution.py:143
  64.7 5.3 %experts.3 = (f32[64,3072]{1,0:T(8,128)S(1)}, bf16[64,3072]{1,0:T(8,128)(2,1)S(1)}) custom-call(bf16[64,3072]{1,0:T(8,128)(2,1)S(1)} %collective-permute-done.15.own, bf16[64,3072]{1,0:T(8,128)(2,1)S(1)} %collective-permute-done.16.other, bf16[3072,2048]{1,0:T(8,128)(2,1)S(1)} %stage.3.gate, bf16[3072,2048]{1,0:T(8,128)(2,1)S(1)} %stage.4.up, ...), custom_call_target="tpu_custom_call" | custom-call | flops 11324620800 | bytes 25165824 | tf_op jit(solution)/shard_map/experts/pallas_call | solution.py:89
  70.0 0.2 collective-permute-start.17
  70.2 0.4 fusion.39
  70.7 1.1 %collective-permute-done.17 = bf16[64,3072]{1,0:T(8,128)(2,1)S(1)} collective-permute-done((bf16[64,3072]{1,0:T(8,128)(2,1)S(1)}, bf16[64,3072]{1,0:T(8,128)(2,1)S(1)}, u32[]{:S(2)}, u32[]{:S(2)}) %collective-permute-start.17) | collective-permute-done | bytes 393248 | tf_op jit(solution)/shard_map/ppermute | solution.py:143
  72.1 2.4 %collective-permute-start.20 = (bf16[16,3072]{1,0:T(8,128)(2,1)S(1)}, bf16[16,3072]{1,0:T(8,128)(2,1)S(1)}, u32[]{:S(2)}, u32[]{:S(2)}) collective-permute-start(bf16[16,3072]{1,0:T(8,128)(2,1)S(1)} %get-tuple-element.81), channel_id=1, source_target_pairs={{0,12},{2,14},{4,8},{6,10},{8,4},{10,6},{12,0},{14,2},{1,13},{3,15... | collective-permute-start | bytes 294920 | tf_op jit(solution)/shard_map/ppermute | solution.py:149
  74.5 2.0 %collective-permute-start.18 = (bf16[16,3072]{1,0:T(8,128)(2,1)S(1)}, bf16[16,3072]{1,0:T(8,128)(2,1)S(1)}, u32[]{:S(2)}, u32[]{:S(2)}) collective-permute-start(bf16[16,3072]{1,0:T(8,128)(2,1)S(1)} %get-tuple-element.80), channel_id=1, source_target_pairs={{0,4},{2,6},{4,0},{6,2},{8,12},{10,14},{12,8},{14,10},{1,5},{3,7},... | collective-permute-start | bytes 294920 | tf_op jit(solution)/shard_map/ppermute | solution.py:149
  76.5 2.4 %collective-permute-start.14 = (bf16[16,3072]{1,0:T(8,128)(2,1)S(1)}, bf16[16,3072]{1,0:T(8,128)(2,1)S(1)}, u32[]{:S(2)}, u32[]{:S(2)}) collective-permute-start(bf16[16,3072]{1,0:T(8,128)(2,1)S(1)} %get-tuple-element.78), channel_id=1, source_target_pairs={{0,12},{2,14},{4,8},{6,10},{8,4},{10,6},{12,0},{14,2},{1,13},{3,15... | collective-permute-start | bytes 294920 | tf_op jit(solution)/shard_map/ppermute | solution.py:149
  78.9 0.7 collective-permute-done.20
  79.7 1.3 %collective-permute-start.12 = (bf16[16,3072]{1,0:T(8,128)(2,1)S(1)}, bf16[16,3072]{1,0:T(8,128)(2,1)S(1)}, u32[]{:S(2)}, u32[]{:S(2)}) collective-permute-start(bf16[16,3072]{1,0:T(8,128)(2,1)S(1)} %get-tuple-element.77), channel_id=1, source_target_pairs={{0,4},{2,6},{4,0},{6,2},{8,12},{10,14},{12,8},{14,10},{1,5},{3,7},... | collective-permute-start | bytes 294920 | tf_op jit(solution)/shard_map/ppermute | solution.py:149
  81.0 5.8 %collective-permute-done.19 = bf16[16,3072]{1,0:T(8,128)(2,1)S(1)} collective-permute-done((bf16[16,3072]{1,0:T(8,128)(2,1)S(1)}, bf16[16,3072]{1,0:T(8,128)(2,1)S(1)}, u32[]{:S(2)}, u32[]{:S(2)}) %collective-permute-start.19) | collective-permute-done | bytes 98336 | tf_op jit(solution)/shard_map/ppermute | solution.py:149
  86.8 1.6 %collective-permute-start.21 = (bf16[16,3072]{1,0:T(8,128)(2,1)S(1)}, bf16[16,3072]{1,0:T(8,128)(2,1)S(1)}, u32[]{:S(2)}, u32[]{:S(2)}) collective-permute-start(bf16[16,3072]{1,0:T(8,128)(2,1)S(1)} %fusion.15), channel_id=1, source_target_pairs={{0,2},{2,0},{4,6},{6,4},{8,10},{10,8},{12,14},{14,12},{1,3},{3,1},... | collective-permute-start | bytes 294920 | tf_op jit(solution)/shard_map/ppermute | solution.py:146
  88.5 3.1 %collective-permute-done.13 = bf16[16,3072]{1,0:T(8,128)(2,1)S(1)} collective-permute-done((bf16[16,3072]{1,0:T(8,128)(2,1)S(1)}, bf16[16,3072]{1,0:T(8,128)(2,1)S(1)}, u32[]{:S(2)}, u32[]{:S(2)}) %collective-permute-start.13) | collective-permute-done | bytes 98336 | tf_op jit(solution)/shard_map/ppermute | solution.py:149
  91.8 1.2 %collective-permute-done.22 = bf16[16,3072]{1,0:T(8,128)(2,1)S(1)} collective-permute-done((bf16[16,3072]{1,0:T(8,128)(2,1)S(1)}, bf16[16,3072]{1,0:T(8,128)(2,1)S(1)}, u32[]{:S(2)}, u32[]{:S(2)}) %collective-permute-start.22) | collective-permute-done | bytes 98336 | tf_op jit(solution)/shard_map/ppermute | solution.py:143
  93.1 0.7 pad_maximum_fusion.3
  (80 shorter events, 1.9 us)
Async XLA Ops:
  0.0 8.3 %copy-start = (bf16[32,2,128,128]{3,2,1,0:T(8,128)(2,1)S(1)}, bf16[32,2,128,128]{3,2,1,0:T(8,128)(2,1)}, u32[]{:S(2)}) copy-start(bf16[32,2,128,128]{3,2,1,0:T(8,128)(2,1)} %param.18) | copy-start | bytes 6291460
  0.0 8.3 %copy-start.4 = (bf16[32,12,128]{2,0,1:T(8,128)(2,1)S(1)}, bf16[32,12,128]{2,0,1:T(8,128)(2,1)}, u32[]{:S(2)}) copy-start(bf16[32,12,128]{2,0,1:T(8,128)(2,1)} %param.15) | copy-start | bytes 294916
  1.4 33.7 %collective-permute-start.5 = (bf16[512,384]{1,0:T(8,128)(2,1)S(1)}, bf16[512,384]{1,0:T(8,128)(2,1)}, u32[]{:S(2)}, u32[]{:S(2)}) collective-permute-start(bf16[512,384]{1,0:T(8,128)(2,1)S(1)} %get-tuple-element.74), channel_id=1, source_target_pairs={{0,2},{2,0},{4,6},{6,4},{8,10},{10,8},{12,14},{14,12},{1,3},{3,1},... | collective-permute-start | bytes 1179656 | tf_op jit(solution)/shard_map/ppermute | solution.py:146
  4.4 20.5 %collective-permute-start.3 = (bf16[512,384]{1,0:T(8,128)(2,1)S(1)}, bf16[512,384]{1,0:T(8,128)(2,1)S(1)}, u32[]{:S(2)}, u32[]{:S(2)}) collective-permute-start(bf16[512,384]{1,0:T(8,128)(2,1)S(1)} %get-tuple-element.73), channel_id=1, source_target_pairs={{0,2},{2,0},{4,6},{6,4},{8,10},{10,8},{12,14},{14,12},{1,3},{3,1},... | collective-permute-start | bytes 1179656 | tf_op jit(solution)/shard_map/ppermute | solution.py:146
  5.5 4.4 %copy-start.7 = (bf16[32,2,128,128]{3,2,1,0:T(8,128)(2,1)S(1)}, bf16[32,2,128,128]{3,2,1,0:T(8,128)(2,1)}, u32[]{:S(2)}) copy-start(bf16[32,2,128,128]{3,2,1,0:T(8,128)(2,1)} %param.19) | copy-start | bytes 6291460
  10.0 0.9 copy-start.5
  11.1 13.8 %collective-permute-start = (bf16[40,1536]{1,0:T(8,128)(2,1)S(1)}, bf16[40,1536]{1,0:T(8,128)(2,1)S(1)}, u32[]{:S(2)}, u32[]{:S(2)}) collective-permute-start(bf16[40,1536]{1,0:T(8,128)(2,1)S(1)} %get-tuple-element.114), channel_id=1, source_target_pairs={{0,4},{2,6},{4,0},{6,2},{8,12},{10,14},{12,8},{14,10},{1,5},{3,7},... | collective-permute-start | bytes 368648 | tf_op jit(solution)/shard_map/ppermute | solution.py:149
  13.2 11.8 %collective-permute-start.1 = (bf16[40,1536]{1,0:T(8,128)(2,1)S(1)}, bf16[40,1536]{1,0:T(8,128)(2,1)S(1)}, u32[]{:S(2)}, u32[]{:S(2)}) collective-permute-start(bf16[40,1536]{1,0:T(8,128)(2,1)S(1)} %get-tuple-element.115), channel_id=1, source_target_pairs={{0,8},{2,10},{4,12},{6,14},{8,0},{10,2},{12,4},{14,6},{1,9},{3,11}... | collective-permute-start | bytes 368648 | tf_op jit(solution)/shard_map/ppermute | solution.py:149
  15.7 9.2 %collective-permute-start.2 = (bf16[40,1536]{1,0:T(8,128)(2,1)S(1)}, bf16[40,1536]{1,0:T(8,128)(2,1)S(1)}, u32[]{:S(2)}, u32[]{:S(2)}) collective-permute-start(bf16[40,1536]{1,0:T(8,128)(2,1)S(1)} %get-tuple-element.113), channel_id=1, source_target_pairs={{0,12},{2,14},{4,8},{6,10},{8,4},{10,6},{12,0},{14,2},{1,13},{3,15... | collective-permute-start | bytes 368648 | tf_op jit(solution)/shard_map/ppermute | solution.py:149
  25.0 9.8 %collective-permute-start.4 = (bf16[512,384]{1,0:T(8,128)(2,1)S(1)}, bf16[512,384]{1,0:T(8,128)(2,1)S(1)}, u32[]{:S(2)}, u32[]{:S(2)}) collective-permute-start(bf16[512,384]{1,0:T(8,128)(2,1)S(1)} %collective-permute-done.3), channel_id=1, source_target_pairs={{0,16},{16,0},{1,17},{17,1},{2,18},{18,2},{3,19},{19,3},{4,20},{20... | collective-permute-start | bytes 1179656 | tf_op jit(solution)/shard_map/ppermute | solution.py:157
  35.1 1.5 %copy-start.2 = (bf16[1536,384]{1,0:T(8,128)(2,1)S(1)}, bf16[1536,384]{1,0:T(8,128)(2,1)}, u32[]{:S(2)}) copy-start(bf16[1536,384]{1,0:T(8,128)(2,1)} %param.21) | copy-start | bytes 3538948
  37.0 1.5 %collective-permute-start.6 = (f32[4,16,768]{2,1,0:T(8,128)S(1)}, f32[4,16,768]{2,1,0:T(8,128)S(1)}, u32[]{:S(2)}, u32[]{:S(2)}) collective-permute-start(f32[4,16,768]{2,1,0:T(8,128)S(1)} %dynamic-slice_bitcast_fusion.1), channel_id=1, source_target_pairs={{0,1},{1,0},{2,3},{3,2},{4,5},{5,4},{6,7},{7,6},{8,9},{9,8},{10,11... | collective-permute-start | bytes 589832 | tf_op jit(solution)/shard_map/ppermute | solution.py:143
  38.6 12.6 %copy-start.6 = (f32[3072]{0:T(1024)S(1)}, f32[3072]{0:T(1024)}, u32[]{:S(2)}) copy-start(f32[3072]{0:T(1024)} %param.22) | copy-start | bytes 36868
  38.6 9.0 %collective-permute-start.9 = (bf16[64,768]{1,0:T(8,128)(2,1)S(1)}, bf16[64,768]{1,0:T(8,128)(2,1)S(1)}, u32[]{:S(2)}, u32[]{:S(2)}) collective-permute-start(bf16[64,768]{1,0:T(8,128)(2,1)S(1)} %get-tuple-element.108), channel_id=1, source_target_pairs={{0,12},{2,14},{4,8},{6,10},{8,4},{10,6},{12,0},{14,2},{1,13},{3,15... | collective-permute-start | bytes 294920 | tf_op jit(solution)/shard_map/ppermute | solution.py:149
  42.2 8.7 %collective-permute-start.8 = (bf16[64,768]{1,0:T(8,128)(2,1)S(1)}, bf16[64,768]{1,0:T(8,128)(2,1)S(1)}, u32[]{:S(2)}, u32[]{:S(2)}) collective-permute-start(bf16[64,768]{1,0:T(8,128)(2,1)S(1)} %get-tuple-element.108), channel_id=1, source_target_pairs={{0,8},{2,10},{4,12},{6,14},{8,0},{10,2},{12,4},{14,6},{1,9},{3,11}... | collective-permute-start | bytes 294920 | tf_op jit(solution)/shard_map/ppermute | solution.py:149
  42.3 8.7 %collective-permute-start.7 = (bf16[64,768]{1,0:T(8,128)(2,1)S(1)}, bf16[64,768]{1,0:T(8,128)(2,1)S(1)}, u32[]{:S(2)}, u32[]{:S(2)}) collective-permute-start(bf16[64,768]{1,0:T(8,128)(2,1)S(1)} %get-tuple-element.108), channel_id=1, source_target_pairs={{0,4},{2,6},{4,0},{6,2},{8,12},{10,14},{12,8},{14,10},{1,5},{3,7},... | collective-permute-start | bytes 294920 | tf_op jit(solution)/shard_map/ppermute | solution.py:149
  51.4 7.1 %copy-start.3 = (f32[3072,4]{0,1:T(4,128)S(1)}, f32[3072,4]{0,1:T(4,128)}, u32[]{:S(2)}) copy-start(f32[3072,4]{0,1:T(4,128)} %param.23) | copy-start | bytes 147460
  51.4 1.8 %collective-permute-start.10 = (bf16[64,3072]{1,0:T(8,128)(2,1)S(1)}, bf16[64,3072]{1,0:T(8,128)(2,1)S(1)}, u32[]{:S(2)}, u32[]{:S(2)}) collective-permute-start(bf16[64,3072]{1,0:T(8,128)(2,1)S(1)} %multiply_convert_fusion.own), channel_id=1, source_target_pairs={{0,1},{1,0},{2,3},{3,2},{4,5},{5,4},{6,7},{7,6},{8,9},{9,8},{10,11... | collective-permute-start | bytes 1179656 | tf_op jit(solution)/shard_map/ppermute | solution.py:143
  51.5 11.5 %collective-permute-start.15 = (bf16[64,3072]{1,0:T(8,128)(2,1)S(1)}, bf16[64,3072]{1,0:T(8,128)(2,1)S(1)}, u32[]{:S(2)}, u32[]{:S(2)}) collective-permute-start(bf16[64,3072]{1,0:T(8,128)(2,1)S(1)} %multiply_convert_fusion.own), channel_id=1, source_target_pairs={{0,2},{2,0},{4,6},{6,4},{8,10},{10,8},{12,14},{14,12},{1,3},{3,1},... | collective-permute-start | bytes 1179656 | tf_op jit(solution)/shard_map/ppermute | solution.py:146
  58.3 1.8 %collective-permute-start.11 = (bf16[64,3072]{1,0:T(8,128)(2,1)S(1)}, bf16[64,3072]{1,0:T(8,128)(2,1)S(1)}, u32[]{:S(2)}, u32[]{:S(2)}) collective-permute-start(bf16[64,3072]{1,0:T(8,128)(2,1)S(1)} %get-tuple-element.65), channel_id=1, source_target_pairs={{0,1},{1,0},{2,3},{3,2},{4,5},{5,4},{6,7},{7,6},{8,9},{9,8},{10,11... | collective-permute-start | bytes 1179656 | tf_op jit(solution)/shard_map/ppermute | solution.py:143
  63.0 1.7 %collective-permute-start.16 = (bf16[64,3072]{1,0:T(8,128)(2,1)S(1)}, bf16[64,3072]{1,0:T(8,128)(2,1)S(1)}, u32[]{:S(2)}, u32[]{:S(2)}) collective-permute-start(bf16[64,3072]{1,0:T(8,128)(2,1)S(1)} %collective-permute-done.15.own), channel_id=1, source_target_pairs={{0,1},{1,0},{2,3},{3,2},{4,5},{5,4},{6,7},{7,6},{8,9},{9,8},{10,11... | collective-permute-start | bytes 1179656 | tf_op jit(solution)/shard_map/ppermute | solution.py:143
  70.0 1.8 %collective-permute-start.17 = (bf16[64,3072]{1,0:T(8,128)(2,1)S(1)}, bf16[64,3072]{1,0:T(8,128)(2,1)S(1)}, u32[]{:S(2)}, u32[]{:S(2)}) collective-permute-start(bf16[64,3072]{1,0:T(8,128)(2,1)S(1)} %get-tuple-element.70), channel_id=1, source_target_pairs={{0,1},{1,0},{2,3},{3,2},{4,5},{5,4},{6,7},{7,6},{8,9},{9,8},{10,11... | collective-permute-start | bytes 1179656 | tf_op jit(solution)/shard_map/ppermute | solution.py:143
  71.9 21.8 %copy-start.1 = (bf16[32,2,128,128]{3,2,1,0:T(8,128)(2,1)S(1)}, bf16[32,2,128,128]{3,2,1,0:T(8,128)(2,1)}, u32[]{:S(2)}) copy-start(bf16[32,2,128,128]{3,2,1,0:T(8,128)(2,1)} %param.18) | copy-start | bytes 6291460
  72.1 7.6 %collective-permute-start.20 = (bf16[16,3072]{1,0:T(8,128)(2,1)S(1)}, bf16[16,3072]{1,0:T(8,128)(2,1)S(1)}, u32[]{:S(2)}, u32[]{:S(2)}) collective-permute-start(bf16[16,3072]{1,0:T(8,128)(2,1)S(1)} %get-tuple-element.81), channel_id=1, source_target_pairs={{0,12},{2,14},{4,8},{6,10},{8,4},{10,6},{12,0},{14,2},{1,13},{3,15... | collective-permute-start | bytes 294920 | tf_op jit(solution)/shard_map/ppermute | solution.py:149
  74.5 12.3 %collective-permute-start.19 = (bf16[16,3072]{1,0:T(8,128)(2,1)S(1)}, bf16[16,3072]{1,0:T(8,128)(2,1)S(1)}, u32[]{:S(2)}, u32[]{:S(2)}) collective-permute-start(bf16[16,3072]{1,0:T(8,128)(2,1)S(1)} %get-tuple-element.82), channel_id=1, source_target_pairs={{0,8},{2,10},{4,12},{6,14},{8,0},{10,2},{12,4},{14,6},{1,9},{3,11}... | collective-permute-start | bytes 294920 | tf_op jit(solution)/shard_map/ppermute | solution.py:149
  74.5 12.3 %collective-permute-start.18 = (bf16[16,3072]{1,0:T(8,128)(2,1)S(1)}, bf16[16,3072]{1,0:T(8,128)(2,1)S(1)}, u32[]{:S(2)}, u32[]{:S(2)}) collective-permute-start(bf16[16,3072]{1,0:T(8,128)(2,1)S(1)} %get-tuple-element.80), channel_id=1, source_target_pairs={{0,4},{2,6},{4,0},{6,2},{8,12},{10,14},{12,8},{14,10},{1,5},{3,7},... | collective-permute-start | bytes 294920 | tf_op jit(solution)/shard_map/ppermute | solution.py:149
  76.5 11.9 %collective-permute-start.14 = (bf16[16,3072]{1,0:T(8,128)(2,1)S(1)}, bf16[16,3072]{1,0:T(8,128)(2,1)S(1)}, u32[]{:S(2)}, u32[]{:S(2)}) collective-permute-start(bf16[16,3072]{1,0:T(8,128)(2,1)S(1)} %get-tuple-element.78), channel_id=1, source_target_pairs={{0,12},{2,14},{4,8},{6,10},{8,4},{10,6},{12,0},{14,2},{1,13},{3,15... | collective-permute-start | bytes 294920 | tf_op jit(solution)/shard_map/ppermute | solution.py:149
  78.9 12.7 %collective-permute-start.13 = (bf16[16,3072]{1,0:T(8,128)(2,1)S(1)}, bf16[16,3072]{1,0:T(8,128)(2,1)S(1)}, u32[]{:S(2)}, u32[]{:S(2)}) collective-permute-start(bf16[16,3072]{1,0:T(8,128)(2,1)S(1)} %get-tuple-element.79), channel_id=1, source_target_pairs={{0,8},{2,10},{4,12},{6,14},{8,0},{10,2},{12,4},{14,6},{1,9},{3,11}... | collective-permute-start | bytes 294920 | tf_op jit(solution)/shard_map/ppermute | solution.py:149
  79.7 11.9 %collective-permute-start.12 = (bf16[16,3072]{1,0:T(8,128)(2,1)S(1)}, bf16[16,3072]{1,0:T(8,128)(2,1)S(1)}, u32[]{:S(2)}, u32[]{:S(2)}) collective-permute-start(bf16[16,3072]{1,0:T(8,128)(2,1)S(1)} %get-tuple-element.77), channel_id=1, source_target_pairs={{0,4},{2,6},{4,0},{6,2},{8,12},{10,14},{12,8},{14,10},{1,5},{3,7},... | collective-permute-start | bytes 294920 | tf_op jit(solution)/shard_map/ppermute | solution.py:149
  86.8 4.7 %collective-permute-start.21 = (bf16[16,3072]{1,0:T(8,128)(2,1)S(1)}, bf16[16,3072]{1,0:T(8,128)(2,1)S(1)}, u32[]{:S(2)}, u32[]{:S(2)}) collective-permute-start(bf16[16,3072]{1,0:T(8,128)(2,1)S(1)} %fusion.15), channel_id=1, source_target_pairs={{0,2},{2,0},{4,6},{6,4},{8,10},{10,8},{12,14},{14,12},{1,3},{3,1},... | collective-permute-start | bytes 294920 | tf_op jit(solution)/shard_map/ppermute | solution.py:146
  91.7 1.4 %collective-permute-start.22 = (bf16[16,3072]{1,0:T(8,128)(2,1)S(1)}, bf16[16,3072]{1,0:T(8,128)(2,1)S(1)}, u32[]{:S(2)}, u32[]{:S(2)}) collective-permute-start(bf16[16,3072]{1,0:T(8,128)(2,1)S(1)} %add_convert_fusion), channel_id=1, source_target_pairs={{0,1},{1,0},{2,3},{3,2},{4,5},{5,4},{6,7},{7,6},{8,9},{9,8},{10,11... | collective-permute-start | bytes 294920 | tf_op jit(solution)/shard_map/ppermute | solution.py:143

commit v3 on v2

--- a/solution.py
+++ b/solution.py
@@ -187,7 +187,8 @@
     queries, ahead, away = lax.optimization_barrier((queries, ahead, 1 - side))
     own_masks, far_masks, order, starts, shares_order, even, first_side, corner, side = ahead
     attn_out = attend(queries, key_new, value_new, cache_keys, cache_values, lengths)
-    staged = [stage(w) for w in (gate_weight, up_weight, down_weight)]
+    up_staged = stage(up_weight)
+    staged = [stage(gate_weight), up_staged, stage(down_weight)]
     arrived = []
     for k in range(lines):
         part = cut(hidden_half, starts[k], 2 * cols, 1)
@@ -196,7 +197,7 @@
         extra = jnp.concatenate([part[i * deep : (i + 1) * deep] for i in range(folds)], axis=1)
         message = jnp.concatenate([attn_out, extra], axis=0)
         arrived.append(line(message, k) if k else message)
-    arrived, staged[0] = lax.optimization_barrier((arrived, staged[0]))
+    arrived, staged[:2] = lax.optimization_barrier((arrived, staged[:2]))
     blocks = jnp.concatenate([m[:rows] for m in arrived], axis=0)
     hidden_blocks = jnp.stack(
         [
@@ -234,26 +235,25 @@
     kept, sent = run_experts(normed, mate_rows, *staged)
     back = across(sent)
 
-    def reduce_line(values, weights):
+    def weigh(values, weights):
         weighted = (values * weights).reshape(lines, half, width)
-        low = weighted.astype(jnp.bfloat16)
-        others = []
-        for k in range(1, lines):
-            others.append(line(pick(low, order[k]), k))
-        return pick(weighted, order[0]), others
-
-    own_part, own_others = reduce_line(kept + back.astype(jnp.float32), scale)
-    distant, _ = lax.optimization_barrier((distant, own_part))
+        return weighted, weighted.astype(jnp.bfloat16)
+
+    def slant(value, k):
+        return lax.ppermute(value, "tok", [(t, t ^ (2 * k) ^ 1) for t in range(toks)])
+
+    own_others = []
+    weighted, low = weigh(kept + back.astype(jnp.float32), scale)
+    total = pick(weighted, order[0])
+    for k in range(1, lines):
+        own_others.append(line(pick(low, order[k]), k))
+    distant, _ = lax.optimization_barrier((distant, total))
     far_mates = across(distant)
     far_kept, far_sent = run_experts(distant, far_mates, *staged)
     far_scale = scales(distant, *far_masks, router_weight)
-    far_part, far_others = reduce_line(
-        far_kept + across(far_sent).astype(jnp.float32), far_scale
-    )
-    for value in far_others:
-        far_part = far_part + value.astype(jnp.float32)
-    total = own_part
-    for value in own_others + [near(far_part.astype(jnp.bfloat16))]:
+    _, far_low = weigh(far_kept + across(far_sent).astype(jnp.float32), far_scale)
+    far_others = [slant(pick(far_low, order[k]), k) for k in reversed(range(lines))]
+    for value in own_others + far_others:
         total = total + value.astype(jnp.float32)
     result = (mine_stream + total).astype(jnp.bfloat16)
     mate = across(result)

time: 94.1 us -> 92.6 us (0.984)
  waiting for transfers between devices: 30.3 us -> 27.1 us
  starting transfers between devices: 26 us -> 27.9 us
    ppermute x0 -> x4, starting transfers between devices: none -> 7.22 us  [slant(): return lax.ppermute(value, 'tok', [(t, t ^ 2 * k ^ 1) for t in range(toks)])]
    ppermute x12 -> x9, waiting for transfers between devices: 12.9 us -> 6 us  [line(): return lax.ppermute(value, 'tok', [(t, t ^ 2 * k) for t in range(toks)])]
    ppermute x0 -> x4, waiting for transfers between devices: none -> 4.79 us  [slant(): return lax.ppermute(value, 'tok', [(t, t ^ 2 * k ^ 1) for t in range(toks)])]
    ppermute x12 -> x9, starting transfers between devices: 17.3 us -> 13.5 us  [line(): return lax.ppermute(value, 'tok', [(t, t ^ 2 * k) for t in range(toks)])]
    ppermute x4 -> x3, starting transfers between devices: 6.31 us -> 4.72 us  [near(): return lax.ppermute(value, 'tok', first_swap)]
    ppermute x6, waiting for transfers between devices: 6.64 us -> 5.52 us  [across(): return lax.ppermute(value, 'side', side_swap)]
    ppermute x4 -> x3, waiting for transfers between devices: 2.8 us -> 2.8 us  [near(): return lax.ppermute(value, 'tok', first_swap)]
where the time goes in v3:
time: 92.6 us; the launch traced here: 92.3 us
  starting transfers between devices  27.9 us (30%)
  waiting for transfers between devices  27.1 us (29%)
  Pallas kernels  24.1 us (26%)
  matrix products  5.76 us (6%)
  other arithmetic  4.09 us (4%)
  local copies, waits for them, and re-layouts  2.89 us (3%)
    pallas_call x3, Pallas kernels, stage(): pl.pallas_call(body, in_specs=[pl.BlockSpec(memory_space=pltpu.HBM)], out...  13.7 us
    ppermute x9, starting transfers between devices, line(): return lax.ppermute(value, 'tok', [(t, t ^ 2 * k) for t in range(toks)])  13.5 us
    pallas_call x2, Pallas kernels, run_experts(): pl.pallas_call(experts_kernel, in_specs=[fast] * 5, out_specs=[fast] * 2,...  10.4 us
    ppermute x1, waiting for transfers between devices, over(): return lax.ppermute(value, 'grp', [(g, g ^ k) for g in range(groups)])  7.95 us
    ppermute x4, starting transfers between devices, slant(): return lax.ppermute(value, 'tok', [(t, t ^ 2 * k ^ 1) for t in range(toks)])  7.22 us
    ppermute x9, waiting for transfers between devices, line(): return lax.ppermute(value, 'tok', [(t, t ^ 2 * k) for t in range(toks)])  6 us
    ppermute x6, waiting for transfers between devices, across(): return lax.ppermute(value, 'side', side_swap)  5.52 us
    ppermute x4, waiting for transfers between devices, slant(): return lax.ppermute(value, 'tok', [(t, t ^ 2 * k ^ 1) for t in range(toks)])  4.79 us
  transfers between devices with their start and end apart: 23, of which 12 were waited for; matrix products, arithmetic and copies ran while one was open for 9% of the time, Pallas kernels for 20%

profile of v3, /device:TPU:0, one launch (start us, length us, event | category | flops | bytes accessed | tf_op | source)
XLA Modules:
  0.0 92.3 jit_solution(6266543060089734783)
XLA Ops:
  0.0 1.3 %constant_dynamic-slice_fusion.1 = (bf16[512,384]{1,0:T(8,128)(2,1)S(1)}, bf16[512,384]{1,0:T(8,128)(2,1)S(1)}) fusion(bf16[1536,384]{1,0:T(8,128)(2,1)} %param.21, s32[]{:T(128)S(6)} %mul.133), kind=kLoop, calls=%fused_computation.77 | loop fusion | bytes 1572868 | tf_op jit(solution)/shard_map/dynamic_slice | solution.py:50
  1.4 3.1 %collective-permute-start.5 = (bf16[512,384]{1,0:T(8,128)(2,1)S(1)}, bf16[512,384]{1,0:T(8,128)(2,1)}, u32[]{:S(2)}, u32[]{:S(2)}) collective-permute-start(bf16[512,384]{1,0:T(8,128)(2,1)S(1)} %get-tuple-element.76), channel_id=1, source_target_pairs={{0,2},{2,0},{4,6},{6,4},{8,10},{10,8},{12,14},{14,12},{1,3},{3,1},... | collective-permute-start | bytes 1179656 | tf_op jit(solution)/shard_map/ppermute | solution.py:146
  4.5 0.8 reshape.114
  5.5 0.9 iota_compare_fusion
  6.4 0.7 convert_element_type.87
  7.2 1.1 %fusion.15 = f32[32,2,1,6]{3,2,1,0:T(1,128)S(1)} fusion(bf16[32,2,6,128]{3,0,2,1:T(8,128)(2,1)} %bitcast.94, bf16[32,2,128,1]{2,1,0,3:T(2,128)(2,1)} %bitcast.103), kind=kOutput, calls=%fused_computation.36 | convolution fusion | flops 98304 | bytes 116224 | tf_op jit(solution)/shard_map/skgd,skd->skg/dot_general | solution.py:24
  8.3 1.3 %fusion.34 = (f32[32,2,6]{2,1,0:T(2,128)S(1)}, f32[32,2,6,128]{3,2,1,0:T(8,128)S(1)}) fusion(bf16[32,2,128,128]{3,2,1,0:T(8,128)(2,1)S(1)} %copy-done, bf16[32,2,6,128]{3,0,2,1:T(8,128)(2,1)S(1)} %bitcast.95, pred[32,128]{1,0:T(8,128)(4,1)S(1)} %iota_compare_fusion), kind=kOutput, calls=%fused_computation.100 | convolution fusion | flops 12729984 | bytes 2397696 | tf_op jit(solution)/shard_map/skgd,skpd->skgp/dot_general | solution.py:18
  9.6 0.3 fusion.12
  10.0 0.7 fusion.7
  10.7 0.1 reshape.116
  10.9 0.1 fusion.29
  11.1 2.1 %collective-permute-start = (bf16[40,1536]{1,0:T(8,128)(2,1)S(1)}, bf16[40,1536]{1,0:T(8,128)(2,1)S(1)}, u32[]{:S(2)}, u32[]{:S(2)}) collective-permute-start(bf16[40,1536]{1,0:T(8,128)(2,1)S(1)} %get-tuple-element.117), channel_id=1, source_target_pairs={{0,4},{2,6},{4,0},{6,2},{8,12},{10,14},{12,8},{14,10},{1,5},{3,7},... | collective-permute-start | bytes 368648 | tf_op jit(solution)/shard_map/ppermute | solution.py:149
  13.2 2.6 %collective-permute-start.1 = (bf16[40,1536]{1,0:T(8,128)(2,1)S(1)}, bf16[40,1536]{1,0:T(8,128)(2,1)S(1)}, u32[]{:S(2)}, u32[]{:S(2)}) collective-permute-start(bf16[40,1536]{1,0:T(8,128)(2,1)S(1)} %get-tuple-element.118), channel_id=1, source_target_pairs={{0,8},{2,10},{4,12},{6,14},{8,0},{10,2},{12,4},{14,6},{1,9},{3,11}... | collective-permute-start | bytes 368648 | tf_op jit(solution)/shard_map/ppermute | solution.py:149
  15.7 4.6 %stage.3.gate = bf16[3072,2048]{1,0:T(8,128)(2,1)S(1)} custom-call(bf16[3072,2048]{1,0:T(8,128)(2,1)} %source.3), custom_call_target="tpu_custom_call" | custom-call | flops 3774873600 | bytes 12582912 | tf_op jit(solution)/shard_map/stage/pallas_call | solution.py:72
  20.3 4.6 %stage.4.up = bf16[3072,2048]{1,0:T(8,128)(2,1)S(1)} custom-call(bf16[3072,2048]{1,0:T(8,128)(2,1)} %source.4), custom_call_target="tpu_custom_call" | custom-call | flops 3774873600 | bytes 12582912 | tf_op jit(solution)/shard_map/stage/pallas_call | solution.py:72
  25.0 1.8 %collective-permute-start.4 = (bf16[512,384]{1,0:T(8,128)(2,1)S(1)}, bf16[512,384]{1,0:T(8,128)(2,1)S(1)}, u32[]{:S(2)}, u32[]{:S(2)}) collective-permute-start(bf16[512,384]{1,0:T(8,128)(2,1)S(1)} %collective-permute-done.3), channel_id=1, source_target_pairs={{0,16},{16,0},{1,17},{17,1},{2,18},{18,2},{3,19},{19,3},{4,20},{20... | collective-permute-start | bytes 1179656 | tf_op jit(solution)/shard_map/ppermute | solution.py:157
  26.8 7.9 %collective-permute-done.4 = bf16[512,384]{1,0:T(8,128)(2,1)S(1)} collective-permute-done((bf16[512,384]{1,0:T(8,128)(2,1)S(1)}, bf16[512,384]{1,0:T(8,128)(2,1)S(1)}, u32[]{:S(2)}, u32[]{:S(2)}) %collective-permute-start.4) | collective-permute-done | bytes 393248 | tf_op jit(solution)/shard_map/ppermute | solution.py:157
  34.8 0.3 fusion.11
  35.1 1.5 %fusion = f32[128,384]{1,0:T(8,128)S(1)} fusion(bf16[512,384]{1,0:T(8,128)(2,1)} %collective-permute-done.5, bf16[512,384]{1,0:T(8,128)(2,1)S(1)} %get-tuple-element.78, bf16[512,384]{1,0:T(8,128)(2,1)S(1)} %get-tuple-element.77, bf16[32,1536]{1,0:T(8,128)(2,1)S(1)} %slice.106, bf16[32,1536]{1,0:T(8,128)(2,1)S(1)} %slice.105, ...), kind=kOutput, calls=%fused_computation | convolution fusion | flops 156106752 | bytes 1769472 | tf_op jit(solution)/shard_map/dot_general | solution.py:212
  36.6 0.4 broadcast_select_fusion.1
  37.1 1.4 %collective-permute-done.6 = f32[4,16,768]{2,1,0:T(8,128)S(1)} collective-permute-done((f32[4,16,768]{2,1,0:T(8,128)S(1)}, f32[4,16,768]{2,1,0:T(8,128)S(1)}, u32[]{:S(2)}, u32[]{:S(2)}) %collective-permute-start.6) | collective-permute-done | bytes 196640 | tf_op jit(solution)/shard_map/ppermute | solution.py:143
  38.6 3.6 %collective-permute-start.9 = (bf16[64,768]{1,0:T(8,128)(2,1)S(1)}, bf16[64,768]{1,0:T(8,128)(2,1)S(1)}, u32[]{:S(2)}, u32[]{:S(2)}) collective-permute-start(bf16[64,768]{1,0:T(8,128)(2,1)S(1)} %get-tuple-element.111), channel_id=1, source_target_pairs={{0,12},{2,14},{4,8},{6,10},{8,4},{10,6},{12,0},{14,2},{1,13},{3,15... | collective-permute-start | bytes 294920 | tf_op jit(solution)/shard_map/ppermute | solution.py:149
  42.3 0.8 collective-permute-start.7
  43.1 4.6 %stage.5.down = bf16[2048,3072]{1,0:T(8,128)(2,1)S(1)} custom-call(bf16[2048,3072]{1,0:T(8,128)(2,1)} %source.5), custom_call_target="tpu_custom_call" | custom-call | flops 3774873600 | bytes 12582912 | tf_op jit(solution)/shard_map/stage/pallas_call | solution.py:72
  47.7 3.3 %collective-permute-done.8 = bf16[64,768]{1,0:T(8,128)(2,1)S(1)} collective-permute-done((bf16[64,768]{1,0:T(8,128)(2,1)S(1)}, bf16[64,768]{1,0:T(8,128)(2,1)S(1)}, u32[]{:S(2)}, u32[]{:S(2)}) %collective-permute-start.8) | collective-permute-done | bytes 98336 | tf_op jit(solution)/shard_map/ppermute | solution.py:149
  51.0 0.2 multiply_reduce_fusion
  51.2 0.2 multiply_convert_fusion.1.own
  51.5 1.6 %collective-permute-start.15 = (bf16[64,3072]{1,0:T(8,128)(2,1)S(1)}, bf16[64,3072]{1,0:T(8,128)(2,1)S(1)}, u32[]{:S(2)}, u32[]{:S(2)}) collective-permute-start(bf16[64,3072]{1,0:T(8,128)(2,1)S(1)} %multiply_convert_fusion.1.own), channel_id=1, source_target_pairs={{0,2},{2,0},{4,6},{6,4},{8,10},{10,8},{12,14},{14,12},{1,3},{3,1},... | collective-permute-start | bytes 1179656 | tf_op jit(solution)/shard_map/ppermute | solution.py:146
  53.2 5.1 %experts.2 = (f32[64,3072]{1,0:T(8,128)S(1)}, bf16[64,3072]{1,0:T(8,128)(2,1)S(1)}) custom-call(bf16[64,3072]{1,0:T(8,128)(2,1)S(1)} %multiply_convert_fusion.1.own, bf16[64,3072]{1,0:T(8,128)(2,1)S(1)} %collective-permute-done.10.other, bf16[3072,2048]{1,0:T(8,128)(2,1)S(1)} %stage.3.gate, bf16[3072,2048]{1,0:T(8,128)(2,1)S(1)} %stage.4.up, ...), custom_call_target="tpu_custom_call" | custom-call | flops 11324620800 | bytes 25165824 | tf_op jit(solution)/shard_map/experts/pallas_call | solution.py:89
  58.3 0.2 collective-permute-start.11
  58.5 0.4 fusion.35
  59.0 1.1 %collective-permute-done.11 = bf16[64,3072]{1,0:T(8,128)(2,1)S(1)} collective-permute-done((bf16[64,3072]{1,0:T(8,128)(2,1)S(1)}, bf16[64,3072]{1,0:T(8,128)(2,1)S(1)}, u32[]{:S(2)}, u32[]{:S(2)}) %collective-permute-start.11) | collective-permute-done | bytes 393248 | tf_op jit(solution)/shard_map/ppermute | solution.py:143
  60.2 2.8 %collective-permute-done.15.own = bf16[64,3072]{1,0:T(8,128)(2,1)S(1)} collective-permute-done((bf16[64,3072]{1,0:T(8,128)(2,1)S(1)}, bf16[64,3072]{1,0:T(8,128)(2,1)S(1)}, u32[]{:S(2)}, u32[]{:S(2)}) %collective-permute-start.15) | collective-permute-done | bytes 393248 | tf_op jit(solution)/shard_map/ppermute | solution.py:146
  63.2 1.6 %collective-permute-done.16.other = bf16[64,3072]{1,0:T(8,128)(2,1)S(1)} collective-permute-done((bf16[64,3072]{1,0:T(8,128)(2,1)S(1)}, bf16[64,3072]{1,0:T(8,128)(2,1)S(1)}, u32[]{:S(2)}, u32[]{:S(2)}) %collective-permute-start.16) | collective-permute-done | bytes 393248 | tf_op jit(solution)/shard_map/ppermute | solution.py:143
  64.7 5.3 %experts.3 = (f32[64,3072]{1,0:T(8,128)S(1)}, bf16[64,3072]{1,0:T(8,128)(2,1)S(1)}) custom-call(bf16[64,3072]{1,0:T(8,128)(2,1)S(1)} %collective-permute-done.15.own, bf16[64,3072]{1,0:T(8,128)(2,1)S(1)} %collective-permute-done.16.other, bf16[3072,2048]{1,0:T(8,128)(2,1)S(1)} %stage.3.gate, bf16[3072,2048]{1,0:T(8,128)(2,1)S(1)} %stage.4.up, ...), custom_call_target="tpu_custom_call" | custom-call | flops 11324620800 | bytes 25165824 | tf_op jit(solution)/shard_map/experts/pallas_call | solution.py:89
  70.0 0.2 collective-permute-start.17
  70.2 0.4 fusion.36
  70.6 2.4 %collective-permute-start.14 = (bf16[16,3072]{1,0:T(8,128)(2,1)S(1)}, bf16[16,3072]{1,0:T(8,128)(2,1)S(1)}, u32[]{:S(2)}, u32[]{:S(2)}) collective-permute-start(bf16[16,3072]{1,0:T(8,128)(2,1)S(1)} %get-tuple-element.80), channel_id=1, source_target_pairs={{0,12},{2,14},{4,8},{6,10},{8,4},{10,6},{12,0},{14,2},{1,13},{3,15... | collective-permute-start | bytes 294920 | tf_op jit(solution)/shard_map/ppermute | solution.py:149
  73.0 2.0 %collective-permute-start.12 = (bf16[16,3072]{1,0:T(8,128)(2,1)S(1)}, bf16[16,3072]{1,0:T(8,128)(2,1)S(1)}, u32[]{:S(2)}, u32[]{:S(2)}) collective-permute-start(bf16[16,3072]{1,0:T(8,128)(2,1)S(1)} %get-tuple-element.79), channel_id=1, source_target_pairs={{0,4},{2,6},{4,0},{6,2},{8,12},{10,14},{12,8},{14,10},{1,5},{3,7},... | collective-permute-start | bytes 294920 | tf_op jit(solution)/shard_map/ppermute | solution.py:149
  75.3 1.6 %collective-permute-start.21 = (bf16[16,3072]{1,0:T(8,128)(2,1)S(1)}, bf16[16,3072]{1,0:T(8,128)(2,1)S(1)}, u32[]{:S(2)}, u32[]{:S(2)}) collective-permute-start(bf16[16,3072]{1,0:T(8,128)(2,1)S(1)} %get-tuple-element.83), channel_id=1, source_target_pairs={{0,2},{2,0},{4,6},{6,4},{8,10},{10,8},{12,14},{14,12},{1,3},{3,1},... | collective-permute-start | bytes 294920 | tf_op jit(solution)/shard_map/ppermute | solution.py:243
  76.9 1.4 %collective-permute-done.14 = bf16[16,3072]{1,0:T(8,128)(2,1)S(1)} collective-permute-done((bf16[16,3072]{1,0:T(8,128)(2,1)S(1)}, bf16[16,3072]{1,0:T(8,128)(2,1)S(1)}, u32[]{:S(2)}, u32[]{:S(2)}) %collective-permute-start.14) | collective-permute-done | bytes 98336 | tf_op jit(solution)/shard_map/ppermute | solution.py:149
  78.2 2.4 %collective-permute-start.19 = (bf16[16,3072]{1,0:T(8,128)(2,1)S(1)}, bf16[16,3072]{1,0:T(8,128)(2,1)S(1)}, u32[]{:S(2)}, u32[]{:S(2)}) collective-permute-start(bf16[16,3072]{1,0:T(8,128)(2,1)S(1)} %get-tuple-element.85), channel_id=1, source_target_pairs={{0,10},{2,8},{4,14},{6,12},{8,2},{10,0},{12,6},{14,4},{1,11},{3,9}... | collective-permute-start | bytes 294920 | tf_op jit(solution)/shard_map/ppermute | solution.py:243
  80.7 1.4 %collective-permute-done.13 = bf16[16,3072]{1,0:T(8,128)(2,1)S(1)} collective-permute-done((bf16[16,3072]{1,0:T(8,128)(2,1)S(1)}, bf16[16,3072]{1,0:T(8,128)(2,1)S(1)}, u32[]{:S(2)}, u32[]{:S(2)}) %collective-permute-start.13) | collective-permute-done | bytes 98336 | tf_op jit(solution)/shard_map/ppermute | solution.py:149
  82.0 3.2 %collective-permute-start.18 = (bf16[16,3072]{1,0:T(8,128)(2,1)S(1)}, bf16[16,3072]{1,0:T(8,128)(2,1)S(1)}, u32[]{:S(2)}, u32[]{:S(2)}) collective-permute-start(bf16[16,3072]{1,0:T(8,128)(2,1)S(1)} %get-tuple-element.82), channel_id=1, source_target_pairs={{0,14},{2,12},{4,10},{6,8},{8,6},{10,4},{12,2},{14,0},{1,15},{3,13... | collective-permute-start | bytes 294920 | tf_op jit(solution)/shard_map/ppermute | solution.py:243
  85.3 1.4 %collective-permute-done.20 = bf16[16,3072]{1,0:T(8,128)(2,1)S(1)} collective-permute-done((bf16[16,3072]{1,0:T(8,128)(2,1)S(1)}, bf16[16,3072]{1,0:T(8,128)(2,1)S(1)}, u32[]{:S(2)}, u32[]{:S(2)}) %collective-permute-start.20) | collective-permute-done | bytes 98336 | tf_op jit(solution)/shard_map/ppermute | solution.py:243
  86.6 3.4 %collective-permute-done.19 = bf16[16,3072]{1,0:T(8,128)(2,1)S(1)} collective-permute-done((bf16[16,3072]{1,0:T(8,128)(2,1)S(1)}, bf16[16,3072]{1,0:T(8,128)(2,1)S(1)}, u32[]{:S(2)}, u32[]{:S(2)}) %collective-permute-start.19) | collective-permute-done | bytes 98336 | tf_op jit(solution)/shard_map/ppermute | solution.py:243
  90.3 1.3 %collective-permute-done.22 = bf16[16,3072]{1,0:T(8,128)(2,1)S(1)} collective-permute-done((bf16[16,3072]{1,0:T(8,128)(2,1)S(1)}, bf16[16,3072]{1,0:T(8,128)(2,1)S(1)}, u32[]{:S(2)}, u32[]{:S(2)}) %collective-permute-start.22) | collective-permute-done | bytes 98336 | tf_op jit(solution)/shard_map/ppermute | solution.py:143
  91.6 0.7 pad_maximum_fusion.3
  (78 shorter events, 1.8 us)
Async XLA Ops:
  0.0 8.3 %copy-start = (bf16[32,2,128,128]{3,2,1,0:T(8,128)(2,1)S(1)}, bf16[32,2,128,128]{3,2,1,0:T(8,128)(2,1)}, u32[]{:S(2)}) copy-start(bf16[32,2,128,128]{3,2,1,0:T(8,128)(2,1)} %param.18) | copy-start | bytes 6291460
  0.0 8.3 %copy-start.4 = (bf16[32,12,128]{2,0,1:T(8,128)(2,1)S(1)}, bf16[32,12,128]{2,0,1:T(8,128)(2,1)}, u32[]{:S(2)}) copy-start(bf16[32,12,128]{2,0,1:T(8,128)(2,1)} %param.15) | copy-start | bytes 294916
  1.4 33.7 %collective-permute-start.5 = (bf16[512,384]{1,0:T(8,128)(2,1)S(1)}, bf16[512,384]{1,0:T(8,128)(2,1)}, u32[]{:S(2)}, u32[]{:S(2)}) collective-permute-start(bf16[512,384]{1,0:T(8,128)(2,1)S(1)} %get-tuple-element.76), channel_id=1, source_target_pairs={{0,2},{2,0},{4,6},{6,4},{8,10},{10,8},{12,14},{14,12},{1,3},{3,1},... | collective-permute-start | bytes 1179656 | tf_op jit(solution)/shard_map/ppermute | solution.py:146
  4.4 20.5 %collective-permute-start.3 = (bf16[512,384]{1,0:T(8,128)(2,1)S(1)}, bf16[512,384]{1,0:T(8,128)(2,1)S(1)}, u32[]{:S(2)}, u32[]{:S(2)}) collective-permute-start(bf16[512,384]{1,0:T(8,128)(2,1)S(1)} %get-tuple-element.75), channel_id=1, source_target_pairs={{0,2},{2,0},{4,6},{6,4},{8,10},{10,8},{12,14},{14,12},{1,3},{3,1},... | collective-permute-start | bytes 1179656 | tf_op jit(solution)/shard_map/ppermute | solution.py:146
  5.5 4.4 %copy-start.7 = (bf16[32,2,128,128]{3,2,1,0:T(8,128)(2,1)S(1)}, bf16[32,2,128,128]{3,2,1,0:T(8,128)(2,1)}, u32[]{:S(2)}) copy-start(bf16[32,2,128,128]{3,2,1,0:T(8,128)(2,1)} %param.19) | copy-start | bytes 6291460
  10.0 0.9 %copy-start.5 = (bf16[32,3072]{1,0:T(8,128)(2,1)S(1)}, bf16[32,3072]{1,0:T(8,128)(2,1)}, u32[]{:S(2)}) copy-start(bf16[32,3072]{1,0:T(8,128)(2,1)} %param.14) | copy-start | bytes 589828
  11.1 13.8 %collective-permute-start = (bf16[40,1536]{1,0:T(8,128)(2,1)S(1)}, bf16[40,1536]{1,0:T(8,128)(2,1)S(1)}, u32[]{:S(2)}, u32[]{:S(2)}) collective-permute-start(bf16[40,1536]{1,0:T(8,128)(2,1)S(1)} %get-tuple-element.117), channel_id=1, source_target_pairs={{0,4},{2,6},{4,0},{6,2},{8,12},{10,14},{12,8},{14,10},{1,5},{3,7},... | collective-permute-start | bytes 368648 | tf_op jit(solution)/shard_map/ppermute | solution.py:149
  13.2 11.8 %collective-permute-start.1 = (bf16[40,1536]{1,0:T(8,128)(2,1)S(1)}, bf16[40,1536]{1,0:T(8,128)(2,1)S(1)}, u32[]{:S(2)}, u32[]{:S(2)}) collective-permute-start(bf16[40,1536]{1,0:T(8,128)(2,1)S(1)} %get-tuple-element.118), channel_id=1, source_target_pairs={{0,8},{2,10},{4,12},{6,14},{8,0},{10,2},{12,4},{14,6},{1,9},{3,11}... | collective-permute-start | bytes 368648 | tf_op jit(solution)/shard_map/ppermute | solution.py:149
  15.7 9.2 %collective-permute-start.2 = (bf16[40,1536]{1,0:T(8,128)(2,1)S(1)}, bf16[40,1536]{1,0:T(8,128)(2,1)S(1)}, u32[]{:S(2)}, u32[]{:S(2)}) collective-permute-start(bf16[40,1536]{1,0:T(8,128)(2,1)S(1)} %get-tuple-element.116), channel_id=1, source_target_pairs={{0,12},{2,14},{4,8},{6,10},{8,4},{10,6},{12,0},{14,2},{1,13},{3,15... | collective-permute-start | bytes 368648 | tf_op jit(solution)/shard_map/ppermute | solution.py:149
  25.0 9.8 %collective-permute-start.4 = (bf16[512,384]{1,0:T(8,128)(2,1)S(1)}, bf16[512,384]{1,0:T(8,128)(2,1)S(1)}, u32[]{:S(2)}, u32[]{:S(2)}) collective-permute-start(bf16[512,384]{1,0:T(8,128)(2,1)S(1)} %collective-permute-done.3), channel_id=1, source_target_pairs={{0,16},{16,0},{1,17},{17,1},{2,18},{18,2},{3,19},{19,3},{4,20},{20... | collective-permute-start | bytes 1179656 | tf_op jit(solution)/shard_map/ppermute | solution.py:157
  35.1 1.5 %copy-start.2 = (bf16[1536,384]{1,0:T(8,128)(2,1)S(1)}, bf16[1536,384]{1,0:T(8,128)(2,1)}, u32[]{:S(2)}) copy-start(bf16[1536,384]{1,0:T(8,128)(2,1)} %param.21) | copy-start | bytes 3538948
  37.0 1.5 %collective-permute-start.6 = (f32[4,16,768]{2,1,0:T(8,128)S(1)}, f32[4,16,768]{2,1,0:T(8,128)S(1)}, u32[]{:S(2)}, u32[]{:S(2)}) collective-permute-start(f32[4,16,768]{2,1,0:T(8,128)S(1)} %dynamic-slice_bitcast_fusion.1), channel_id=1, source_target_pairs={{0,1},{1,0},{2,3},{3,2},{4,5},{5,4},{6,7},{7,6},{8,9},{9,8},{10,11... | collective-permute-start | bytes 589832 | tf_op jit(solution)/shard_map/ppermute | solution.py:143
  38.6 12.6 %copy-start.6 = (f32[3072]{0:T(1024)S(1)}, f32[3072]{0:T(1024)}, u32[]{:S(2)}) copy-start(f32[3072]{0:T(1024)} %param.22) | copy-start | bytes 36868
  38.6 9.0 %collective-permute-start.9 = (bf16[64,768]{1,0:T(8,128)(2,1)S(1)}, bf16[64,768]{1,0:T(8,128)(2,1)S(1)}, u32[]{:S(2)}, u32[]{:S(2)}) collective-permute-start(bf16[64,768]{1,0:T(8,128)(2,1)S(1)} %get-tuple-element.111), channel_id=1, source_target_pairs={{0,12},{2,14},{4,8},{6,10},{8,4},{10,6},{12,0},{14,2},{1,13},{3,15... | collective-permute-start | bytes 294920 | tf_op jit(solution)/shard_map/ppermute | solution.py:149
  42.2 8.7 %collective-permute-start.8 = (bf16[64,768]{1,0:T(8,128)(2,1)S(1)}, bf16[64,768]{1,0:T(8,128)(2,1)S(1)}, u32[]{:S(2)}, u32[]{:S(2)}) collective-permute-start(bf16[64,768]{1,0:T(8,128)(2,1)S(1)} %get-tuple-element.111), channel_id=1, source_target_pairs={{0,8},{2,10},{4,12},{6,14},{8,0},{10,2},{12,4},{14,6},{1,9},{3,11}... | collective-permute-start | bytes 294920 | tf_op jit(solution)/shard_map/ppermute | solution.py:149
  42.3 8.7 %collective-permute-start.7 = (bf16[64,768]{1,0:T(8,128)(2,1)S(1)}, bf16[64,768]{1,0:T(8,128)(2,1)S(1)}, u32[]{:S(2)}, u32[]{:S(2)}) collective-permute-start(bf16[64,768]{1,0:T(8,128)(2,1)S(1)} %get-tuple-element.111), channel_id=1, source_target_pairs={{0,4},{2,6},{4,0},{6,2},{8,12},{10,14},{12,8},{14,10},{1,5},{3,7},... | collective-permute-start | bytes 294920 | tf_op jit(solution)/shard_map/ppermute | solution.py:149
  51.4 7.1 %copy-start.3 = (f32[3072,4]{0,1:T(4,128)S(1)}, f32[3072,4]{0,1:T(4,128)}, u32[]{:S(2)}) copy-start(f32[3072,4]{0,1:T(4,128)} %param.23) | copy-start | bytes 147460
  51.4 1.8 %collective-permute-start.10 = (bf16[64,3072]{1,0:T(8,128)(2,1)S(1)}, bf16[64,3072]{1,0:T(8,128)(2,1)S(1)}, u32[]{:S(2)}, u32[]{:S(2)}) collective-permute-start(bf16[64,3072]{1,0:T(8,128)(2,1)S(1)} %multiply_convert_fusion.1.own), channel_id=1, source_target_pairs={{0,1},{1,0},{2,3},{3,2},{4,5},{5,4},{6,7},{7,6},{8,9},{9,8},{10,11... | collective-permute-start | bytes 1179656 | tf_op jit(solution)/shard_map/ppermute | solution.py:143
  51.5 11.5 %collective-permute-start.15 = (bf16[64,3072]{1,0:T(8,128)(2,1)S(1)}, bf16[64,3072]{1,0:T(8,128)(2,1)S(1)}, u32[]{:S(2)}, u32[]{:S(2)}) collective-permute-start(bf16[64,3072]{1,0:T(8,128)(2,1)S(1)} %multiply_convert_fusion.1.own), channel_id=1, source_target_pairs={{0,2},{2,0},{4,6},{6,4},{8,10},{10,8},{12,14},{14,12},{1,3},{3,1},... | collective-permute-start | bytes 1179656 | tf_op jit(solution)/shard_map/ppermute | solution.py:146
  58.3 1.8 %collective-permute-start.11 = (bf16[64,3072]{1,0:T(8,128)(2,1)S(1)}, bf16[64,3072]{1,0:T(8,128)(2,1)S(1)}, u32[]{:S(2)}, u32[]{:S(2)}) collective-permute-start(bf16[64,3072]{1,0:T(8,128)(2,1)S(1)} %get-tuple-element.67), channel_id=1, source_target_pairs={{0,1},{1,0},{2,3},{3,2},{4,5},{5,4},{6,7},{7,6},{8,9},{9,8},{10,11... | collective-permute-start | bytes 1179656 | tf_op jit(solution)/shard_map/ppermute | solution.py:143
  63.0 1.7 %collective-permute-start.16 = (bf16[64,3072]{1,0:T(8,128)(2,1)S(1)}, bf16[64,3072]{1,0:T(8,128)(2,1)S(1)}, u32[]{:S(2)}, u32[]{:S(2)}) collective-permute-start(bf16[64,3072]{1,0:T(8,128)(2,1)S(1)} %collective-permute-done.15.own), channel_id=1, source_target_pairs={{0,1},{1,0},{2,3},{3,2},{4,5},{5,4},{6,7},{7,6},{8,9},{9,8},{10,11... | collective-permute-start | bytes 1179656 | tf_op jit(solution)/shard_map/ppermute | solution.py:143
  70.0 5.1 %collective-permute-start.17 = (bf16[64,3072]{1,0:T(8,128)(2,1)S(1)}, bf16[64,3072]{1,0:T(8,128)(2,1)S(1)}, u32[]{:S(2)}, u32[]{:S(2)}) collective-permute-start(bf16[64,3072]{1,0:T(8,128)(2,1)S(1)} %get-tuple-element.72), channel_id=1, source_target_pairs={{0,1},{1,0},{2,3},{3,2},{4,5},{5,4},{6,7},{7,6},{8,9},{9,8},{10,11... | collective-permute-start | bytes 1179656 | tf_op jit(solution)/shard_map/ppermute | solution.py:143
  70.6 7.6 %collective-permute-start.14 = (bf16[16,3072]{1,0:T(8,128)(2,1)S(1)}, bf16[16,3072]{1,0:T(8,128)(2,1)S(1)}, u32[]{:S(2)}, u32[]{:S(2)}) collective-permute-start(bf16[16,3072]{1,0:T(8,128)(2,1)S(1)} %get-tuple-element.80), channel_id=1, source_target_pairs={{0,12},{2,14},{4,8},{6,10},{8,4},{10,6},{12,0},{14,2},{1,13},{3,15... | collective-permute-start | bytes 294920 | tf_op jit(solution)/shard_map/ppermute | solution.py:149
  73.0 9.0 %collective-permute-start.13 = (bf16[16,3072]{1,0:T(8,128)(2,1)S(1)}, bf16[16,3072]{1,0:T(8,128)(2,1)S(1)}, u32[]{:S(2)}, u32[]{:S(2)}) collective-permute-start(bf16[16,3072]{1,0:T(8,128)(2,1)S(1)} %get-tuple-element.81), channel_id=1, source_target_pairs={{0,8},{2,10},{4,12},{6,14},{8,0},{10,2},{12,4},{14,6},{1,9},{3,11}... | collective-permute-start | bytes 294920 | tf_op jit(solution)/shard_map/ppermute | solution.py:149
  73.0 12.3 %collective-permute-start.12 = (bf16[16,3072]{1,0:T(8,128)(2,1)S(1)}, bf16[16,3072]{1,0:T(8,128)(2,1)S(1)}, u32[]{:S(2)}, u32[]{:S(2)}) collective-permute-start(bf16[16,3072]{1,0:T(8,128)(2,1)S(1)} %get-tuple-element.79), channel_id=1, source_target_pairs={{0,4},{2,6},{4,0},{6,2},{8,12},{10,14},{12,8},{14,10},{1,5},{3,7},... | collective-permute-start | bytes 294920 | tf_op jit(solution)/shard_map/ppermute | solution.py:149
  75.1 17.2 %copy-start.1 = (bf16[32,2,128,128]{3,2,1,0:T(8,128)(2,1)S(1)}, bf16[32,2,128,128]{3,2,1,0:T(8,128)(2,1)}, u32[]{:S(2)}) copy-start(bf16[32,2,128,128]{3,2,1,0:T(8,128)(2,1)} %param.18) | copy-start | bytes 6291460
  75.3 10.0 %collective-permute-start.21 = (bf16[16,3072]{1,0:T(8,128)(2,1)S(1)}, bf16[16,3072]{1,0:T(8,128)(2,1)S(1)}, u32[]{:S(2)}, u32[]{:S(2)}) collective-permute-start(bf16[16,3072]{1,0:T(8,128)(2,1)S(1)} %get-tuple-element.83), channel_id=1, source_target_pairs={{0,2},{2,0},{4,6},{6,4},{8,10},{10,8},{12,14},{14,12},{1,3},{3,1},... | collective-permute-start | bytes 294920 | tf_op jit(solution)/shard_map/ppermute | solution.py:243
  76.9 9.8 %collective-permute-start.20 = (bf16[16,3072]{1,0:T(8,128)(2,1)S(1)}, bf16[16,3072]{1,0:T(8,128)(2,1)S(1)}, u32[]{:S(2)}, u32[]{:S(2)}) collective-permute-start(bf16[16,3072]{1,0:T(8,128)(2,1)S(1)} %get-tuple-element.84), channel_id=1, source_target_pairs={{0,6},{2,4},{4,2},{6,0},{8,14},{10,12},{12,10},{14,8},{1,7},{3,5},... | collective-permute-start | bytes 294920 | tf_op jit(solution)/shard_map/ppermute | solution.py:243
  78.2 11.8 %collective-permute-start.19 = (bf16[16,3072]{1,0:T(8,128)(2,1)S(1)}, bf16[16,3072]{1,0:T(8,128)(2,1)S(1)}, u32[]{:S(2)}, u32[]{:S(2)}) collective-permute-start(bf16[16,3072]{1,0:T(8,128)(2,1)S(1)} %get-tuple-element.85), channel_id=1, source_target_pairs={{0,10},{2,8},{4,14},{6,12},{8,2},{10,0},{12,6},{14,4},{1,11},{3,9}... | collective-permute-start | bytes 294920 | tf_op jit(solution)/shard_map/ppermute | solution.py:243
  82.0 8.0 %collective-permute-start.18 = (bf16[16,3072]{1,0:T(8,128)(2,1)S(1)}, bf16[16,3072]{1,0:T(8,128)(2,1)S(1)}, u32[]{:S(2)}, u32[]{:S(2)}) collective-permute-start(bf16[16,3072]{1,0:T(8,128)(2,1)S(1)} %get-tuple-element.82), channel_id=1, source_target_pairs={{0,14},{2,12},{4,10},{6,8},{8,6},{10,4},{12,2},{14,0},{1,15},{3,13... | collective-permute-start | bytes 294920 | tf_op jit(solution)/shard_map/ppermute | solution.py:243
  90.2 1.4 %collective-permute-start.22 = (bf16[16,3072]{1,0:T(8,128)(2,1)S(1)}, bf16[16,3072]{1,0:T(8,128)(2,1)S(1)}, u32[]{:S(2)}, u32[]{:S(2)}) collective-permute-start(bf16[16,3072]{1,0:T(8,128)(2,1)S(1)} %add_convert_fusion), channel_id=1, source_target_pairs={{0,1},{1,0},{2,3},{3,2},{4,5},{5,4},{6,7},{7,6},{8,9},{9,8},{10,11... | collective-permute-start | bytes 294920 | tf_op jit(solution)/shard_map/ppermute | solution.py:143

commit v4 on v3

--- a/solution.py
+++ b/solution.py
@@ -50,14 +50,16 @@
     return lax.dynamic_slice_in_dim(array, start, size, axis, allow_negative_indices=False)
 
 
-def experts_kernel(own, other, gate, up, down, kept, sent, block, active):
+def experts_kernel(own, other, gate, up_low, up_high, down, kept, sent, block, active):
     rows = own.shape[0]
-    step = min(512, gate.shape[1])
+    middle = up_low.shape[1]
+    step = min(512, middle)
     block[:rows] = own[...]
     block[rows:] = other[...]
     for c in range(0, gate.shape[1], step):
         gated = jnp.dot(block[...], gate[:, c : c + step], preferred_element_type=jnp.float32)
-        upward = jnp.dot(block[...], up[:, c : c + step], preferred_element_type=jnp.float32)
+        up, at = (up_low, c) if c < middle else (up_high, c - middle)
+        upward = jnp.dot(block[...], up[:, at : at + step], preferred_element_type=jnp.float32)
         active[:, c : c + step] = (jax.nn.silu(gated) * upward).astype(jnp.bfloat16)
     for c in range(0, down.shape[1], 512):
         out = jnp.dot(active[...], down[:, c : c + 512], preferred_element_type=jnp.float32)
@@ -65,17 +67,21 @@
         sent[:, c : c + 512] = out[rows:].astype(jnp.bfloat16)
 
 
-def stage(weight):
+def stage(weight, begin=0, count=None):
+    shape = (weight.shape[0], count or weight.shape[1])
+
     def body(source, target):
-        pltpu.sync_copy(source, target)
+        pltpu.sync_copy(source.at[:, pl.ds(begin, shape[1])], target)
 
     return pl.pallas_call(
         body,
         in_specs=[pl.BlockSpec(memory_space=pltpu.HBM)],
         out_specs=pl.BlockSpec(memory_space=pltpu.VMEM),
-        out_shape=pltpu.VMEM(weight.shape, weight.dtype),
+        out_shape=pltpu.VMEM(shape, weight.dtype),
         cost_estimate=pl.CostEstimate(
-            flops=weight.size * 600, transcendentals=0, bytes_accessed=2 * weight.size
+            flops=math.prod(shape) * 600,
+            transcendentals=0,
+            bytes_accessed=2 * math.prod(shape),
         ),
         compiler_params=pltpu.CompilerParams(vmem_limit_bytes=1 << 20),
         name="stage",
@@ -88,7 +94,7 @@
     fast = pl.BlockSpec(memory_space=pltpu.VMEM)
     return pl.pallas_call(
         experts_kernel,
-        in_specs=[fast] * 5,
+        in_specs=[fast] * 6,
         out_specs=[fast] * 2,
         out_shape=[
             jax.ShapeDtypeStruct((rows, width), jnp.float32),
@@ -187,16 +193,23 @@
     queries, ahead, away = lax.optimization_barrier((queries, ahead, 1 - side))
     own_masks, far_masks, order, starts, shares_order, even, first_side, corner, side = ahead
     attn_out = attend(queries, key_new, value_new, cache_keys, cache_values, lengths)
-    up_staged = stage(up_weight)
-    staged = [stage(gate_weight), up_staged, stage(down_weight)]
-    arrived = []
+    up_half = up_weight.shape[1] // 2
+    up_low = stage(up_weight, 0, up_half)
+    up_high = stage(up_weight, up_half, up_half)
+    down_staged = stage(down_weight)
+    staged = [stage(gate_weight), up_low, up_high, down_staged]
+    messages = []
     for k in range(lines):
         part = cut(hidden_half, starts[k], 2 * cols, 1)
         folds = span // (2 * cols)
         deep = half // folds
         extra = jnp.concatenate([part[i * deep : (i + 1) * deep] for i in range(folds)], axis=1)
         message = jnp.concatenate([attn_out, extra], axis=0)
-        arrived.append(line(message, k) if k else message)
+        messages.append(message)
+    sent_lines = {}
+    for k in reversed(range(1, lines)):
+        sent_lines[k] = line(messages[k], k)
+    arrived = [messages[0]] + [sent_lines[k] for k in range(1, lines)]
     arrived, staged[:2] = lax.optimization_barrier((arrived, staged[:2]))
     blocks = jnp.concatenate([m[:rows] for m in arrived], axis=0)
     hidden_blocks = jnp.stack(
@@ -207,8 +220,9 @@
             for m in arrived
         ]
     )
+    own_columns = jnp.dot(blocks, out_weight, preferred_element_type=jnp.float32)
+    blocks, own_columns = lax.optimization_barrier((blocks, own_columns))
     far_weight = jnp.concatenate([pick(gathered, b) for b in shares_order] + rest, axis=0)
-    own_columns = jnp.dot(blocks, out_weight, preferred_element_type=jnp.float32)
     far_columns = jnp.dot(blocks, far_weight, preferred_element_type=jnp.float32)
     columns = jnp.concatenate(
         [
@@ -221,7 +235,8 @@
     own = cut(columns, side, 1, 1).reshape(lines, half, 2 * cols)
     relative = (hidden_blocks.astype(jnp.float32) + (own + across(other))).astype(jnp.bfloat16)
     residual = jnp.concatenate([pick(relative, b) for b in order], axis=0)
-    parts = jnp.stack([residual] + [line(residual, k) for k in range(1, lines)])
+    gathers = [line(residual, k) for k in range(1, lines)]
+    parts = jnp.stack([residual] + gathers)
     parts, staged = lax.optimization_barrier((parts, staged))
     stream = jnp.concatenate([pick(parts, b) for b in order], axis=1)
     wide = stream.astype(jnp.float32)

time: 92.6 us -> 97.7 us (1.055)
  waiting for transfers between devices: 27.1 us -> 32.5 us
  local copies, waits for them, and re-layouts: 2.89 us -> 1.76 us
  Pallas kernels: 24.1 us -> 25.1 us
    ppermute x3, waiting for transfers between devices: 2.8 us -> 7.03 us  [near(): return lax.ppermute(value, 'tok', first_swap)]
    dynamic_slice x2, local copies, waits for them, and re-layouts: 1.37 us -> 0.1 us  [cut(): lax.dynamic_slice_in_dim(array, start, size, axis, allow_negative_indices...]
    ppermute x3, starting transfers between devices: 4.72 us -> 3.6 us  [near(): return lax.ppermute(value, 'tok', first_swap)]
    dot_general x1, matrix products: 1.46 us -> 0.37 us  [local(): jnp.dot(blocks, far_weight, preferred_element_type=jnp.float32)]
    ppermute x9, starting transfers between devices: 13.5 us -> 14.6 us  [line(): return lax.ppermute(value, 'tok', [(t, t ^ 2 * k) for t in range(toks)])]
    pallas_call x3 -> x4, Pallas kernels: 13.7 us -> 14.7 us  [stage(): pl.pallas_call(body, in_specs=[pl.BlockSpec(memory_space=pltpu.HBM)], out...]
  transfers between devices with their start and end apart: 23 -> 23, of which waited for: 12 -> 15; matrix products, arithmetic and copies ran while one was open for 9% -> 2% of each run, Pallas kernels for 20% -> 20%
where the time goes in v4:
time: 97.7 us; the launch traced here: 97.3 us
  waiting for transfers between devices  32.5 us (33%)
  starting transfers between devices  27.8 us (28%)
  Pallas kernels  25.1 us (26%)
  matrix products  5.55 us (6%)
  other arithmetic  4.11 us (4%)
  local copies, waits for them, and re-layouts  1.76 us (2%)
    pallas_call x4, Pallas kernels, stage(): pl.pallas_call(body, in_specs=[pl.BlockSpec(memory_space=pltpu.HBM)], out...  14.7 us
    ppermute x9, starting transfers between devices, line(): return lax.ppermute(value, 'tok', [(t, t ^ 2 * k) for t in range(toks)])  14.6 us
    pallas_call x2, Pallas kernels, run_experts(): pl.pallas_call(experts_kernel, in_specs=[fast] * 6, out_specs=[fast] * 2,...  10.4 us
    ppermute x1, waiting for transfers between devices, over(): return lax.ppermute(value, 'grp', [(g, g ^ k) for g in range(groups)])  7.94 us
    ppermute x4, starting transfers between devices, slant(): return lax.ppermute(value, 'tok', [(t, t ^ 2 * k ^ 1) for t in range(toks)])  7.48 us
    ppermute x3, waiting for transfers between devices, near(): return lax.ppermute(value, 'tok', first_swap)  7.03 us
    ppermute x9, waiting for transfers between devices, line(): return lax.ppermute(value, 'tok', [(t, t ^ 2 * k) for t in range(toks)])  6.35 us
    ppermute x4, waiting for transfers between devices, slant(): return lax.ppermute(value, 'tok', [(t, t ^ 2 * k ^ 1) for t in range(toks)])  5.63 us
  transfers between devices with their start and end apart: 23, of which 15 were waited for; matrix products, arithmetic and copies ran while one was open for 2% of the time, Pallas kernels for 20%

profile of v4, /device:TPU:0, one launch (start us, length us, event | category | flops | bytes accessed | tf_op | source)
XLA Modules:
  0.0 97.3 jit_solution(2124460221041564584)
XLA Ops:
  0.0 0.9 reshape.114
  1.2 0.9 iota_compare_fusion
  2.1 0.7 convert_element_type.87
  2.8 1.1 %fusion.15 = f32[32,2,1,6]{3,2,1,0:T(1,128)S(1)} fusion(bf16[32,2,6,128]{3,0,2,1:T(8,128)(2,1)} %bitcast.95, bf16[32,2,128,1]{2,1,0,3:T(2,128)(2,1)} %bitcast.104), kind=kOutput, calls=%fused_computation.36 | convolution fusion | flops 98304 | bytes 116224 | tf_op jit(solution)/shard_map/skgd,skd->skg/dot_general | solution.py:24
  3.9 2.2 %fusion.33 = (f32[32,2,6]{2,1,0:T(2,128)S(1)}, f32[32,2,6,128]{3,2,1,0:T(8,128)S(1)}) fusion(bf16[32,2,128,128]{3,2,1,0:T(8,128)(2,1)S(1)} %copy-done, bf16[32,2,6,128]{3,0,2,1:T(8,128)(2,1)} %bitcast.96, pred[32,128]{1,0:T(8,128)(4,1)S(1)} %iota_compare_fusion), kind=kOutput, calls=%fused_computation.99 | convolution fusion | flops 12729984 | bytes 2397696 | tf_op jit(solution)/shard_map/skgd,skpd->skgp/dot_general | solution.py:18
  6.2 0.3 fusion.12
  6.5 0.7 fusion.7
  7.6 3.1 %collective-permute-start = (bf16[40,1536]{1,0:T(8,128)(2,1)S(1)}, bf16[40,1536]{1,0:T(8,128)(2,1)S(1)}, u32[]{:S(2)}, u32[]{:S(2)}) collective-permute-start(bf16[40,1536]{1,0:T(8,128)(2,1)S(1)} %get-tuple-element.123), channel_id=1, source_target_pairs={{0,4},{2,6},{4,0},{6,2},{8,12},{10,14},{12,8},{14,10},{1,5},{3,7},... | collective-permute-start | bytes 368648 | tf_op jit(solution)/shard_map/ppermute | solution.py:155
  10.7 2.6 %collective-permute-start.1 = (bf16[40,1536]{1,0:T(8,128)(2,1)S(1)}, bf16[40,1536]{1,0:T(8,128)(2,1)S(1)}, u32[]{:S(2)}, u32[]{:S(2)}) collective-permute-start(bf16[40,1536]{1,0:T(8,128)(2,1)S(1)} %get-tuple-element.124), channel_id=1, source_target_pairs={{0,8},{2,10},{4,12},{6,14},{8,0},{10,2},{12,4},{14,6},{1,9},{3,11}... | collective-permute-start | bytes 368648 | tf_op jit(solution)/shard_map/ppermute | solution.py:155
  13.4 1.8 %collective-permute-start.5 = (bf16[512,384]{1,0:T(8,128)(2,1)S(1)}, bf16[512,384]{1,0:T(8,128)(2,1)S(1)}, u32[]{:S(2)}, u32[]{:S(2)}) collective-permute-start(bf16[512,384]{1,0:T(8,128)(2,1)S(1)} %get-tuple-element.82), channel_id=1, source_target_pairs={{0,2},{2,0},{4,6},{6,4},{8,10},{10,8},{12,14},{14,12},{1,3},{3,1},... | collective-permute-start | bytes 1179656 | tf_op jit(solution)/shard_map/ppermute | solution.py:152
  15.2 0.3 collective-permute-start.3
  15.5 4.6 %stage.4.gate = bf16[3072,2048]{1,0:T(8,128)(2,1)S(1)} custom-call(bf16[3072,2048]{1,0:T(8,128)(2,1)} %source.4), custom_call_target="tpu_custom_call" | custom-call | flops 3774873600 | bytes 12582912 | tf_op jit(solution)/shard_map/stage/pallas_call | solution.py:76
  20.1 4.6 %stage.7.down = bf16[2048,3072]{1,0:T(8,128)(2,1)S(1)} custom-call(bf16[2048,3072]{1,0:T(8,128)(2,1)} %source.7), custom_call_target="tpu_custom_call" | custom-call | flops 3774873600 | bytes 12582912 | tf_op jit(solution)/shard_map/stage/pallas_call | solution.py:76
  24.7 2.8 %stage.5.up_low = bf16[3072,1024]{1,0:T(8,128)(2,1)S(1)} custom-call(bf16[3072,2048]{1,0:T(8,128)(2,1)} %source.6), custom_call_target="tpu_custom_call" | custom-call | flops 1887436800 | bytes 6291456 | tf_op jit(solution)/shard_map/stage/pallas_call | solution.py:76
  27.6 0.4 fusion.27
  28.0 4.2 %collective-permute-done.3 = bf16[512,384]{1,0:T(8,128)(2,1)S(1)} collective-permute-done((bf16[512,384]{1,0:T(8,128)(2,1)S(1)}, bf16[512,384]{1,0:T(8,128)(2,1)S(1)}, u32[]{:S(2)}, u32[]{:S(2)}) %collective-permute-start.3) | collective-permute-done | bytes 393248 | tf_op jit(solution)/shard_map/ppermute | solution.py:152
  32.2 1.5 %collective-permute-start.4 = (bf16[512,384]{1,0:T(8,128)(2,1)S(1)}, bf16[512,384]{1,0:T(8,128)(2,1)S(1)}, u32[]{:S(2)}, u32[]{:S(2)}) collective-permute-start(bf16[512,384]{1,0:T(8,128)(2,1)S(1)} %collective-permute-done.3), channel_id=1, source_target_pairs={{0,16},{16,0},{1,17},{17,1},{2,18},{18,2},{3,19},{19,3},{4,20},{20... | collective-permute-start | bytes 1179656 | tf_op jit(solution)/shard_map/ppermute | solution.py:163
  33.7 7.9 %collective-permute-done.4 = bf16[512,384]{1,0:T(8,128)(2,1)S(1)} collective-permute-done((bf16[512,384]{1,0:T(8,128)(2,1)S(1)}, bf16[512,384]{1,0:T(8,128)(2,1)S(1)}, u32[]{:S(2)}, u32[]{:S(2)}) %collective-permute-start.4) | collective-permute-done | bytes 393248 | tf_op jit(solution)/shard_map/ppermute | solution.py:163
  41.6 0.3 fusion.11
  42.0 0.4 broadcast_select_fusion.1
  42.5 1.4 %collective-permute-done.6 = f32[4,16,768]{2,1,0:T(8,128)S(1)} collective-permute-done((f32[4,16,768]{2,1,0:T(8,128)S(1)}, f32[4,16,768]{2,1,0:T(8,128)S(1)}, u32[]{:S(2)}, u32[]{:S(2)}) %collective-permute-start.6) | collective-permute-done | bytes 196640 | tf_op jit(solution)/shard_map/ppermute | solution.py:149
  44.0 3.3 %collective-permute-start.9 = (bf16[64,768]{1,0:T(8,128)(2,1)S(1)}, bf16[64,768]{1,0:T(8,128)(2,1)S(1)}, u32[]{:S(2)}, u32[]{:S(2)}) collective-permute-start(bf16[64,768]{1,0:T(8,128)(2,1)S(1)} %get-tuple-element.117), channel_id=1, source_target_pairs={{0,12},{2,14},{4,8},{6,10},{8,4},{10,6},{12,0},{14,2},{1,13},{3,15... | collective-permute-start | bytes 294920 | tf_op jit(solution)/shard_map/ppermute | solution.py:155
  47.4 1.1 %collective-permute-start.7 = (bf16[64,768]{1,0:T(8,128)(2,1)S(1)}, bf16[64,768]{1,0:T(8,128)(2,1)S(1)}, u32[]{:S(2)}, u32[]{:S(2)}) collective-permute-start(bf16[64,768]{1,0:T(8,128)(2,1)S(1)} %get-tuple-element.117), channel_id=1, source_target_pairs={{0,4},{2,6},{4,0},{6,2},{8,12},{10,14},{12,8},{14,10},{1,5},{3,7},... | collective-permute-start | bytes 294920 | tf_op jit(solution)/shard_map/ppermute | solution.py:155
  48.5 2.8 %stage.6.up_high = bf16[3072,1024]{1,0:T(8,128)(2,1)S(1)} custom-call(bf16[3072,2048]{1,0:T(8,128)(2,1)} %source.6), custom_call_target="tpu_custom_call" | custom-call | flops 1887436800 | bytes 6291456 | tf_op jit(solution)/shard_map/stage/pallas_call | solution.py:76
  51.3 0.4 collective-permute-done.9
  51.7 3.4 %collective-permute-done.8 = bf16[64,768]{1,0:T(8,128)(2,1)S(1)} collective-permute-done((bf16[64,768]{1,0:T(8,128)(2,1)S(1)}, bf16[64,768]{1,0:T(8,128)(2,1)S(1)}, u32[]{:S(2)}, u32[]{:S(2)}) %collective-permute-start.8) | collective-permute-done | bytes 98336 | tf_op jit(solution)/shard_map/ppermute | solution.py:155
  55.7 1.5 %collective-permute-start.15 = (bf16[64,3072]{1,0:T(8,128)(2,1)S(1)}, bf16[64,3072]{1,0:T(8,128)(2,1)S(1)}, u32[]{:S(2)}, u32[]{:S(2)}) collective-permute-start(bf16[64,3072]{1,0:T(8,128)(2,1)S(1)} %multiply_convert_fusion.1.own), channel_id=1, source_target_pairs={{0,2},{2,0},{4,6},{6,4},{8,10},{10,8},{12,14},{14,12},{1,3},{3,1},... | collective-permute-start | bytes 1179656 | tf_op jit(solution)/shard_map/ppermute | solution.py:152
  57.3 5.1 %experts.2 = (f32[64,3072]{1,0:T(8,128)S(1)}, bf16[64,3072]{1,0:T(8,128)(2,1)S(1)}) custom-call(bf16[64,3072]{1,0:T(8,128)(2,1)S(1)} %multiply_convert_fusion.1.own, bf16[64,3072]{1,0:T(8,128)(2,1)S(1)} %collective-permute-done.10.other, bf16[3072,2048]{1,0:T(8,128)(2,1)S(1)} %stage.4.gate, bf16[3072,1024]{1,0:T(8,128)(2,1)S(1)} %stage.5.up_low, ...), custom_call_target="tpu_custom_call" | custom-call | flops 11324620800 | bytes 25165824 | tf_op jit(solution)/shard_map/experts/pallas_call | solution.py:95
  62.6 0.4 fusion.34
  63.1 1.1 %collective-permute-done.11 = bf16[64,3072]{1,0:T(8,128)(2,1)S(1)} collective-permute-done((bf16[64,3072]{1,0:T(8,128)(2,1)S(1)}, bf16[64,3072]{1,0:T(8,128)(2,1)S(1)}, u32[]{:S(2)}, u32[]{:S(2)}) %collective-permute-start.11) | collective-permute-done | bytes 393248 | tf_op jit(solution)/shard_map/ppermute | solution.py:149
  64.3 2.8 %collective-permute-done.15.own = bf16[64,3072]{1,0:T(8,128)(2,1)S(1)} collective-permute-done((bf16[64,3072]{1,0:T(8,128)(2,1)S(1)}, bf16[64,3072]{1,0:T(8,128)(2,1)S(1)}, u32[]{:S(2)}, u32[]{:S(2)}) %collective-permute-start.15) | collective-permute-done | bytes 393248 | tf_op jit(solution)/shard_map/ppermute | solution.py:152
  67.3 1.6 %collective-permute-done.16.other = bf16[64,3072]{1,0:T(8,128)(2,1)S(1)} collective-permute-done((bf16[64,3072]{1,0:T(8,128)(2,1)S(1)}, bf16[64,3072]{1,0:T(8,128)(2,1)S(1)}, u32[]{:S(2)}, u32[]{:S(2)}) %collective-permute-start.16) | collective-permute-done | bytes 393248 | tf_op jit(solution)/shard_map/ppermute | solution.py:149
  68.8 5.3 %experts.3 = (f32[64,3072]{1,0:T(8,128)S(1)}, bf16[64,3072]{1,0:T(8,128)(2,1)S(1)}) custom-call(bf16[64,3072]{1,0:T(8,128)(2,1)S(1)} %collective-permute-done.15.own, bf16[64,3072]{1,0:T(8,128)(2,1)S(1)} %collective-permute-done.16.other, bf16[3072,2048]{1,0:T(8,128)(2,1)S(1)} %stage.4.gate, bf16[3072,1024]{1,0:T(8,128)(2,1)S(1)} %stage.5.up_low, ...), custom_call_target="tpu_custom_call" | custom-call | flops 11324620800 | bytes 25165824 | tf_op jit(solution)/shard_map/experts/pallas_call | solution.py:95
  74.3 0.4 fusion.35
  74.7 2.6 %collective-permute-start.14 = (bf16[16,3072]{1,0:T(8,128)(2,1)S(1)}, bf16[16,3072]{1,0:T(8,128)(2,1)S(1)}, u32[]{:S(2)}, u32[]{:S(2)}) collective-permute-start(bf16[16,3072]{1,0:T(8,128)(2,1)S(1)} %get-tuple-element.86), channel_id=1, source_target_pairs={{0,12},{2,14},{4,8},{6,10},{8,4},{10,6},{12,0},{14,2},{1,13},{3,15... | collective-permute-start | bytes 294920 | tf_op jit(solution)/shard_map/ppermute | solution.py:155
  77.3 0.3 collective-permute-start.13
  77.6 1.5 %collective-permute-start.12 = (bf16[16,3072]{1,0:T(8,128)(2,1)S(1)}, bf16[16,3072]{1,0:T(8,128)(2,1)S(1)}, u32[]{:S(2)}, u32[]{:S(2)}) collective-permute-start(bf16[16,3072]{1,0:T(8,128)(2,1)S(1)} %get-tuple-element.85), channel_id=1, source_target_pairs={{0,4},{2,6},{4,0},{6,2},{8,12},{10,14},{12,8},{14,10},{1,5},{3,7},... | collective-permute-start | bytes 294920 | tf_op jit(solution)/shard_map/ppermute | solution.py:155
  79.4 1.6 %collective-permute-start.21 = (bf16[16,3072]{1,0:T(8,128)(2,1)S(1)}, bf16[16,3072]{1,0:T(8,128)(2,1)S(1)}, u32[]{:S(2)}, u32[]{:S(2)}) collective-permute-start(bf16[16,3072]{1,0:T(8,128)(2,1)S(1)} %get-tuple-element.89), channel_id=1, source_target_pairs={{0,2},{2,0},{4,6},{6,4},{8,10},{10,8},{12,14},{14,12},{1,3},{3,1},... | collective-permute-start | bytes 294920 | tf_op jit(solution)/shard_map/ppermute | solution.py:258
  81.0 0.5 collective-permute-start.20
  81.4 0.9 collective-permute-done.14
  82.3 3.7 %collective-permute-start.19 = (bf16[16,3072]{1,0:T(8,128)(2,1)S(1)}, bf16[16,3072]{1,0:T(8,128)(2,1)S(1)}, u32[]{:S(2)}, u32[]{:S(2)}) collective-permute-start(bf16[16,3072]{1,0:T(8,128)(2,1)S(1)} %get-tuple-element.91), channel_id=1, source_target_pairs={{0,10},{2,8},{4,14},{6,12},{8,2},{10,0},{12,6},{14,4},{1,11},{3,9}... | collective-permute-start | bytes 294920 | tf_op jit(solution)/shard_map/ppermute | solution.py:258
  86.0 1.7 %collective-permute-done.13 = bf16[16,3072]{1,0:T(8,128)(2,1)S(1)} collective-permute-done((bf16[16,3072]{1,0:T(8,128)(2,1)S(1)}, bf16[16,3072]{1,0:T(8,128)(2,1)S(1)}, u32[]{:S(2)}, u32[]{:S(2)}) %collective-permute-start.13) | collective-permute-done | bytes 98336 | tf_op jit(solution)/shard_map/ppermute | solution.py:155
  87.7 1.7 %collective-permute-start.18 = (bf16[16,3072]{1,0:T(8,128)(2,1)S(1)}, bf16[16,3072]{1,0:T(8,128)(2,1)S(1)}, u32[]{:S(2)}, u32[]{:S(2)}) collective-permute-start(bf16[16,3072]{1,0:T(8,128)(2,1)S(1)} %get-tuple-element.88), channel_id=1, source_target_pairs={{0,14},{2,12},{4,10},{6,8},{8,6},{10,4},{12,2},{14,0},{1,15},{3,13... | collective-permute-start | bytes 294920 | tf_op jit(solution)/shard_map/ppermute | solution.py:258
  89.5 0.5 collective-permute-done.20
  90.0 3.9 %collective-permute-done.19 = bf16[16,3072]{1,0:T(8,128)(2,1)S(1)} collective-permute-done((bf16[16,3072]{1,0:T(8,128)(2,1)S(1)}, bf16[16,3072]{1,0:T(8,128)(2,1)S(1)}, u32[]{:S(2)}, u32[]{:S(2)}) %collective-permute-start.19) | collective-permute-done | bytes 98336 | tf_op jit(solution)/shard_map/ppermute | solution.py:258
  93.9 1.2 %collective-permute-done.18 = bf16[16,3072]{1,0:T(8,128)(2,1)S(1)} collective-permute-done((bf16[16,3072]{1,0:T(8,128)(2,1)S(1)}, bf16[16,3072]{1,0:T(8,128)(2,1)S(1)}, u32[]{:S(2)}, u32[]{:S(2)}) %collective-permute-start.18) | collective-permute-done | bytes 98336 | tf_op jit(solution)/shard_map/ppermute | solution.py:258
  95.3 1.3 %collective-permute-done.22 = bf16[16,3072]{1,0:T(8,128)(2,1)S(1)} collective-permute-done((bf16[16,3072]{1,0:T(8,128)(2,1)S(1)}, bf16[16,3072]{1,0:T(8,128)(2,1)S(1)}, u32[]{:S(2)}, u32[]{:S(2)}) %collective-permute-start.22) | collective-permute-done | bytes 98336 | tf_op jit(solution)/shard_map/ppermute | solution.py:149
  96.6 0.7 pad_maximum_fusion.3
  (78 shorter events, 2.9 us)
Async XLA Ops:
  0.0 3.9 %copy-start = (bf16[32,2,128,128]{3,2,1,0:T(8,128)(2,1)S(1)}, bf16[32,2,128,128]{3,2,1,0:T(8,128)(2,1)}, u32[]{:S(2)}) copy-start(bf16[32,2,128,128]{3,2,1,0:T(8,128)(2,1)} %param.18) | copy-start | bytes 6291460
  1.2 5.3 %copy-start.6 = (bf16[32,2,128,128]{3,2,1,0:T(8,128)(2,1)S(1)}, bf16[32,2,128,128]{3,2,1,0:T(8,128)(2,1)}, u32[]{:S(2)}) copy-start(bf16[32,2,128,128]{3,2,1,0:T(8,128)(2,1)} %param.19) | copy-start | bytes 6291460
  6.5 0.9 copy-start.4
  6.5 6.8 %copy-start.2 = (bf16[1536,384]{1,0:T(8,128)(2,1)S(1)}, bf16[1536,384]{1,0:T(8,128)(2,1)}, u32[]{:S(2)}) copy-start(bf16[1536,384]{1,0:T(8,128)(2,1)} %param.21) | copy-start | bytes 3538948
  7.6 19.8 %collective-permute-start = (bf16[40,1536]{1,0:T(8,128)(2,1)S(1)}, bf16[40,1536]{1,0:T(8,128)(2,1)S(1)}, u32[]{:S(2)}, u32[]{:S(2)}) collective-permute-start(bf16[40,1536]{1,0:T(8,128)(2,1)S(1)} %get-tuple-element.123), channel_id=1, source_target_pairs={{0,4},{2,6},{4,0},{6,2},{8,12},{10,14},{12,8},{14,10},{1,5},{3,7},... | collective-permute-start | bytes 368648 | tf_op jit(solution)/shard_map/ppermute | solution.py:155
  10.7 16.7 %collective-permute-start.1 = (bf16[40,1536]{1,0:T(8,128)(2,1)S(1)}, bf16[40,1536]{1,0:T(8,128)(2,1)S(1)}, u32[]{:S(2)}, u32[]{:S(2)}) collective-permute-start(bf16[40,1536]{1,0:T(8,128)(2,1)S(1)} %get-tuple-element.124), channel_id=1, source_target_pairs={{0,8},{2,10},{4,12},{6,14},{8,0},{10,2},{12,4},{14,6},{1,9},{3,11}... | collective-permute-start | bytes 368648 | tf_op jit(solution)/shard_map/ppermute | solution.py:155
  13.3 14.1 %collective-permute-start.2 = (bf16[40,1536]{1,0:T(8,128)(2,1)S(1)}, bf16[40,1536]{1,0:T(8,128)(2,1)S(1)}, u32[]{:S(2)}, u32[]{:S(2)}) collective-permute-start(bf16[40,1536]{1,0:T(8,128)(2,1)S(1)} %get-tuple-element.122), channel_id=1, source_target_pairs={{0,12},{2,14},{4,8},{6,10},{8,4},{10,6},{12,0},{14,2},{1,13},{3,15... | collective-permute-start | bytes 368648 | tf_op jit(solution)/shard_map/ppermute | solution.py:155
  13.4 28.6 %collective-permute-start.5 = (bf16[512,384]{1,0:T(8,128)(2,1)S(1)}, bf16[512,384]{1,0:T(8,128)(2,1)S(1)}, u32[]{:S(2)}, u32[]{:S(2)}) collective-permute-start(bf16[512,384]{1,0:T(8,128)(2,1)S(1)} %get-tuple-element.82), channel_id=1, source_target_pairs={{0,2},{2,0},{4,6},{6,4},{8,10},{10,8},{12,14},{14,12},{1,3},{3,1},... | collective-permute-start | bytes 1179656 | tf_op jit(solution)/shard_map/ppermute | solution.py:152
  15.2 17.0 %collective-permute-start.3 = (bf16[512,384]{1,0:T(8,128)(2,1)S(1)}, bf16[512,384]{1,0:T(8,128)(2,1)S(1)}, u32[]{:S(2)}, u32[]{:S(2)}) collective-permute-start(bf16[512,384]{1,0:T(8,128)(2,1)S(1)} %get-tuple-element.81), channel_id=1, source_target_pairs={{0,2},{2,0},{4,6},{6,4},{8,10},{10,8},{12,14},{14,12},{1,3},{3,1},... | collective-permute-start | bytes 1179656 | tf_op jit(solution)/shard_map/ppermute | solution.py:152
  32.2 9.4 %collective-permute-start.4 = (bf16[512,384]{1,0:T(8,128)(2,1)S(1)}, bf16[512,384]{1,0:T(8,128)(2,1)S(1)}, u32[]{:S(2)}, u32[]{:S(2)}) collective-permute-start(bf16[512,384]{1,0:T(8,128)(2,1)S(1)} %collective-permute-done.3), channel_id=1, source_target_pairs={{0,16},{16,0},{1,17},{17,1},{2,18},{18,2},{3,19},{19,3},{4,20},{20... | collective-permute-start | bytes 1179656 | tf_op jit(solution)/shard_map/ppermute | solution.py:163
  42.4 1.5 %collective-permute-start.6 = (f32[4,16,768]{2,1,0:T(8,128)S(1)}, f32[4,16,768]{2,1,0:T(8,128)S(1)}, u32[]{:S(2)}, u32[]{:S(2)}) collective-permute-start(f32[4,16,768]{2,1,0:T(8,128)S(1)} %dynamic-slice_bitcast_fusion.1), channel_id=1, source_target_pairs={{0,1},{1,0},{2,3},{3,2},{4,5},{5,4},{6,7},{7,6},{8,9},{9,8},{10,11... | collective-permute-start | bytes 589832 | tf_op jit(solution)/shard_map/ppermute | solution.py:149
  44.0 11.3 %copy-start.5 = (f32[3072]{0:T(1024)S(1)}, f32[3072]{0:T(1024)}, u32[]{:S(2)}) copy-start(f32[3072]{0:T(1024)} %param.22) | copy-start | bytes 36868
  44.0 7.6 %collective-permute-start.9 = (bf16[64,768]{1,0:T(8,128)(2,1)S(1)}, bf16[64,768]{1,0:T(8,128)(2,1)S(1)}, u32[]{:S(2)}, u32[]{:S(2)}) collective-permute-start(bf16[64,768]{1,0:T(8,128)(2,1)S(1)} %get-tuple-element.117), channel_id=1, source_target_pairs={{0,12},{2,14},{4,8},{6,10},{8,4},{10,6},{12,0},{14,2},{1,13},{3,15... | collective-permute-start | bytes 294920 | tf_op jit(solution)/shard_map/ppermute | solution.py:155
  47.4 7.7 %collective-permute-start.8 = (bf16[64,768]{1,0:T(8,128)(2,1)S(1)}, bf16[64,768]{1,0:T(8,128)(2,1)S(1)}, u32[]{:S(2)}, u32[]{:S(2)}) collective-permute-start(bf16[64,768]{1,0:T(8,128)(2,1)S(1)} %get-tuple-element.117), channel_id=1, source_target_pairs={{0,8},{2,10},{4,12},{6,14},{8,0},{10,2},{12,4},{14,6},{1,9},{3,11}... | collective-permute-start | bytes 294920 | tf_op jit(solution)/shard_map/ppermute | solution.py:155
  47.4 7.7 %collective-permute-start.7 = (bf16[64,768]{1,0:T(8,128)(2,1)S(1)}, bf16[64,768]{1,0:T(8,128)(2,1)S(1)}, u32[]{:S(2)}, u32[]{:S(2)}) collective-permute-start(bf16[64,768]{1,0:T(8,128)(2,1)S(1)} %get-tuple-element.117), channel_id=1, source_target_pairs={{0,4},{2,6},{4,0},{6,2},{8,12},{10,14},{12,8},{14,10},{1,5},{3,7},... | collective-permute-start | bytes 294920 | tf_op jit(solution)/shard_map/ppermute | solution.py:155
  55.5 7.1 %copy-start.3 = (f32[3072,4]{0,1:T(4,128)S(1)}, f32[3072,4]{0,1:T(4,128)}, u32[]{:S(2)}) copy-start(f32[3072,4]{0,1:T(4,128)} %param.23) | copy-start | bytes 147460
  55.5 1.8 %collective-permute-start.10 = (bf16[64,3072]{1,0:T(8,128)(2,1)S(1)}, bf16[64,3072]{1,0:T(8,128)(2,1)S(1)}, u32[]{:S(2)}, u32[]{:S(2)}) collective-permute-start(bf16[64,3072]{1,0:T(8,128)(2,1)S(1)} %multiply_convert_fusion.1.own), channel_id=1, source_target_pairs={{0,1},{1,0},{2,3},{3,2},{4,5},{5,4},{6,7},{7,6},{8,9},{9,8},{10,11... | collective-permute-start | bytes 1179656 | tf_op jit(solution)/shard_map/ppermute | solution.py:149
  55.7 11.4 %collective-permute-start.15 = (bf16[64,3072]{1,0:T(8,128)(2,1)S(1)}, bf16[64,3072]{1,0:T(8,128)(2,1)S(1)}, u32[]{:S(2)}, u32[]{:S(2)}) collective-permute-start(bf16[64,3072]{1,0:T(8,128)(2,1)S(1)} %multiply_convert_fusion.1.own), channel_id=1, source_target_pairs={{0,2},{2,0},{4,6},{6,4},{8,10},{10,8},{12,14},{14,12},{1,3},{3,1},... | collective-permute-start | bytes 1179656 | tf_op jit(solution)/shard_map/ppermute | solution.py:152
  62.4 1.8 %collective-permute-start.11 = (bf16[64,3072]{1,0:T(8,128)(2,1)S(1)}, bf16[64,3072]{1,0:T(8,128)(2,1)S(1)}, u32[]{:S(2)}, u32[]{:S(2)}) collective-permute-start(bf16[64,3072]{1,0:T(8,128)(2,1)S(1)} %get-tuple-element.73), channel_id=1, source_target_pairs={{0,1},{1,0},{2,3},{3,2},{4,5},{5,4},{6,7},{7,6},{8,9},{9,8},{10,11... | collective-permute-start | bytes 1179656 | tf_op jit(solution)/shard_map/ppermute | solution.py:149
  67.1 1.7 %collective-permute-start.16 = (bf16[64,3072]{1,0:T(8,128)(2,1)S(1)}, bf16[64,3072]{1,0:T(8,128)(2,1)S(1)}, u32[]{:S(2)}, u32[]{:S(2)}) collective-permute-start(bf16[64,3072]{1,0:T(8,128)(2,1)S(1)} %collective-permute-done.15.own), channel_id=1, source_target_pairs={{0,1},{1,0},{2,3},{3,2},{4,5},{5,4},{6,7},{7,6},{8,9},{9,8},{10,11... | collective-permute-start | bytes 1179656 | tf_op jit(solution)/shard_map/ppermute | solution.py:149
  74.1 5.1 %collective-permute-start.17 = (bf16[64,3072]{1,0:T(8,128)(2,1)S(1)}, bf16[64,3072]{1,0:T(8,128)(2,1)S(1)}, u32[]{:S(2)}, u32[]{:S(2)}) collective-permute-start(bf16[64,3072]{1,0:T(8,128)(2,1)S(1)} %get-tuple-element.78), channel_id=1, source_target_pairs={{0,1},{1,0},{2,3},{3,2},{4,5},{5,4},{6,7},{7,6},{8,9},{9,8},{10,11... | collective-permute-start | bytes 1179656 | tf_op jit(solution)/shard_map/ppermute | solution.py:149
  74.7 7.6 %collective-permute-start.14 = (bf16[16,3072]{1,0:T(8,128)(2,1)S(1)}, bf16[16,3072]{1,0:T(8,128)(2,1)S(1)}, u32[]{:S(2)}, u32[]{:S(2)}) collective-permute-start(bf16[16,3072]{1,0:T(8,128)(2,1)S(1)} %get-tuple-element.86), channel_id=1, source_target_pairs={{0,12},{2,14},{4,8},{6,10},{8,4},{10,6},{12,0},{14,2},{1,13},{3,15... | collective-permute-start | bytes 294920 | tf_op jit(solution)/shard_map/ppermute | solution.py:155
  77.3 10.4 %collective-permute-start.13 = (bf16[16,3072]{1,0:T(8,128)(2,1)S(1)}, bf16[16,3072]{1,0:T(8,128)(2,1)S(1)}, u32[]{:S(2)}, u32[]{:S(2)}) collective-permute-start(bf16[16,3072]{1,0:T(8,128)(2,1)S(1)} %get-tuple-element.87), channel_id=1, source_target_pairs={{0,8},{2,10},{4,12},{6,14},{8,0},{10,2},{12,4},{14,6},{1,9},{3,11}... | collective-permute-start | bytes 294920 | tf_op jit(solution)/shard_map/ppermute | solution.py:155
  77.6 11.8 %collective-permute-start.12 = (bf16[16,3072]{1,0:T(8,128)(2,1)S(1)}, bf16[16,3072]{1,0:T(8,128)(2,1)S(1)}, u32[]{:S(2)}, u32[]{:S(2)}) collective-permute-start(bf16[16,3072]{1,0:T(8,128)(2,1)S(1)} %get-tuple-element.85), channel_id=1, source_target_pairs={{0,4},{2,6},{4,0},{6,2},{8,12},{10,14},{12,8},{14,10},{1,5},{3,7},... | collective-permute-start | bytes 294920 | tf_op jit(solution)/shard_map/ppermute | solution.py:155
  79.2 18.1 %copy-start.1 = (bf16[32,2,128,128]{3,2,1,0:T(8,128)(2,1)S(1)}, bf16[32,2,128,128]{3,2,1,0:T(8,128)(2,1)}, u32[]{:S(2)}) copy-start(bf16[32,2,128,128]{3,2,1,0:T(8,128)(2,1)} %param.18) | copy-start | bytes 6291460
  79.4 10.1 %collective-permute-start.21 = (bf16[16,3072]{1,0:T(8,128)(2,1)S(1)}, bf16[16,3072]{1,0:T(8,128)(2,1)S(1)}, u32[]{:S(2)}, u32[]{:S(2)}) collective-permute-start(bf16[16,3072]{1,0:T(8,128)(2,1)S(1)} %get-tuple-element.89), channel_id=1, source_target_pairs={{0,2},{2,0},{4,6},{6,4},{8,10},{10,8},{12,14},{14,12},{1,3},{3,1},... | collective-permute-start | bytes 294920 | tf_op jit(solution)/shard_map/ppermute | solution.py:258
  81.0 9.1 %collective-permute-start.20 = (bf16[16,3072]{1,0:T(8,128)(2,1)S(1)}, bf16[16,3072]{1,0:T(8,128)(2,1)S(1)}, u32[]{:S(2)}, u32[]{:S(2)}) collective-permute-start(bf16[16,3072]{1,0:T(8,128)(2,1)S(1)} %get-tuple-element.90), channel_id=1, source_target_pairs={{0,6},{2,4},{4,2},{6,0},{8,14},{10,12},{12,10},{14,8},{1,7},{3,5},... | collective-permute-start | bytes 294920 | tf_op jit(solution)/shard_map/ppermute | solution.py:258
  82.3 11.6 %collective-permute-start.19 = (bf16[16,3072]{1,0:T(8,128)(2,1)S(1)}, bf16[16,3072]{1,0:T(8,128)(2,1)S(1)}, u32[]{:S(2)}, u32[]{:S(2)}) collective-permute-start(bf16[16,3072]{1,0:T(8,128)(2,1)S(1)} %get-tuple-element.91), channel_id=1, source_target_pairs={{0,10},{2,8},{4,14},{6,12},{8,2},{10,0},{12,6},{14,4},{1,11},{3,9}... | collective-permute-start | bytes 294920 | tf_op jit(solution)/shard_map/ppermute | solution.py:258
  87.7 7.4 %collective-permute-start.18 = (bf16[16,3072]{1,0:T(8,128)(2,1)S(1)}, bf16[16,3072]{1,0:T(8,128)(2,1)S(1)}, u32[]{:S(2)}, u32[]{:S(2)}) collective-permute-start(bf16[16,3072]{1,0:T(8,128)(2,1)S(1)} %get-tuple-element.88), channel_id=1, source_target_pairs={{0,14},{2,12},{4,10},{6,8},{8,6},{10,4},{12,2},{14,0},{1,15},{3,13... | collective-permute-start | bytes 294920 | tf_op jit(solution)/shard_map/ppermute | solution.py:258
  95.2 1.4 %collective-permute-start.22 = (bf16[16,3072]{1,0:T(8,128)(2,1)S(1)}, bf16[16,3072]{1,0:T(8,128)(2,1)S(1)}, u32[]{:S(2)}, u32[]{:S(2)}) collective-permute-start(bf16[16,3072]{1,0:T(8,128)(2,1)S(1)} %add_convert_fusion), channel_id=1, source_target_pairs={{0,1},{1,0},{2,3},{3,2},{4,5},{5,4},{6,7},{7,6},{8,9},{9,8},{10,11... | collective-permute-start | bytes 294920 | tf_op jit(solution)/shard_map/ppermute | solution.py:149
